TPU v7x, 32 devices: a whole 2x2x4 slice. The times are simulated.
32 devices in a mesh: dp: 2 (over x), ctx: 16 (over z, y, core).
Axes of the slice: x: 2, y: 2, z: 4, core: 2. Of those that a mesh axis runs over, the one named last changes fastest.
Arguments:
- patches: bfloat16 [2, 1024, 1280], P('dp', 'ctx'), may hold values from -6 to 6
- vit_norm_gain: float32 [1280], replicated, may hold values from 0.1 to 1.9
- vit_qkv: bfloat16 [1280, 1920], P('dp'), may hold values from -0.15625 to 0.15625
- vit_out: bfloat16 [640, 1280], P('dp'), may hold values from -0.25 to 0.25
- merger: bfloat16 [5120, 8192], P('dp', 'ctx'), may hold values from -0.078125 to 0.078125
- text_embed: bfloat16 [2, 2048, 8192], P('dp', 'ctx'), may hold values from -6 to 6
- lang_norm_gain: float32 [8192], replicated, may hold values from 0.1 to 1.9
- key_weight: bfloat16 [8192, 512], P('dp'), may hold values from -0.0625 to 0.0625
- key_cotangent: bfloat16 [2, 2048, 512], P('dp', 'ctx'), may hold values from -6 to 6
- image_grid: int32 [2, 16, 2], P('dp'), may hold values from 1 to 16, as said below
- image_start: int32 [2, 16], P('dp'), may hold values from 0 to 2047, as said below
Outputs:
- key_rot: bfloat16 [2, 2048, 512], P('dp', 'ctx')
- merger_grad: float32 [5120, 8192], P('dp', 'ctx')
Inputs may be any that keep to these rules, and one draw needn't show every extreme that they name: `image_grid`: the image held by device c of ctx has a grid of rows by columns merged tokens with rows times columns at most 16, equal to 16 for some device of every sequence. Its 4 * rows * columns patches are the first rows of that device's patch block, each 2x2 merge window as 4 consecutive rows, windows in row-major order; the remaining rows are unused. `image_start`: the image occupies rows * columns consecutive positions from here. The range of 128 positions of each device along ctx holds exactly one image, wholly.
All inputs are finite; a program needn't handle non-finite values.
Results may differ from a plain program's by a relative error of at most 0.015.
Values may be sent and summed in bfloat16 or wider, within the bound.
No kernel may reach another device: no remote copies, remote signals or barrier semaphores. Data moves between devices by JAX's collectives and lax.ppermute only.
A program may use at most 128 MiB of HBM per device.

v0:
```python
import math

import jax
import jax.numpy as jnp
from jax import lax
from jax.sharding import PartitionSpec as P

VHD = 80
HD = 128


EPS = 1e-06
THETA = 1000000.0


def layer_norm(values):
    average = jnp.mean(values, axis=-1, keepdims=True)
    centered = values - average
    variance = jnp.mean(centered * centered, axis=-1, keepdims=True)
    return centered * lax.rsqrt(variance + EPS)


def vision_image(patch_rows, count, norm_gain, qkv_weight, out_weight):
    values = patch_rows.astype(jnp.float32)
    normed = (layer_norm(values) * norm_gain).astype(jnp.bfloat16)
    projected = jnp.dot(normed, qkv_weight, preferred_element_type=jnp.float32).astype(jnp.bfloat16)
    width = qkv_weight.shape[1] // 3
    head_count = width // VHD
    queries = projected[:, :width].reshape(-1, head_count, VHD)
    key_vecs = projected[:, width : 2 * width].reshape(-1, head_count, VHD)
    value_vecs = projected[:, 2 * width :].reshape(-1, head_count, VHD)
    scores = jnp.einsum(
        "qhd,khd->hqk", queries, key_vecs, preferred_element_type=jnp.float32
    ) / math.sqrt(VHD)
    alive_mask = (jnp.arange(values.shape[0], dtype=jnp.int32) < 4 * count).astype(jnp.float32)
    weights = jnp.exp(scores) * alive_mask[None, None, :]
    probability = (weights / jnp.sum(weights, axis=-1, keepdims=True)).astype(jnp.bfloat16)
    attended = jnp.einsum(
        "hqk,khd->qhd", probability, value_vecs, preferred_element_type=jnp.float32
    )
    attended = attended.reshape(values.shape[0], width).astype(jnp.bfloat16)
    vit_hidden = values + jnp.dot(attended, out_weight, preferred_element_type=jnp.float32)
    merged = layer_norm(vit_hidden).astype(jnp.bfloat16).reshape(-1, 4 * values.shape[1])
    keeping = jnp.arange(merged.shape[0], dtype=jnp.int32) < count
    return jnp.where(keeping[:, None], merged, jnp.zeros_like(merged))


def rope_tables(pos_t, pos_h, pos_w):
    half_dim = HD // 2
    freq_index = jnp.arange(half_dim, dtype=jnp.int32)
    inverse = THETA ** (-(2.0 * freq_index.astype(jnp.float32)) / HD)
    first_cut = HD // 8
    second_cut = first_cut + 3 * HD // 16
    chosen = jnp.where(
        freq_index[None, :] < first_cut,
        pos_t[:, None],
        jnp.where(freq_index[None, :] < second_cut, pos_h[:, None], pos_w[:, None]),
    )
    angles = chosen.astype(jnp.float32) * inverse[None, :]
    return (jnp.cos(angles), jnp.sin(angles))


def rotate(vectors, cosine, sines):
    half_dim = vectors.shape[-1] // 2
    first_half = vectors[..., :half_dim]
    second_half = vectors[..., half_dim:]
    cos_part = cosine[:, None, :]
    sin_part = sines[:, None, :]
    return jnp.concatenate(
        [
            first_half * cos_part - second_half * sin_part,
            second_half * cos_part + first_half * sin_part,
        ],
        axis=-1,
    )


def unrotate(vectors, cosine, sines):
    half_dim = vectors.shape[-1] // 2
    first_half = vectors[..., :half_dim]
    second_half = vectors[..., half_dim:]
    cos_part = cosine[:, None, :]
    sin_part = sines[:, None, :]
    return jnp.concatenate(
        [
            first_half * cos_part + second_half * sin_part,
            second_half * cos_part - first_half * sin_part,
        ],
        axis=-1,
    )


def norm_backward(rows, grad_rows, gain):
    values = rows.astype(jnp.float32)
    row_scale = lax.rsqrt(jnp.mean(values * values, axis=-1, keepdims=True) + EPS)
    weighted = grad_rows * gain
    return row_scale * weighted - values * row_scale**3 * jnp.mean(
        values * weighted, axis=-1, keepdims=True
    )


def on_device(
    patches,
    vit_norm_gain,
    vit_qkv,
    vit_out,
    merger,
    text_embed,
    lang_norm_gain,
    key_weight,
    key_cotangent,
    image_grid,
    image_start,
):
    tokens = text_embed.shape[1]
    groups = lax.axis_size("ctx")
    own_index = lax.axis_index("ctx")
    qkv_full, out_full, merger_rows = (
        lax.all_gather(vit_qkv, "dp", axis=0, tiled=True),
        lax.all_gather(vit_out, "dp", axis=0, tiled=True),
        lax.all_gather(merger, "dp", axis=0, tiled=True),
    )
    grid_sizes = image_grid[0]
    start_pos = image_start[0]
    grid_rows = grid_sizes[:, 0]
    grid_cols = grid_sizes[:, 1]
    counts = grid_rows * grid_cols
    own_count = lax.dynamic_index_in_dim(counts, own_index, 0, keepdims=False)
    merged = vision_image(patches[0], own_count, vit_norm_gain, qkv_full, out_full)
    capacity = merged.shape[0]
    merged_all = lax.all_gather(merged, "ctx", axis=0, tiled=True)
    embedded = jnp.dot(merged_all, merger_rows, preferred_element_type=jnp.float32).astype(
        jnp.bfloat16
    )
    blocks = embedded.reshape(groups, capacity, -1)
    target_range = start_pos // tokens
    routing = (target_range[None, :] == jnp.arange(groups, dtype=jnp.int32)[:, None]).astype(
        jnp.bfloat16
    )
    outgoing = jnp.einsum(
        "do,okc->dkc", routing, blocks, preferred_element_type=jnp.float32
    ).astype(jnp.bfloat16)
    arrived = lax.all_to_all(outgoing, "ctx", split_axis=0, concat_axis=2, tiled=True)[0]
    own_range = target_range == own_index
    image_first = jnp.sum(jnp.where(own_range, start_pos, 0))
    own_cols = jnp.sum(jnp.where(own_range, grid_cols, 0))
    image_count = jnp.sum(jnp.where(own_range, counts, 0))
    offset = image_first - own_index * tokens
    local_index = jnp.arange(tokens, dtype=jnp.int32)
    inner_index = local_index - offset
    image_mask = (inner_index >= 0) & (inner_index < image_count)
    slot_index = jnp.arange(capacity, dtype=jnp.int32)
    slot_alive = slot_index < image_count
    selector = (inner_index[:, None] == slot_index[None, :]) & slot_alive[None, :]
    placed = jnp.dot(
        selector.astype(jnp.bfloat16), arrived, preferred_element_type=jnp.float32
    ).astype(jnp.bfloat16)
    hidden = jnp.where(image_mask[:, None], placed, text_embed[0])
    hidden_float = hidden.astype(jnp.float32)
    row_scale = lax.rsqrt(jnp.mean(hidden_float * hidden_float, axis=-1, keepdims=True) + EPS)
    normed = (hidden_float * row_scale * lang_norm_gain).astype(jnp.bfloat16)
    pieces = lax.all_to_all(normed, "dp", split_axis=1, concat_axis=0, tiled=True)
    key_proj = lax.psum_scatter(
        jnp.dot(pieces, key_weight, preferred_element_type=jnp.float32).astype(jnp.bfloat16),
        "dp",
        scatter_dimension=0,
        tiled=True,
    ).astype(jnp.float32)
    global_index = own_index * tokens + local_index
    inner_safe = jnp.clip(inner_index, 0, capacity - 1)
    pos_t = jnp.where(image_mask, image_first, global_index)
    pos_h = jnp.where(image_mask, image_first + inner_safe // own_cols, global_index)
    pos_w = jnp.where(image_mask, image_first + inner_safe % own_cols, global_index)
    cosine, sines = rope_tables(pos_t, pos_h, pos_w)
    head_count = key_weight.shape[1] // HD
    rotated = (
        rotate(key_proj.reshape(tokens, head_count, HD), cosine, sines)
        .reshape(tokens, -1)
        .astype(jnp.bfloat16)
    )
    grad_key = unrotate(
        key_cotangent[0].astype(jnp.float32).reshape(tokens, head_count, HD), cosine, sines
    ).reshape(tokens, -1)
    grad_image_key = jnp.dot(
        selector.T.astype(jnp.float32), grad_key, precision=lax.Precision.HIGHEST
    ).astype(jnp.bfloat16)
    all_grads = lax.all_gather(grad_image_key, "dp", axis=0, tiled=True)
    partial_value = lax.dot_general(
        all_grads, key_weight, (((1,), (1,)), ((), ())), preferred_element_type=jnp.float32
    )
    grad_normed = lax.all_to_all(
        partial_value.astype(jnp.bfloat16), "dp", split_axis=0, concat_axis=1, tiled=True
    ).astype(partial_value.dtype)
    grad_hidden = norm_backward(arrived, grad_normed, lang_norm_gain)
    grad_embedded = jnp.where(slot_alive[:, None], grad_hidden, 0.0).astype(jnp.bfloat16)
    returned = lax.all_to_all(grad_embedded[None], "ctx", split_axis=2, concat_axis=0, tiled=True)
    grad_blocks = jnp.einsum(
        "do,dkc->okc", routing, returned, preferred_element_type=jnp.float32
    ).astype(jnp.bfloat16)
    grad_all = grad_blocks.reshape(groups * capacity, -1)
    merger_grad = lax.psum_scatter(
        lax.dot_general(
            merged_all, grad_all, (((0,), (0,)), ((), ())), preferred_element_type=jnp.float32
        ).astype(jnp.bfloat16),
        "dp",
        scatter_dimension=0,
        tiled=True,
    ).astype(jnp.float32)
    return (rotated[None], merger_grad)


def solution(mesh):
    return jax.shard_map(
        on_device,
        mesh=mesh,
        in_specs=(
            P("dp", "ctx", None),
            P(),
            P("dp", None),
            P("dp", None),
            P("dp", "ctx"),
            P("dp", "ctx", None),
            P(),
            P("dp", None),
            P("dp", "ctx", None),
            P("dp", None, None),
            P("dp", None),
        ),
        out_specs=(P("dp", "ctx", None), P("dp", "ctx")),
        check_vma=False,
    )
```

profile of v0, /device:TPU:0, one launch (start us, length us, event | category | flops | bytes accessed | tf_op | source)
XLA Modules:
  0.0 469.2 jit_solution(12247656343845873802)
XLA Ops:
  12.5 64.7 %all-gather.5.cloned.1.call-done = bf16[1280,1920]{1,0:T(8,128)(2,1)} async-done(((bf16[640,1920]{1,0:T(8,128)(2,1)}), bf16[1280,1920]{1,0:T(8,128)(2,1)}) %all-gather.5.cloned.1.call-update) | async-done | bytes 4915216 | tf_op jit(solution)/shard_map/all_gather | solution.py:119
  77.2 3.4 convolution_convert_fusion.3
  81.8 24.8 %all-gather.7.cloned.1.call-done = bf16[640,1280]{1,0:T(8,128)(2,1)} async-done(((bf16[320,1280]{1,0:T(8,128)(2,1)}), bf16[640,1280]{1,0:T(8,128)(2,1)}) %all-gather.7.cloned.1.call-update) | async-done | bytes 1638416 | tf_op jit(solution)/shard_map/all_gather | solution.py:120
  106.7 1.9 fusion.49
  109.0 0.8 broadcast_select_fusion
  109.8 67.0 %all-gather.11.cloned.1.call-done = bf16[5120,512]{1,0:T(8,128)(2,1)} async-done(((bf16[2560,512]{1,0:T(8,128)(2,1)}), bf16[5120,512]{1,0:T(8,128)(2,1)}) %all-gather.11.cloned.1.call-update) | async-done | bytes 5242896 | tf_op jit(solution)/shard_map/all_gather | solution.py:121
  176.8 45.8 %all-gather.9.cloned.1.call-done = bf16[256,5120]{1,0:T(8,128)(2,1)} async-done(((bf16[16,5120]{1,0:T(8,128)(2,1)}), bf16[256,5120]{1,0:T(8,128)(2,1)}) %all-gather.9.cloned.1.call-update) | async-done | bytes 2621456 | tf_op jit(solution)/shard_map/all_gather | solution.py:131
  222.6 4.8 %convolution_convert_fusion.7 = bf16[256,512]{1,0:T(8,128)(2,1)S(1)} fusion(bf16[256,5120]{1,0:T(8,128)(2,1)} %all-gather.9.cloned.1.call-done, bf16[5120,512]{1,0:T(8,128)(2,1)} %all-gather.11.cloned.1.call-done), kind=kOutput, calls=%fused_computation.13 | convolution fusion | flops 1342308352 | bytes 8126464 | tf_op jit(solution)/shard_map/dot_general | solution.py:132
  227.8 0.9 copy.48
  228.6 3.6 all-to-all-start
  235.4 1.3 fusion.39
  236.7 1.4 add_select_fusion.1
  238.1 4.0 all-to-all-done
  242.2 0.9 multiply_reduce_fusion
  243.8 28.0 %all_to_all.65 = bf16[128,2,4096]{2,0,1:T(8,128)(2,1)S(1)} all-to-all(bf16[128,2,4096]{2,0,1:T(8,128)(2,1)S(1)} %bitcast.113), channel_id=1, replica_groups=mesh['dp'=2,'ctx'=16] {'dp'}, dimensions={1} | all-to-all | bytes 4194304 | tf_op jit(solution)/shard_map/all_to_all | solution.py:162
  271.8 2.0 convolution_convert_fusion.5
  274.3 9.1 %reduce-scatter.3.cloned.1.call-done = bf16[128,512]{1,0:T(8,128)(2,1)} async-done(((bf16[256,512]{1,0:T(8,128)(2,1)}), bf16[128,512]{1,0:T(8,128)(2,1)}) %reduce-scatter.3.cloned.1.call-update) | async-done | bytes 131088 | tf_op jit(solution)/shard_map/reduce_scatter | solution.py:163
  283.4 1.0 reshape.495
  285.3 4.4 all_gather.19
  289.7 4.2 convolution_convert_fusion.2
  294.0 3.4 all-to-all-start.2
  297.9 4.7 all-to-all-done.2
  304.4 6.7 %copy.53 = bf16[1,16,8192]{1,0,2:T(2,128)(2,1)} copy(bf16[1,16,8192]{2,1,0:T(8,128)(2,1)S(1)} %select_convert_fusion) | data formatting | bytes 524288 | tf_op jit(solution)/shard_map/convert_element_type | solution.py:195
  311.6 45.2 %reduce.3 = bf16[8192,16]{1,0:T(8,128)(2,1)S(1)} reduce(bf16[8192,1,16]{2,1,0:T(2,128)(2,1)} %bitcast.110, bf16[]{:T(256)} %broadcast.478), dimensions={1}, to_apply=%bitcast.90.reduce_sub_computation | reduce | bytes 524290
  356.8 2.1 reshape.502
  359.0 15.4 %all_to_all.66 = bf16[16,2,4096]{2,1,0:T(2,128)(2,1)S(1)} all-to-all(bf16[16,2,4096]{2,1,0:T(2,128)(2,1)S(1)} %reshape.502), channel_id=1, replica_groups=mesh['dp'=2,'ctx'=16] {'ctx'}, dimensions={0} | all-to-all | bytes 524288 | tf_op jit(solution)/shard_map/all_to_all | solution.py:196
  374.4 7.6 %reshape.503 = bf16[8192,1,16]{2,1,0:T(2,128)(2,1)} reshape(bf16[16,2,4096]{2,1,0:T(2,128)(2,1)S(1)} %all_to_all.66) | data formatting | bytes 524288
  382.0 7.9 %copy.54 = bf16[1,16,8192]{2,1,0:T(8,128)(2,1)S(1)} copy(bf16[1,16,8192]{1,0,2:T(2,128)(2,1)} %bitcast.111) | data formatting | bytes 524288 | tf_op jit(solution)/shard_map/all_to_all | solution.py:196
  390.4 3.9 convolution_convert_fusion.1
  394.6 0.7 convert_element_type.180
  395.3 62.3 %reduce-scatter.5.cloned.1.call-done = bf16[2560,512]{1,0:T(8,128)(2,1)} async-done(((bf16[5120,512]{1,0:T(8,128)(2,1)}), bf16[2560,512]{1,0:T(8,128)(2,1)}) %reduce-scatter.5.cloned.1.call-update) | async-done | bytes 2621456 | tf_op jit(solution)/shard_map/reduce_scatter | solution.py:201
  457.6 4.8 %convert_element_type.196 = f32[2560,512]{1,0:T(8,128)} convert(bf16[2560,512]{1,0:T(8,128)(2,1)} %reduce-scatter.5.cloned.1.call-done) | non-fusion elementwise | flops 1310720 | bytes 7864320 | tf_op jit(solution)/shard_map/convert_element_type | solution.py:208
  (81 shorter events, 12.8 us)
Async XLA Ops:
  7.2 2.3 copy-start.7
  7.2 2.3 copy-start.8
  7.2 4.9 %copy-start.2 = (bf16[1,64,1280]{2,1,0:T(8,128)(2,1)S(1)}, bf16[1,64,1280]{2,1,0:T(8,128)(2,1)}, u32[]{:S(2)}) copy-start(bf16[1,64,1280]{2,1,0:T(8,128)(2,1)} %param.11) | copy-start | bytes 491524
  7.2 70.0 %copy-start.6 = (f32[1280]{0:T(1024)S(1)}, f32[1280]{0:T(1024)}, u32[]{:S(2)}) copy-start(f32[1280]{0:T(1024)} %param.12) | copy-start | bytes 15364
  7.2 70.0 %all-gather.5.cloned.1.call-start = ((), (), s32[]{:S(2)}) async-start(), calls=%async_computation.6 | async-start | bytes 7372800 | tf_op jit(solution)/shard_map/all_gather | solution.py:119
  7.9 98.7 %all-gather.7.cloned.1.call-start = ((), (), s32[]{:S(2)}) async-start(), calls=%async_computation.7 | async-start | bytes 2457600 | tf_op jit(solution)/shard_map/all_gather | solution.py:120
  8.7 168.1 %all-gather.11.cloned.1.call-start = ((), (), s32[]{:S(2)}) async-start(), calls=%async_computation.9 | async-start | bytes 7864320 | tf_op jit(solution)/shard_map/all_gather | solution.py:121
  9.4 213.2 %all-gather.9.cloned.1.call-start = ((), (), s32[]{:S(2)}) async-start(), calls=%async_computation.8 | async-start | bytes 2785280 | tf_op jit(solution)/shard_map/all_gather | solution.py:131
  109.8 132.4 %copy-start.3 = (bf16[1,128,8192]{2,1,0:T(8,128)(2,1)S(1)}, bf16[1,128,8192]{2,1,0:T(8,128)(2,1)}, u32[]{:S(2)}) copy-start(bf16[1,128,8192]{2,1,0:T(8,128)(2,1)} %param.16) | copy-start | bytes 6291460
  227.7 15.4 %copy-start.4 = (f32[8192]{0:T(1024)S(1)}, f32[8192]{0:T(1024)}, u32[]{:S(2)}) copy-start(f32[8192]{0:T(1024)} %param.17) | copy-start | bytes 98308
  228.6 13.6 %all-to-all-start = ((bf16[16,16,512]{2,1,0:T(8,128)(2,1)}), bf16[16,16,512]{2,1,0:T(8,128)(2,1)S(1)}, u32[]{:S(2)}, u32[]{:S(2)}) async-start(bf16[16,16,512]{2,1,0:T(8,128)(2,1)} %copy.48), calls=%async_computation | async-start | bytes 524288 | tf_op jit(solution)/shard_map/all_to_all | solution.py:143
  232.2 51.2 %reduce-scatter.3.cloned.1.call-start = ((), (), s32[]{:S(2)}) async-start(), calls=%async_computation.10 | async-start | bytes 393216 | tf_op jit(solution)/shard_map/reduce_scatter | solution.py:163
  243.6 28.2 %copy-start.1 = (bf16[4096,512]{1,0:T(8,128)(2,1)S(1)}, bf16[4096,512]{1,0:T(8,128)(2,1)}, u32[]{:S(2)}) copy-start(bf16[4096,512]{1,0:T(8,128)(2,1)} %param.18) | copy-start | bytes 12582916
  271.8 2.1 copy-start.5
  294.0 8.6 %all-to-all-start.2 = ((bf16[2,16,4096]{2,1,0:T(8,128)(2,1)}), bf16[2,16,4096]{2,1,0:T(8,128)(2,1)S(1)}, u32[]{:S(2)}, u32[]{:S(2)}) async-start(bf16[2,16,4096]{2,1,0:T(8,128)(2,1)} %bitcast.17), calls=%async_computation.3 | async-start | bytes 524288 | tf_op jit(solution)/shard_map/all_to_all | solution.py:191
  297.4 160.2 %reduce-scatter.5.cloned.1.call-start = ((), (), s32[]{:S(2)}) async-start(), calls=%async_computation.11 | async-start | bytes 7864320 | tf_op jit(solution)/shard_map/reduce_scatter | solution.py:201
  374.4 16.0 %copy-start = (bf16[256,5120]{1,0:T(8,128)(2,1)S(1)}, bf16[256,5120]{1,0:T(8,128)(2,1)}, u32[]{:S(2)}) copy-start(bf16[256,5120]{1,0:T(8,128)(2,1)} %all-gather.9.cloned.1.call-done) | copy-start | bytes 7864324
Sparse Core Ops, SparseCore 0:
  9.6 67.5 all-gather.4
  78.7 27.9 all-gather.6
  108.2 68.5 all-gather.10
  179.5 43.0 all-gather.8
  274.0 9.3 reduce-scatter.2
  394.5 63.0 reduce-scatter.4
where the time goes:
time: 470 us; the launch traced here: 469 us
  waiting for transfers between devices  284 us (60%)
  other arithmetic  58.6 us (12%)
  blocking collectives  47.8 us (10%)
  local copies, waits for them, and re-layouts  30.7 us (7%)
  matrix products  22.5 us (5%)
  between operations  17.8 us (4%)
  starting transfers between devices  7.42 us (2%)
    all_gather x1, waiting for transfers between devices, on_device(): lax.all_gather(merger, 'dp', axis=0, tiled=True)  67 us
    all_gather x1, waiting for transfers between devices, on_device(): lax.all_gather(vit_qkv, 'dp', axis=0, tiled=True)  64.7 us
    reduce_scatter x1, waiting for transfers between devices, on_device(): lax.psum_scatter(lax.dot_general(merged_all, grad_all, (((0,), (0,)), (()...  62.3 us
    all_gather x1, waiting for transfers between devices, on_device(): merged_all = lax.all_gather(merged, 'ctx', axis=0, tiled=True)  45.8 us
    unnamed x1, other arithmetic  45.2 us
    all_to_all x1, blocking collectives, on_device(): lax.all_to_all(normed, 'dp', split_axis=1, concat_axis=0, tiled=True)  28 us
    all_gather x1, waiting for transfers between devices, on_device(): lax.all_gather(vit_out, 'dp', axis=0, tiled=True)  24.8 us
    all_to_all x1, blocking collectives, on_device(): lax.all_to_all(grad_embedded[None], 'ctx', split_axis=2, concat_axis=0, t...  15.4 us
  transfers between devices with their start and end apart: 8, of which 8 were waited for; matrix products, arithmetic and copies ran while one was open for 3% of the time, Pallas kernels for 0%

commit v1 on v0

v1 whole, which is shorter than its diff:
```python
import math

import jax
import jax.numpy as jnp
from jax import lax
from jax.sharding import PartitionSpec as P

VHD = 80
HD = 128
EPS = 1e-06
THETA = 1000000.0
HIGHEST = lax.Precision.HIGHEST
BF16 = jnp.bfloat16
F32 = jnp.float32


def layer_norm(values):
    average = jnp.mean(values, axis=-1, keepdims=True)
    centered = values - average
    variance = jnp.mean(centered * centered, axis=-1, keepdims=True)
    return centered * lax.rsqrt(variance + EPS)


def dot(a, b, **kw):
    return jnp.dot(a, b, preferred_element_type=F32, **kw)


def rope_tables(pos_t, pos_h, pos_w):
    half_dim = HD // 2
    freq_index = jnp.arange(half_dim, dtype=jnp.int32)
    inverse = THETA ** (-(2.0 * freq_index.astype(F32)) / HD)
    first_cut = HD // 8
    second_cut = first_cut + 3 * HD // 16
    chosen = jnp.where(
        freq_index[None, :] < first_cut,
        pos_t[:, None],
        jnp.where(freq_index[None, :] < second_cut, pos_h[:, None], pos_w[:, None]),
    )
    angles = chosen.astype(F32) * inverse[None, :]
    return (jnp.cos(angles), jnp.sin(angles))


def rotate(vectors, cosine, sines):
    half_dim = vectors.shape[-1] // 2
    first_half = vectors[..., :half_dim]
    second_half = vectors[..., half_dim:]
    cos_part = cosine[:, None, :]
    sin_part = sines[:, None, :]
    return jnp.concatenate(
        [
            first_half * cos_part - second_half * sin_part,
            second_half * cos_part + first_half * sin_part,
        ],
        axis=-1,
    )


def shift(x, k):
    size = lax.axis_size("dp")
    return lax.ppermute(x, "dp", [(i, (i + k) % size) for i in range(size)])


def gather_dp(x):
    return [x] + [shift(x, k) for k in range(1, lax.axis_size("dp"))]


def gather_ctx(x):
    groups = lax.axis_size("ctx")
    own = lax.axis_index("ctx")
    if groups & (groups - 1):
        return lax.all_gather(x, "ctx", axis=0, tiled=True), jnp.arange(groups, dtype=jnp.int32)
    stride = groups // 2
    order = [0]
    while stride:
        other = lax.ppermute(x, "ctx", [(i, i ^ stride) for i in range(groups)])
        x = jnp.concatenate([x, other], axis=0)
        order = order + [b ^ stride for b in order]
        stride //= 2
    return x, own ^ jnp.asarray(order, jnp.int32)


def on_device(
    patches,
    vit_norm_gain,
    vit_qkv,
    vit_out,
    merger,
    text_embed,
    lang_norm_gain,
    key_weight,
    key_cotangent,
    image_grid,
    image_start,
):
    parts = lax.axis_size("dp")
    groups = lax.axis_size("ctx")
    own_part = lax.axis_index("dp")
    own = lax.axis_index("ctx")
    tokens, width = text_embed.shape[1:]
    vit_width = patches.shape[2]
    capacity = patches.shape[1] // 4
    attn_width = vit_qkv.shape[1] // 3
    key_width = key_weight.shape[1]
    head_count = attn_width // VHD // parts
    block_width = attn_width // parts
    feature_cols = merger.shape[1]

    info = jnp.concatenate([image_grid[0].T, image_start], axis=0)
    infos = jnp.stack(gather_dp(info))
    grid_rows, grid_cols, start_pos = infos[:, 0], infos[:, 1], infos[:, 2]
    counts = grid_rows * grid_cols
    target_range = start_pos // tokens
    group_index = jnp.arange(groups, dtype=jnp.int32)
    slot_index = jnp.arange(capacity, dtype=jnp.int32)
    own_counts = jnp.sum(jnp.where(group_index[None] == own, counts, 0), axis=1)

    row = jnp.arange(4 * capacity, dtype=jnp.int32)
    source_row = (row % capacity) * 4 + row // capacity
    order_rows = (source_row[:, None] == row[None, :]).astype(BF16)
    own_rows = dot(order_rows, patches[0]).astype(BF16)
    images = jnp.stack(gather_dp(own_rows))
    values = images.astype(F32)
    normed = (layer_norm(values) * vit_norm_gain).astype(BF16)
    part_width = vit_width // parts
    normed_part = lax.dynamic_slice_in_dim(normed, own_part * part_width, part_width, 2)
    qkv_blocks = vit_qkv.reshape(part_width, 3, parts, block_width)

    def head_weights(k):
        index = (own_part + k) % parts
        return lax.dynamic_index_in_dim(qkv_blocks, index, 2, keepdims=False).reshape(
            part_width, 3 * block_width
        )

    flat_part = normed_part.reshape(parts * 4 * capacity, part_width)
    projected = dot(flat_part, head_weights(0)).reshape(parts, 4 * capacity, -1)
    for k in range(1, parts):
        sent = dot(flat_part, head_weights(k)).astype(BF16).reshape(parts, 4 * capacity, -1)
        projected = projected + jnp.roll(shift(sent, k).astype(F32), k, axis=0)
    projected = projected.astype(BF16).reshape(parts, 4 * capacity, 3, head_count, VHD)
    scores = jnp.einsum(
        "iqhd,ikhd->ihqk", projected[:, :, 0], projected[:, :, 1], preferred_element_type=F32
    ) / math.sqrt(VHD)
    alive_mask = ((row % capacity)[None, :] < own_counts[:, None]).astype(F32)
    weights = jnp.exp(scores) * alive_mask[:, None, None, :]
    probability = (weights / jnp.sum(weights, axis=-1, keepdims=True)).astype(BF16)
    attended = jnp.einsum(
        "ihqk,ikhd->iqhd", probability, projected[:, :, 2], preferred_element_type=F32
    ).astype(BF16)
    out_part = dot(attended.reshape(parts * 4 * capacity, block_width), vit_out)
    out_part = out_part.reshape(parts, 4 * capacity, vit_width)

    places = max(1, 4 // parts)
    pieces = max(1, parts // 4)
    piece_width = vit_width // pieces

    def place_rows(array, index):
        return lax.dynamic_slice_in_dim(
            array, (index * 4 // parts) * capacity, places * capacity, 1
        )

    hidden_rows = place_rows(values, own_part) + place_rows(out_part, own_part)
    for k in range(1, parts):
        sent = place_rows(out_part, (own_part + k) % parts).astype(BF16)
        hidden_rows = hidden_rows + jnp.roll(shift(sent, k).astype(F32), k, axis=0)
    merged = layer_norm(hidden_rows).astype(BF16)
    keeping = slot_index[None, :] < own_counts[:, None]
    merged = jnp.where(
        keeping[:, None, :, None], merged.reshape(parts, places, capacity, vit_width), 0
    )
    merged = lax.dynamic_slice_in_dim(merged, (own_part % pieces) * piece_width, piece_width, 3)
    merged = jnp.swapaxes(merged, 1, 2).reshape(parts * capacity, places * piece_width)
    merged_all, owners = gather_ctx(merged)

    text = text_embed[0].astype(F32)
    text_scale = lax.rsqrt(jnp.mean(text * text, axis=-1, keepdims=True) + EPS)
    text_normed = (text * text_scale * lang_norm_gain).astype(BF16)
    part_features = width // parts

    def text_part(index):
        return lax.dynamic_slice_in_dim(text_normed, index * part_features, part_features, 1)

    text_rows = [text_part(own_part)]
    for k in range(1, parts):
        text_rows.append(shift(text_part((own_part + k) % parts), k))
    text_keys = dot(jnp.concatenate(text_rows, axis=0), key_weight).reshape(parts, tokens, -1)
    key_proj = text_keys[0]
    for k in range(1, parts):
        key_proj = key_proj + shift(text_keys[k].astype(BF16), -k).astype(F32)

    own_start = own * feature_cols
    holder_part = own_start // part_features
    candidate = lax.dynamic_slice_in_dim(key_weight, own_start % part_features, feature_cols, 0)
    key_rows = jnp.where(own_part == holder_part, candidate, jnp.zeros_like(candidate))
    held_by = [g * feature_cols // part_features for g in range(groups)]
    for k in range(1, parts):
        pairs = [
            (held_by[g] * groups + g, (held_by[g] + k) % parts * groups + g) for g in range(groups)
        ]
        key_rows = key_rows + lax.ppermute(candidate, ("dp", "ctx"), pairs)
    own_gain = lax.dynamic_slice_in_dim(lang_norm_gain, own_start, feature_cols, 0)

    own_range = target_range[0] == own
    image_first = jnp.sum(jnp.where(own_range, start_pos[0], 0))
    own_cols = jnp.sum(jnp.where(own_range, grid_cols[0], 0))
    image_count = jnp.sum(jnp.where(own_range, counts[0], 0))
    local_index = jnp.arange(tokens, dtype=jnp.int32)
    inner_index = local_index - (image_first - own * tokens)
    image_mask = (inner_index >= 0) & (inner_index < image_count)
    selector = (inner_index[:, None] == slot_index[None, :]) & (slot_index < image_count)[None, :]
    global_index = own * tokens + local_index
    inner_safe = jnp.clip(inner_index, 0, capacity - 1)
    pos_t = jnp.where(image_mask, image_first, global_index)
    pos_h = jnp.where(image_mask, image_first + inner_safe // own_cols, global_index)
    pos_w = jnp.where(image_mask, image_first + inner_safe % own_cols, global_index)
    cosine, sines = rope_tables(pos_t, pos_h, pos_w)
    grad_key = rotate(
        key_cotangent[0].astype(F32).reshape(tokens, key_width // HD, HD), cosine, -sines
    ).reshape(tokens, -1)
    grad_image_key = dot(selector.T.astype(F32), grad_key, precision=HIGHEST).astype(BF16)
    grads = jnp.concatenate(gather_dp(grad_image_key), axis=0)
    grads = lax.all_gather(grads, "ctx", axis=0, tiled=True)
    grads = grads.reshape(groups, parts, capacity, key_width)
    block_owner = (owners[:, None] == group_index[None, :]).astype(jnp.int32)
    block_range = jnp.sum(block_owner[None] * target_range[:, None, :], axis=-1)
    routing = (block_range[:, :, None] == group_index[None, None, :]).astype(BF16)
    grads = jnp.einsum("rih,hrkw->irkw", routing, grads, preferred_element_type=F32).astype(BF16)
    weighted = (
        lax.dot_general(
            grads.reshape(-1, key_width),
            key_rows,
            (((1,), (1,)), ((), ())),
            preferred_element_type=F32,
        )
        * own_gain
    )

    embed_part = dot(merged_all, merger).reshape(groups, parts, capacity, feature_cols)
    embedded = embed_part
    for k in range(1, parts):
        embedded = embedded + jnp.roll(shift(embed_part.astype(BF16), k).astype(F32), k, axis=1)
    embedded = embedded.reshape(-1, feature_cols).astype(BF16)
    values = embedded.astype(F32)
    sums = jnp.stack([jnp.sum(values * values, axis=-1), jnp.sum(values * weighted, axis=-1)])
    sums = jnp.swapaxes(sums.reshape(2, groups, -1), 0, 1).reshape(groups, -1)
    block_owner = block_owner.astype(F32)
    sums = dot(block_owner.T, sums, precision=HIGHEST)
    sums = lax.all_to_all(
        jnp.broadcast_to(sums[None], (groups,) + sums.shape), "ctx", 0, 0, tiled=True
    )
    sums = dot(block_owner, jnp.sum(sums, axis=0), precision=HIGHEST).reshape(groups, 2, -1)
    row_scale = lax.rsqrt(sums[:, 0] / width + EPS)
    slope = (row_scale**3 * sums[:, 1] / width).reshape(-1, 1)
    grad_embedded = (row_scale.reshape(-1, 1) * weighted - values * slope).astype(BF16)
    merger_grad = lax.dot_general(
        merged_all, grad_embedded, (((0,), (0,)), ((), ())), preferred_element_type=F32
    )

    own_seq = values.reshape(groups, parts, capacity, feature_cols)[:, 0] * own_gain
    image_part = dot(own_seq.reshape(-1, feature_cols).astype(BF16), key_rows).astype(BF16)
    outgoing = jnp.einsum(
        "ih,ikw->hkw",
        routing[0],
        image_part.reshape(groups, capacity, key_width),
        preferred_element_type=F32,
    ).astype(BF16)
    arrived = lax.all_to_all(outgoing, "ctx", 0, 0, tiled=True)
    image_scale = jnp.sum(
        jnp.where(
            (block_range[0] == own)[:, None],
            row_scale.reshape(groups, parts, capacity)[:, 0],
            0.0,
        ),
        axis=0,
    )
    image_keys = jnp.sum(arrived.astype(F32), axis=0) * image_scale[:, None]
    placed = dot(selector.astype(F32), image_keys, precision=HIGHEST)
    key_proj = jnp.where(image_mask[:, None], placed, key_proj)
    rotated = (
        rotate(key_proj.reshape(tokens, key_width // HD, HD), cosine, sines)
        .reshape(tokens, -1)
        .astype(BF16)
    )
    return (rotated[None], merger_grad)


def solution(mesh):
    return jax.shard_map(
        on_device,
        mesh=mesh,
        in_specs=(
            P("dp", "ctx", None),
            P(),
            P("dp", None),
            P("dp", None),
            P("dp", "ctx"),
            P("dp", "ctx", None),
            P(),
            P("dp", None),
            P("dp", "ctx", None),
            P("dp", None, None),
            P("dp", None),
        ),
        out_specs=(P("dp", "ctx", None), P("dp", "ctx")),
        check_vma=False,
    )
```

time: 470 us -> 172 us (0.37)
  waiting for transfers between devices: 284 us -> 34 us
  other arithmetic: 58.6 us -> 22 us
  starting transfers between devices: 7.42 us -> 28.1 us
  blocking collectives: 47.8 us -> 28.7 us
  between operations: 17.8 us -> 3.93 us
    all_gather x4 -> x0, waiting for transfers between devices: 202 us -> none  [the longest x1 67 us: on_device(): lax.all_gather(merger, 'dp', axis=0, tiled=True)]
    reduce_scatter x2 -> x0, waiting for transfers between devices: 71.3 us -> none  [the longest x1 62.3 us: on_device(): lax.psum_scatter(lax.dot_general(merged_all, grad_all, (((0,), (0,)), (()...]
    unnamed x1 -> x0, other arithmetic: 45.2 us -> none
    all_to_all x2 -> x0, blocking collectives: 43.4 us -> none  [the longest x1 28 us: on_device(): lax.all_to_all(normed, 'dp', split_axis=1, concat_axis=0, tiled=True)]
    ppermute x0 -> x13, waiting for transfers between devices: none -> 30 us  [the longest x8 18.2 us: shift(): return lax.ppermute(x, 'dp', [(i, (i + k) % size) for i in range(size)])]
    all_gather x1, blocking collectives: 4.4 us -> 28.7 us  [on_device(): grads = lax.all_gather(grads, 'ctx', axis=0, tiled=True)]
    ppermute x0 -> x13, starting transfers between devices: none -> 20.3 us  [the longest x8 9.52 us: shift(): return lax.ppermute(x, 'dp', [(i, (i + k) % size) for i in range(size)])]
    dynamic_slice x1 -> x5, local copies, waits for them, and re-layouts: 0.58 us -> 8.39 us  [the longest x1 3.3 us: head_weights(): lax.dynamic_index_in_dim(qkv_blocks, index, 2, keepdims=False)]
  transfers between devices with their start and end apart: 8 -> 15, of which waited for: 8 -> 7; matrix products, arithmetic and copies ran while one was open for 3% -> 42% of each run, Pallas kernels for 0% -> 0%
where the time goes in v1:
time: 172 us; the launch traced here: 170 us
  waiting for transfers between devices  34 us (20%)
  blocking collectives  28.7 us (17%)
  local copies, waits for them, and re-layouts  28.1 us (16%)
  starting transfers between devices  28.1 us (16%)
  matrix products  25.5 us (15%)
  other arithmetic  22 us (13%)
  between operations  3.93 us (2%)
    all_gather x1, blocking collectives, on_device(): grads = lax.all_gather(grads, 'ctx', axis=0, tiled=True)  28.7 us
    ppermute x8, waiting for transfers between devices, shift(): return lax.ppermute(x, 'dp', [(i, (i + k) % size) for i in range(size)])  18.2 us
    dot_general x11, matrix products, dot(): return jnp.dot(a, b, preferred_element_type=F32, **kw)  13.8 us
    ppermute x4, waiting for transfers between devices, gather_ctx(): other = lax.ppermute(x, 'ctx', [(i, i ^ stride) for i in range(groups)])  11.8 us
    ppermute x8, starting transfers between devices, shift(): return lax.ppermute(x, 'dp', [(i, (i + k) % size) for i in range(size)])  9.52 us
    unnamed x52, local copies, waits for them, and re-layouts  8.32 us
    ppermute x4, starting transfers between devices, gather_ctx(): other = lax.ppermute(x, 'ctx', [(i, i ^ stride) for i in range(groups)])  6.08 us
    dot_general x1, matrix products, on_device(): lax.dot_general(merged_all, grad_embedded, (((0,), (0,)), ((), ())), pref...  6.08 us
  transfers between devices with their start and end apart: 15, of which 7 were waited for; matrix products, arithmetic and copies ran while one was open for 42% of the time, Pallas kernels for 0%

profile of v1, /device:TPU:0, one launch (start us, length us, event | category | flops | bytes accessed | tf_op | source)
XLA Modules:
  0.0 170.4 jit_solution(13405503743995200871)
XLA Ops:
  1.5 3.0 %collective-permute-start = (s32[3,16]{1,0:T(4,128)S(1)}, s32[3,16]{1,0:T(4,128)S(1)}, u32[]{:S(2)}, u32[]{:S(2)}) collective-permute-start(s32[3,16]{1,0:T(4,128)S(1)} %get-tuple-element.39), channel_id=1, source_target_pairs={{0,16},{16,0},{1,17},{17,1},{2,18},{18,2},{3,19},{19,3},{4,20},{20... | collective-permute-start | bytes 584 | tf_op jit(solution)/shard_map/ppermute | solution.py:60
  5.7 1.9 %constant_dynamic-slice_fusion.2 = bf16[512,512]{1,0:T(8,128)(2,1)} fusion(bf16[4096,512]{1,0:T(8,128)(2,1)} %param.19, s32[]{:T(128)S(6)} %select_n.225), kind=kLoop, calls=%fused_computation.117 | loop fusion | bytes 1048580 | tf_op jit(solution)/shard_map/dynamic_slice | solution.py:192
  7.6 4.7 %collective-permute-start.9 = (bf16[512,512]{1,0:T(8,128)(2,1)}, bf16[512,512]{1,0:T(8,128)(2,1)}, u32[]{:S(2)}, u32[]{:S(2)}) collective-permute-start(bf16[512,512]{1,0:T(8,128)(2,1)} %constant_dynamic-slice_fusion.2), channel_id=1, source_target_pairs={{0,16},{1,17},{2,18},{3,19},{4,20},{5,21},{6,22},{7,23},{24,8},{25... | collective-permute-start | bytes 1572872 | tf_op jit(solution)/shard_map/ppermute | solution.py:199
  12.3 2.2 %fusion = f32[128]{0:T(128)S(1)} fusion(bf16[1,128,8192]{2,1,0:T(8,128)(2,1)} %param.17), kind=kLoop, calls=%fused_computation.2 | loop fusion | flops 3145600 | bytes 2097664 | tf_op jit(solution)/shard_map/reduce_sum | solution.py:175
  14.5 1.9 %fusion.2 = bf16[128,8192]{1,0:T(8,128)(2,1)} fusion(bf16[1,128,8192]{2,1,0:T(8,128)(2,1)S(1)} %copy-done.1, f32[8192]{0:T(1024)S(1)} %copy-done.10, f32[128]{0:T(128)S(1)} %add_rsqrt_fusion.2), kind=kLoop, calls=%fused_computation.4 | loop fusion | flops 4194304 | bytes 4227584 | tf_op jit(solution)/shard_map/convert_element_type | solution.py:176
  16.4 3.1 %constant_dynamic-slice_fusion.1 = (bf16[128,4096]{1,0:T(8,128)(2,1)}, bf16[128,4096]{1,0:T(8,128)(2,1)}) fusion(bf16[128,8192]{1,0:T(8,128)(2,1)} %fusion.2, s32[]{:T(128)S(6)} %select_n.238, s32[]{:T(128)S(6)} %select_n.239), kind=kLoop, calls=%fused_computation.116 | loop fusion | bytes 4194312 | tf_op jit(solution)/shard_map/dynamic_slice | solution.py:180
  20.1 4.3 %copy.49 = bf16[640,1920]{0,1:T(8,128)(2,1)} copy(bf16[640,1920]{1,0:T(8,128)(2,1)} %param.14) | data formatting | bytes 4915200 | tf_op args[2]
  25.2 3.3 %constant_dynamic-slice_fusion.3 = (bf16[640,3,1,320]{0,3,2,1:T(8,128)(2,1)}, bf16[640,3,1,320]{0,3,2,1:T(8,128)(2,1)}) fusion(bf16[640,3,2,320]{0,3,2,1:T(8,128)(2,1)} %bitcast.126, s32[]{:T(128)S(6)} %select_n.217, s32[]{:T(128)S(6)} %select_n.215), kind=kLoop, calls=%fused_computation.118 | loop fusion | bytes 4915208 | tf_op jit(solution)/shard_map/jit(dynamic_index_in_dim)/dynamic_slice | solution.py:130
  36.3 2.5 %convolution_convert_fusion.4 = bf16[128,960]{0,1:T(8,128)(2,1)} fusion(bf16[128,640]{1,0:T(8,128)(2,1)S(1)} %bitcast.140, bf16[640,960]{0,1:T(8,128)(2,1)} %bitcast.128), kind=kOutput, calls=%fused_computation.16 | convolution fusion | flops 157409280 | bytes 1638400 | tf_op jit(solution)/shard_map/dot_general | solution.py:25
  38.7 1.8 %copy.50 = bf16[128,960]{1,0:T(8,128)(2,1)} copy(bf16[128,960]{0,1:T(8,128)(2,1)} %convolution_convert_fusion.4) | data formatting | bytes 491520 | tf_op jit(solution)/shard_map/convert_element_type | solution.py:137
  40.5 2.0 %collective-permute-start.2 = (bf16[2,64,960]{2,1,0:T(8,128)(2,1)}, bf16[2,64,960]{2,1,0:T(8,128)(2,1)S(1)}, u32[]{:S(2)}, u32[]{:S(2)}) collective-permute-start(bf16[2,64,960]{2,1,0:T(8,128)(2,1)} %bitcast.147), channel_id=1, source_target_pairs={{0,16},{16,0},{1,17},{17,1},{2,18},{18,2},{3,19},{19,3},{4,20},{20... | collective-permute-start | bytes 737288 | tf_op jit(solution)/shard_map/ppermute | solution.py:60
  42.5 1.8 %multiply_subtract_fusion = (f32[128,4,64]{2,1,0:T(4,128)}, f32[128,4,64]{2,1,0:T(4,128)}) fusion(f32[128,4,128]{2,1,0:T(4,128)S(1)} %reshape.562, f32[128,64]{1,0:T(8,128)} %get-tuple-element.37, f32[128,64]{1,0:T(8,128)S(1)} %get-tuple-element.38), kind=kLoop, calls=%fused_computation.64 | loop fusion | flops 196608 | bytes 589824 | tf_op jit(solution)/shard_map/sub | solution.py:51
  44.3 6.2 %collective-permute-done.2 = bf16[2,64,960]{2,1,0:T(8,128)(2,1)S(1)} collective-permute-done((bf16[2,64,960]{2,1,0:T(8,128)(2,1)}, bf16[2,64,960]{2,1,0:T(8,128)(2,1)S(1)}, u32[]{:S(2)}, u32[]{:S(2)}) %collective-permute-start.2) | collective-permute-done | bytes 245792 | tf_op jit(solution)/shard_map/ppermute | solution.py:60
  58.0 2.4 %collective-permute-start.3 = (bf16[2,32,1280]{2,1,0:T(8,128)(2,1)S(1)}, bf16[2,32,1280]{2,1,0:T(8,128)(2,1)S(1)}, u32[]{:S(2)}, u32[]{:S(2)}) collective-permute-start(bf16[2,32,1280]{2,1,0:T(8,128)(2,1)S(1)} %dynamic-slice_convert_fusion), channel_id=1, source_target_pairs={{0,16},{16,0},{1,17},{17,1},{2,18},{18,2},{3,19},{19,3},{4,20},{20... | collective-permute-start | bytes 491528 | tf_op jit(solution)/shard_map/ppermute | solution.py:60
  60.5 3.2 %collective-permute-done.3 = bf16[2,32,1280]{2,1,0:T(8,128)(2,1)S(1)} collective-permute-done((bf16[2,32,1280]{2,1,0:T(8,128)(2,1)S(1)}, bf16[2,32,1280]{2,1,0:T(8,128)(2,1)S(1)}, u32[]{:S(2)}, u32[]{:S(2)}) %collective-permute-start.3) | collective-permute-done | bytes 163872 | tf_op jit(solution)/shard_map/ppermute | solution.py:60
  64.5 3.2 %collective-permute-start.4 = (bf16[32,2560]{1,0:T(8,128)(2,1)S(1)}, bf16[32,2560]{1,0:T(8,128)(2,1)S(1)}, u32[]{:S(2)}, u32[]{:S(2)}) collective-permute-start(bf16[32,2560]{1,0:T(8,128)(2,1)S(1)} %bitcast.130), channel_id=1, source_target_pairs={{0,8},{1,9},{2,10},{3,11},{4,12},{5,13},{6,14},{7,15},{8,0},{9,1},... | collective-permute-start | bytes 491528 | tf_op jit(solution)/shard_map/ppermute | solution.py:75
  68.5 4.4 %collective-permute-done.4 = bf16[32,2560]{1,0:T(8,128)(2,1)S(1)} collective-permute-done((bf16[32,2560]{1,0:T(8,128)(2,1)S(1)}, bf16[32,2560]{1,0:T(8,128)(2,1)S(1)}, u32[]{:S(2)}, u32[]{:S(2)}) %collective-permute-start.4) | collective-permute-done | bytes 163872 | tf_op jit(solution)/shard_map/ppermute | solution.py:75
  75.2 4.9 %collective-permute-done.5 = bf16[64,2560]{1,0:T(8,128)(2,1)S(1)} collective-permute-done((bf16[64,2560]{1,0:T(8,128)(2,1)S(1)}, bf16[64,2560]{1,0:T(8,128)(2,1)S(1)}, u32[]{:S(2)}, u32[]{:S(2)}) %collective-permute-start.5) | collective-permute-done | bytes 327712 | tf_op jit(solution)/shard_map/ppermute | solution.py:75
  80.1 1.6 collective-permute-start.6
  82.3 28.7 %all_gather.3 = bf16[512,512]{1,0:T(8,128)(2,1)S(1)} all-gather(bf16[32,512]{1,0:T(8,128)(2,1)S(1)} %pad_maximum_fusion.6), channel_id=1, replica_groups=mesh['dp'=2,'ctx'=16] {'ctx'}, dimensions={0}, use_global_device_ids=true | all-gather | bytes 557056 | tf_op jit(solution)/shard_map/all_gather | solution.py:221
  111.6 2.6 %collective-permute-done.7 = bf16[256,2560]{1,0:T(8,128)(2,1)S(1)} collective-permute-done((bf16[256,2560]{1,0:T(8,128)(2,1)S(1)}, bf16[256,2560]{1,0:T(8,128)(2,1)S(1)}, u32[]{:S(2)}, u32[]{:S(2)}) %collective-permute-start.7) | collective-permute-done | bytes 1310752 | tf_op jit(solution)/shard_map/ppermute | solution.py:75
  114.3 1.5 fusion.79
  117.7 2.5 %fusion.3 = f32[256,512]{1,0:T(8,128)S(1)} fusion(bf16[4096,512]{1,0:T(8,128)(2,1)S(1)} %copy-done.9, bf16[128,4096]{1,0:T(8,128)(2,1)} %collective-permute-done.11, bf16[128,4096]{1,0:T(8,128)(2,1)S(1)} %copy-done.4), kind=kOutput, calls=%fused_computation.6 | convolution fusion | flops 1077936128 | bytes 6815744 | tf_op jit(solution)/shard_map/dot_general | solution.py:25
  122.0 8.7 %collective-permute-done.8 = bf16[16,2,16,512]{3,2,1,0:T(8,128)(2,1)S(1)} collective-permute-done((bf16[16,2,16,512]{3,2,1,0:T(8,128)(2,1)S(1)}, bf16[16,2,16,512]{3,2,1,0:T(8,128)(2,1)S(1)}, u32[]{:S(2)}, u32[]{:S(2)}) %collective-permute-start.8) | collective-permute-done | bytes 524320 | tf_op jit(solution)/shard_map/ppermute | solution.py:60
  130.9 2.7 %multiply_reduce_fusion.1 = (f32[512]{0:T(512)S(1)}, f32[512]{0:T(512)S(1)}, bf16[512,512]{1,0:T(8,128)(2,1)S(1)}, f32[512,512]{1,0:T(8,128)}) fusion(f32[512,512]{1,0:T(8,128)S(1)} %get-tuple-element.44, f32[16,2,16,512]{3,2,1,0:T(8,128)S(1)} %pad_maximum_fusion.1, f32[512]{0:T(512)S(1)} %dynamic_slice.38, bf16[512,512]{1,0:T(8,128)(2,1)S(1)} %bitcast.138, ...), kind=kOutput, calls=%fused_computation.28 | convolution fusion | flops 271055872 | bytes 5249025 | tf_op jit(solution)/shard_map/dot_general | solution.py:228
  135.8 4.3 %all-to-all-start.1 = ((f32[16,1,1024]{2,1,0:T(1,128)}), f32[16,1,1024]{2,1,0:T(1,128)}, u32[]{:S(2)}, u32[]{:S(2)}) async-start(f32[16,1,1024]{2,1,0:T(1,128)} %reshape.569), calls=%async_computation.1 | async-start | bytes 131072 | tf_op jit(solution)/shard_map/all_to_all | solution.py:247
  140.1 1.6 convolution_convert_fusion.3
  142.8 4.0 %all-to-all-done.1 = f32[16,1,1024]{2,1,0:T(1,128)} async-done(((f32[16,1,1024]{2,1,0:T(1,128)}), f32[16,1,1024]{2,1,0:T(1,128)}, u32[]{:S(2)}, u32[]{:S(2)}) %all-to-all-start.1) | async-done | bytes 65568 | tf_op jit(solution)/shard_map/all_to_all | solution.py:247
  146.8 3.5 %all-to-all-start = ((bf16[16,16,512]{2,1,0:T(8,128)(2,1)}), bf16[16,16,512]{2,1,0:T(8,128)(2,1)S(1)}, u32[]{:S(2)}, u32[]{:S(2)}) async-start(bf16[16,16,512]{2,1,0:T(8,128)(2,1)} %copy.58), calls=%async_computation | async-start | bytes 524288 | tf_op jit(solution)/shard_map/all_to_all | solution.py:266
  150.9 2.3 %reduce = f32[16,1024]{1,0:T(8,128)} reduce(f32[16,1,1024]{2,1,0:T(1,128)} %all-to-all-done.1, f32[]{:T(128)} %broadcast.550), dimensions={1}, to_apply=%all_to_all.7.reduce_sub_computation | reduce | bytes 131076 | tf_op jit(solution)/shard_map/all_to_all | solution.py:247
  153.1 1.6 reshape.570
  161.5 6.1 %fusion.14 = f32[2560,512]{1,0:T(8,128)} fusion(bf16[512,2560]{1,0:T(8,128)(2,1)} %copy-done.3, f32[512,512]{1,0:T(8,128)} %get-tuple-element.45, bf16[512,512]{1,0:T(8,128)(2,1)S(1)} %get-tuple-element.7, f32[512]{0:T(512)S(1)} %fusion.59, f32[512]{0:T(512)} %rsqrt.46), kind=kOutput, calls=%fused_computation.33 | convolution fusion | flops 1343488000 | bytes 9441280 | tf_op jit(solution)/shard_map/dot_general | solution.py:254
  (153 shorter events, 38.1 us)
Async XLA Ops:
  0.6 113.6 %copy-start = (bf16[2560,512]{1,0:T(8,128)(2,1)S(1)}, bf16[2560,512]{1,0:T(8,128)(2,1)}, u32[]{:S(2)}) copy-start(bf16[2560,512]{1,0:T(8,128)(2,1)} %param.16) | copy-start | bytes 7864324
  0.6 13.9 %copy-start.10 = (f32[8192]{0:T(1024)S(1)}, f32[8192]{0:T(1024)}, u32[]{:S(2)}) copy-start(f32[8192]{0:T(1024)} %param.18) | copy-start | bytes 98308
  1.5 27.0 %collective-permute-start = (s32[3,16]{1,0:T(4,128)S(1)}, s32[3,16]{1,0:T(4,128)S(1)}, u32[]{:S(2)}, u32[]{:S(2)}) collective-permute-start(s32[3,16]{1,0:T(4,128)S(1)} %get-tuple-element.39), channel_id=1, source_target_pairs={{0,16},{16,0},{1,17},{17,1},{2,18},{18,2},{3,19},{19,3},{4,20},{20... | collective-permute-start | bytes 584 | tf_op jit(solution)/shard_map/ppermute | solution.py:60
  5.6 30.1 %collective-permute-start.1 = (bf16[64,1280]{1,0:T(8,128)(2,1)S(1)}, bf16[64,1280]{1,0:T(8,128)(2,1)S(1)}, u32[]{:S(2)}, u32[]{:S(2)}) collective-permute-start(bf16[64,1280]{1,0:T(8,128)(2,1)S(1)} %convolution_convert_fusion), channel_id=1, source_target_pairs={{0,16},{16,0},{1,17},{17,1},{2,18},{18,2},{3,19},{19,3},{4,20},{20... | collective-permute-start | bytes 491528 | tf_op jit(solution)/shard_map/ppermute | solution.py:60
  7.6 123.3 %collective-permute-start.9 = (bf16[512,512]{1,0:T(8,128)(2,1)}, bf16[512,512]{1,0:T(8,128)(2,1)}, u32[]{:S(2)}, u32[]{:S(2)}) collective-permute-start(bf16[512,512]{1,0:T(8,128)(2,1)} %constant_dynamic-slice_fusion.2), channel_id=1, source_target_pairs={{0,16},{1,17},{2,18},{3,19},{4,20},{5,21},{6,22},{7,23},{24,8},{25... | collective-permute-start | bytes 1572872 | tf_op jit(solution)/shard_map/ppermute | solution.py:199
  19.5 4.9 %copy-start.8 = (bf16[1,128,512]{2,1,0:T(8,128)(2,1)S(1)}, bf16[1,128,512]{2,1,0:T(8,128)(2,1)}, u32[]{:S(2)}) copy-start(bf16[1,128,512]{2,1,0:T(8,128)(2,1)} %param.20) | copy-start | bytes 393220
  19.5 97.2 %collective-permute-start.11 = (bf16[128,4096]{1,0:T(8,128)(2,1)}, bf16[128,4096]{1,0:T(8,128)(2,1)}, u32[]{:S(2)}, u32[]{:S(2)}) collective-permute-start(bf16[128,4096]{1,0:T(8,128)(2,1)} %get-tuple-element.17), channel_id=1, source_target_pairs={{0,16},{16,0},{1,17},{17,1},{2,18},{18,2},{3,19},{19,3},{4,20},{20... | collective-permute-start | bytes 3145736 | tf_op jit(solution)/shard_map/ppermute | solution.py:60
  20.1 4.5 %copy-start.21 = (s32[16]{0:T(128)S(1)}, s32[16]{0:T(128)}, u32[]{:S(2)}) copy-start(s32[16]{0:T(128)} %constant.193.clone) | copy-start | bytes 196
  24.5 4.0 %copy-start.17 = (f32[1280]{0:T(1024)S(1)}, f32[1280]{0:T(1024)}, u32[]{:S(2)}) copy-start(f32[1280]{0:T(1024)} %param.13) | copy-start | bytes 15364
  24.5 10.2 %copy-start.18 = (pred[64]{0:T(512)(128)(4,1)S(1)}, pred[64]{0:T(512)(128)(4,1)}, u32[]{:S(2)}) copy-start(pred[64]{0:T(512)(128)(4,1)} %get-tuple-element.51) | copy-start | bytes 196
  33.2 2.9 %copy-start.11 = (pred[128]{0:T(512)(128)(4,1)}, pred[128]{0:T(512)(128)(4,1)S(1)}, u32[]{:S(2)}) copy-start(pred[128]{0:T(512)(128)(4,1)S(1)} %get-tuple-element.9) | copy-start | bytes 388
  35.8 38.0 %copy-start.13 = (s32[128]{0:T(128)}, s32[128]{0:T(128)S(1)}, u32[]{:S(2)}) copy-start(s32[128]{0:T(128)S(1)} %iota_subtract_fusion) | copy-start | bytes 1540
  40.5 10.0 %copy-start.2 = (bf16[640,3,1,320]{0,3,2,1:T(8,128)(2,1)S(1)}, bf16[640,3,1,320]{0,3,2,1:T(8,128)(2,1)}, u32[]{:S(2)}) copy-start(bf16[640,3,1,320]{0,3,2,1:T(8,128)(2,1)} %get-tuple-element.15) | copy-start | bytes 3686404
  40.5 10.0 %collective-permute-start.2 = (bf16[2,64,960]{2,1,0:T(8,128)(2,1)}, bf16[2,64,960]{2,1,0:T(8,128)(2,1)S(1)}, u32[]{:S(2)}, u32[]{:S(2)}) collective-permute-start(bf16[2,64,960]{2,1,0:T(8,128)(2,1)} %bitcast.147), channel_id=1, source_target_pairs={{0,16},{16,0},{1,17},{17,1},{2,18},{18,2},{3,19},{19,3},{4,20},{20... | collective-permute-start | bytes 737288 | tf_op jit(solution)/shard_map/ppermute | solution.py:60
  57.9 10.3 %copy-start.5 = (f32[128,4,64]{2,1,0:T(4,128)S(1)}, f32[128,4,64]{2,1,0:T(4,128)}, u32[]{:S(2)}) copy-start(f32[128,4,64]{2,1,0:T(4,128)} %get-tuple-element.25) | copy-start | bytes 393220
  57.9 10.3 %copy-start.6 = (f32[128,4,64]{2,1,0:T(4,128)S(1)}, f32[128,4,64]{2,1,0:T(4,128)}, u32[]{:S(2)}) copy-start(f32[128,4,64]{2,1,0:T(4,128)} %get-tuple-element.26) | copy-start | bytes 393220
  58.0 5.7 %collective-permute-start.3 = (bf16[2,32,1280]{2,1,0:T(8,128)(2,1)S(1)}, bf16[2,32,1280]{2,1,0:T(8,128)(2,1)S(1)}, u32[]{:S(2)}, u32[]{:S(2)}) collective-permute-start(bf16[2,32,1280]{2,1,0:T(8,128)(2,1)S(1)} %dynamic-slice_convert_fusion), channel_id=1, source_target_pairs={{0,16},{16,0},{1,17},{17,1},{2,18},{18,2},{3,19},{19,3},{4,20},{20... | collective-permute-start | bytes 491528 | tf_op jit(solution)/shard_map/ppermute | solution.py:60
  64.5 8.4 %collective-permute-start.4 = (bf16[32,2560]{1,0:T(8,128)(2,1)S(1)}, bf16[32,2560]{1,0:T(8,128)(2,1)S(1)}, u32[]{:S(2)}, u32[]{:S(2)}) collective-permute-start(bf16[32,2560]{1,0:T(8,128)(2,1)S(1)} %bitcast.130), channel_id=1, source_target_pairs={{0,8},{1,9},{2,10},{3,11},{4,12},{5,13},{6,14},{7,15},{8,0},{9,1},... | collective-permute-start | bytes 491528 | tf_op jit(solution)/shard_map/ppermute | solution.py:75
  68.2 5.6 %copy-start.15 = (pred[16]{0:T(512)(128)(4,1)}, pred[16]{0:T(512)(128)(4,1)S(1)}, u32[]{:S(2)}) copy-start(pred[16]{0:T(512)(128)(4,1)S(1)} %iota_compare_fusion.9) | copy-start | bytes 52
  72.9 7.1 %collective-permute-start.5 = (bf16[64,2560]{1,0:T(8,128)(2,1)S(1)}, bf16[64,2560]{1,0:T(8,128)(2,1)S(1)}, u32[]{:S(2)}, u32[]{:S(2)}) collective-permute-start(bf16[64,2560]{1,0:T(8,128)(2,1)S(1)} %pad_maximum_fusion.3), channel_id=1, source_target_pairs={{0,4},{1,5},{2,6},{3,7},{4,0},{5,1},{6,2},{7,3},{8,12},{9,13},{10,... | collective-permute-start | bytes 983048 | tf_op jit(solution)/shard_map/ppermute | solution.py:75
  74.1 8.2 %collective-permute-start.10 = (bf16[16,512]{1,0:T(8,128)(2,1)S(1)}, bf16[16,512]{1,0:T(8,128)(2,1)S(1)}, u32[]{:S(2)}, u32[]{:S(2)}) collective-permute-start(bf16[16,512]{1,0:T(8,128)(2,1)S(1)} %convolution_convert_fusion.6), channel_id=1, source_target_pairs={{0,16},{16,0},{1,17},{17,1},{2,18},{18,2},{3,19},{19,3},{4,20},{20... | collective-permute-start | bytes 49160 | tf_op jit(solution)/shard_map/ppermute | solution.py:60
  80.1 30.9 %collective-permute-start.6 = (bf16[128,2560]{1,0:T(8,128)(2,1)S(1)}, bf16[128,2560]{1,0:T(8,128)(2,1)S(1)}, u32[]{:S(2)}, u32[]{:S(2)}) collective-permute-start(bf16[128,2560]{1,0:T(8,128)(2,1)S(1)} %pad_maximum_fusion.2), channel_id=1, source_target_pairs={{0,2},{1,3},{2,0},{3,1},{4,6},{5,7},{6,4},{7,5},{8,10},{9,11},{10,... | collective-permute-start | bytes 1966088 | tf_op jit(solution)/shard_map/ppermute | solution.py:75
  111.0 3.1 %collective-permute-start.7 = (bf16[256,2560]{1,0:T(8,128)(2,1)S(1)}, bf16[256,2560]{1,0:T(8,128)(2,1)S(1)}, u32[]{:S(2)}, u32[]{:S(2)}) collective-permute-start(bf16[256,2560]{1,0:T(8,128)(2,1)S(1)} %pad_maximum_fusion), channel_id=1, source_target_pairs={{0,1},{1,0},{2,3},{3,2},{4,5},{5,4},{6,7},{7,6},{8,9},{9,8},{10,11... | collective-permute-start | bytes 3932168 | tf_op jit(solution)/shard_map/ppermute | solution.py:75
  114.3 3.4 %copy-start.9 = (bf16[4096,512]{1,0:T(8,128)(2,1)S(1)}, bf16[4096,512]{1,0:T(8,128)(2,1)}, u32[]{:S(2)}) copy-start(bf16[4096,512]{1,0:T(8,128)(2,1)} %param.19) | copy-start | bytes 12582916
  115.8 14.9 %collective-permute-start.8 = (bf16[16,2,16,512]{3,2,1,0:T(8,128)(2,1)S(1)}, bf16[16,2,16,512]{3,2,1,0:T(8,128)(2,1)S(1)}, u32[]{:S(2)}, u32[]{:S(2)}) collective-permute-start(bf16[16,2,16,512]{3,2,1,0:T(8,128)(2,1)S(1)} %bitcast.156), channel_id=1, source_target_pairs={{0,16},{16,0},{1,17},{17,1},{2,18},{18,2},{3,19},{19,3},{4,20},{20... | collective-permute-start | bytes 1572872 | tf_op jit(solution)/shard_map/ppermute | solution.py:60
  121.0 47.0 %collective-permute-start.12 = (bf16[128,512]{1,0:T(8,128)(2,1)}, bf16[128,512]{1,0:T(8,128)(2,1)}, u32[]{:S(2)}, u32[]{:S(2)}) collective-permute-start(bf16[128,512]{1,0:T(8,128)(2,1)} %slice.181), channel_id=1, source_target_pairs={{0,16},{16,0},{1,17},{17,1},{2,18},{18,2},{3,19},{19,3},{4,20},{20... | collective-permute-start | bytes 393224 | tf_op jit(solution)/shard_map/ppermute | solution.py:60
  130.9 3.8 %copy-start.20 = (s32[16]{0:T(128)S(1)}, s32[16]{0:T(128)}, u32[]{:S(2)}) copy-start(s32[16]{0:T(128)} %copy-done.19) | copy-start | bytes 196
  135.8 11.1 %all-to-all-start.1 = ((f32[16,1,1024]{2,1,0:T(1,128)}), f32[16,1,1024]{2,1,0:T(1,128)}, u32[]{:S(2)}, u32[]{:S(2)}) async-start(f32[16,1,1024]{2,1,0:T(1,128)} %reshape.569), calls=%async_computation.1 | async-start | bytes 131072 | tf_op jit(solution)/shard_map/all_to_all | solution.py:247
  146.8 20.7 %all-to-all-start = ((bf16[16,16,512]{2,1,0:T(8,128)(2,1)}), bf16[16,16,512]{2,1,0:T(8,128)(2,1)S(1)}, u32[]{:S(2)}, u32[]{:S(2)}) async-start(bf16[16,16,512]{2,1,0:T(8,128)(2,1)} %copy.58), calls=%async_computation | async-start | bytes 524288 | tf_op jit(solution)/shard_map/all_to_all | solution.py:266
  161.5 6.2 %copy-start.14 = (s32[128]{0:T(128)S(1)}, s32[128]{0:T(128)}, u32[]{:S(2)}) copy-start(s32[128]{0:T(128)} %copy-done.13) | copy-start | bytes 1540
  161.5 6.2 %copy-start.16 = (pred[16]{0:T(512)(128)(4,1)S(1)}, pred[16]{0:T(512)(128)(4,1)}, u32[]{:S(2)}) copy-start(pred[16]{0:T(512)(128)(4,1)} %copy-done.15) | copy-start | bytes 52
  161.5 6.5 %copy-start.12 = (pred[128]{0:T(512)(128)(4,1)S(1)}, pred[128]{0:T(512)(128)(4,1)}, u32[]{:S(2)}) copy-start(pred[128]{0:T(512)(128)(4,1)} %copy-done.11) | copy-start | bytes 388
  (5 other events, 8.6 us)

commit v2 on v1

v2 whole, which is shorter than its diff:
```python
import math

import jax
import jax.numpy as jnp
from jax import lax
from jax.experimental import pallas as pl
from jax.experimental.pallas import tpu as pltpu
from jax.sharding import PartitionSpec as P

VHD = 80
HD = 128
EPS = 1e-06
THETA = 1000000.0
HIGHEST = lax.Precision.HIGHEST
BF16 = jnp.bfloat16
F32 = jnp.float32


def layer_norm(values):
    average = jnp.mean(values, axis=-1, keepdims=True)
    centered = values - average
    variance = jnp.mean(centered * centered, axis=-1, keepdims=True)
    return centered * lax.rsqrt(variance + EPS)


def dot(a, b, **kw):
    return jnp.dot(a, b, preferred_element_type=F32, **kw)


def rope_tables(pos_t, pos_h, pos_w):
    half_dim = HD // 2
    freq_index = jnp.arange(half_dim, dtype=jnp.int32)
    inverse = THETA ** (-(2.0 * freq_index.astype(F32)) / HD)
    first_cut = HD // 8
    second_cut = first_cut + 3 * HD // 16
    chosen = jnp.where(
        freq_index[None, :] < first_cut,
        pos_t[:, None],
        jnp.where(freq_index[None, :] < second_cut, pos_h[:, None], pos_w[:, None]),
    )
    angles = chosen.astype(F32) * inverse[None, :]
    return (jnp.cos(angles), jnp.sin(angles))


def rotate(vectors, cosine, sines):
    half_dim = vectors.shape[-1] // 2
    first_half = vectors[..., :half_dim]
    second_half = vectors[..., half_dim:]
    cos_part = cosine[:, None, :]
    sin_part = sines[:, None, :]
    return jnp.concatenate(
        [
            first_half * cos_part - second_half * sin_part,
            second_half * cos_part + first_half * sin_part,
        ],
        axis=-1,
    )


def shift(x, k):
    size = lax.axis_size("dp")
    return lax.ppermute(x, "dp", [(i, (i + k) % size) for i in range(size)])


def gather_dp(x):
    return [x] + [shift(x, k) for k in range(1, lax.axis_size("dp"))]


def strides_of(size):
    return [1 << b for b in reversed(range(size.bit_length() - 1))]


def xor_gather(x, strides):
    size = lax.axis_size("ctx")
    pieces = [x]
    offsets = [[0]]
    for stride in strides:
        known = [o for piece in offsets for o in piece]
        joined = pieces[0] if len(pieces) == 1 else jnp.concatenate(pieces, axis=0)
        pieces.append(lax.ppermute(joined, "ctx", [(i, i ^ stride) for i in range(size)]))
        offsets.append([o ^ stride for o in known])
    return pieces, offsets


def gather_ctx(x):
    size = lax.axis_size("ctx")
    if size & (size - 1):
        return lax.all_gather(x, "ctx", axis=0, tiled=True), jnp.arange(size, dtype=jnp.int32)
    pieces, offsets = xor_gather(x, strides_of(size))
    order = [o for piece in offsets for o in piece]
    return jnp.concatenate(pieces, axis=0), lax.axis_index("ctx") ^ jnp.asarray(order, jnp.int32)


def gather_pieces(x):
    size = lax.axis_size("ctx")
    if size & (size - 1) or size < 8:
        x, owners = gather_ctx(x)
        return [(x, 0, list(range(size)))], owners
    strides = strides_of(size)
    middle = x.shape[1] // 2
    pieces, offsets = xor_gather(x[:, :middle], strides)
    order = [o for piece in offsets for o in piece]
    found = [(p, 0, [order.index(o) for o in piece]) for p, piece in zip(pieces, offsets)]
    pieces, offsets = xor_gather(x[:, middle:], strides[-2:-1] + strides[:-2] + strides[-1:])
    found += [(p, middle, [order.index(o) for o in piece]) for p, piece in zip(pieces, offsets)]
    return found, lax.axis_index("ctx") ^ jnp.asarray(order, jnp.int32)


SMEM = pl.BlockSpec(memory_space=pltpu.SMEM)
VMEM = pl.BlockSpec(memory_space=pltpu.VMEM)


def call(kernel, outs, ins, scalars=0, scratch=(), name=None):
    return pl.pallas_call(
        kernel,
        out_shape=outs,
        in_specs=[SMEM] * scalars + [VMEM] * (len(ins) - scalars),
        out_specs=[VMEM] * len(outs),
        scratch_shapes=list(scratch),
        name=name,
    )(*ins)


def project(parts, index, images, gain, weight):
    rows, width = images[0].shape
    depth, columns = weight.shape
    third = columns // 3
    block = third // parts

    def kernel(index_ref, *refs):
        image_refs = refs[:parts]
        gain_ref, weight_ref, mine_ref, sent_ref = refs[parts:]
        own = index_ref[0]
        pieces = []
        for r in range(parts):
            normed = layer_norm(image_refs[r][...].astype(F32)) * gain_ref[...]
            piece = normed[:, :depth]
            for b in range(1, parts):
                piece = jnp.where(own == b, normed[:, b * depth : (b + 1) * depth], piece)
            pieces.append(piece.astype(BF16))
        product = dot(jnp.concatenate(pieces, axis=0), weight_ref[...])
        for b in range(parts):
            heads = jnp.concatenate(
                [product[:, j * third + b * block : j * third + (b + 1) * block] for j in range(3)],
                axis=1,
            )

            @pl.when(own == b)
            def _():
                mine_ref[...] = heads.reshape(parts, rows, 3 * block)

            for k in range(1, parts):

                @pl.when((own + k) % parts == b)
                def _():
                    for r in range(parts):
                        sent_ref[k - 1, (r + k) % parts] = heads[r * rows : (r + 1) * rows].astype(
                            BF16
                        )

    return call(
        kernel,
        (
            jax.ShapeDtypeStruct((parts, rows, 3 * block), F32),
            jax.ShapeDtypeStruct((parts - 1, parts, rows, 3 * block), BF16),
        ),
        (index, *images, gain, weight),
        scalars=1,
        name="project",
    )


def attend(parts, places, scalars, mine, received, images, out_weight):
    rows, width = images[0].shape
    capacity = rows // 4
    block = out_weight.shape[0]
    heads = block // VHD
    taken = places * capacity

    def kernel(scalar_ref, *refs):
        mine_ref = refs[0]
        received_refs = refs[1:parts]
        image_refs = refs[parts : 2 * parts]
        weight_ref, hidden_ref, sent_ref, scratch = refs[2 * parts :]
        own = scalar_ref[0]
        lane = lax.broadcasted_iota(jnp.int32, (rows, block), 1)
        key_slot = lax.broadcasted_iota(jnp.int32, (heads * rows, rows), 1) % capacity
        attended = []
        for r in range(parts):
            total = mine_ref[r]
            for ref in received_refs:
                total = total + ref[r].astype(F32)
            total = total.astype(BF16)
            queries = total[:, :block]
            keys = total[:, block : 2 * block]
            contents = total[:, 2 * block :]
            in_head = [(lane >= h * VHD) & (lane < (h + 1) * VHD) for h in range(heads)]
            stacked = jnp.concatenate(
                [jnp.where(inside, queries, jnp.zeros_like(queries)) for inside in in_head], axis=0
            )
            scores = lax.dot_general(
                stacked, keys, (((1,), (1,)), ((), ())), preferred_element_type=F32
            ) / math.sqrt(VHD)
            alive = (key_slot < scalar_ref[1 + r]).astype(F32)
            weights = jnp.exp(scores) * alive
            probability = (weights / jnp.sum(weights, axis=-1, keepdims=True)).astype(BF16)
            spread = dot(probability, contents)
            picked = jnp.where(in_head[0], spread[:rows], 0.0)
            for h in range(1, heads):
                picked = picked + jnp.where(in_head[h], spread[h * rows : (h + 1) * rows], 0.0)
            attended.append(picked.astype(BF16))
        product = dot(jnp.concatenate(attended, axis=0), weight_ref[...])
        scratch[...] = product.reshape(parts, rows, width)

        def start(index):
            return pl.multiple_of((index * 4 // parts) * capacity, capacity)

        for r in range(parts):
            at = pl.ds(start(own), taken)
            hidden_ref[r] = scratch[r, at, :] + image_refs[r][at, :].astype(F32)
            for k in range(1, parts):
                at = pl.ds(start((own + k) % parts), taken)
                sent_ref[k - 1, (r + k) % parts] = scratch[r, at, :].astype(BF16)

    return call(
        kernel,
        (
            jax.ShapeDtypeStruct((parts, taken, width), F32),
            jax.ShapeDtypeStruct((parts - 1, parts, taken, width), BF16),
        ),
        (scalars, mine, *received, *images, out_weight),
        scalars=1,
        scratch=[pltpu.VMEM((parts, rows, width), F32)],
        name="attend",
    )


def embed(rows, groups, pieces, weight):
    depth, columns = weight.shape
    count = len(pieces)

    def kernel(*refs):
        weight_ref, merged_ref, part_ref, sent_ref = refs[count:]
        for ref, (array, column, blocks) in zip(refs[:count], pieces):
            for j, block in enumerate(blocks):
                merged_ref[block * rows : (block + 1) * rows, column : column + array.shape[1]] = ref[
                    j * rows : (j + 1) * rows
                ]
        product = dot(merged_ref[...], weight_ref[...])
        part_ref[...] = product
        sent_ref[...] = product.astype(BF16)

    total = groups * rows
    return call(
        kernel,
        (
            jax.ShapeDtypeStruct((total, depth), BF16),
            jax.ShapeDtypeStruct((total, columns), F32),
            jax.ShapeDtypeStruct((total, columns), BF16),
        ),
        (*[p[0] for p in pieces], weight),
        name="embed",
    )


def features(parts, groups, owners, holders, own_part, received, weighted, gain, key_rows):
    total, columns = own_part.shape
    rows = total // groups
    capacity = rows // parts
    key_width = key_rows.shape[1]
    count = len(received)

    def kernel(owner_ref, holder_ref, *refs):
        part_ref = refs[0]
        received_refs = refs[1 : 1 + count]
        weighted_ref, gain_ref, key_ref, embed_ref, sums_ref, keys_ref = refs[1 + count :]
        picked = []
        for i in range(groups):
            at = pl.ds(i * rows, rows)
            block = part_ref[at, :]
            for ref in received_refs:
                block = block + ref[at, :].astype(F32)
            block = block.astype(BF16)
            picked.append((block[:capacity].astype(F32) * gain_ref[...]).astype(BF16))
            embed_ref[pl.ds(pl.multiple_of(owner_ref[i] * rows, rows), rows), :] = block
        values = embed_ref[...].astype(F32)
        ones = jnp.ones((8, columns), F32)
        contract = (((1,), (1,)), ((), ()))
        squares = lax.dot_general(
            ones, values * values, contract, precision=HIGHEST, preferred_element_type=F32
        )
        products = lax.dot_general(
            ones, values * weighted_ref[...], contract, precision=HIGHEST, preferred_element_type=F32
        )
        for i in range(groups):
            sums_ref[i, 0:1] = squares[0:1]
            sums_ref[i, 1:2] = products[0:1]
        terms = dot(jnp.concatenate(picked, axis=0), key_ref[...]).astype(BF16)
        for i in range(groups):
            keys_ref[holder_ref[i]] = terms[i * capacity : (i + 1) * capacity]

    return call(
        kernel,
        (
            jax.ShapeDtypeStruct((total, columns), BF16),
            jax.ShapeDtypeStruct((groups, 2, total), F32),
            jax.ShapeDtypeStruct((groups, capacity, key_width), BF16),
        ),
        (owners, holders, own_part, *received, weighted, gain, key_rows),
        scalars=2,
        name="features",
    )


def finish(groups, width, owners, sums, embedded, weighted, merged):
    total, columns = embedded.shape
    rows = total // groups
    height = merged.shape[1]
    bands = 5 if height % (5 * 128) == 0 else 1
    band = height // bands

    def kernel(
        owner_ref, sums_ref, embed_ref, weighted_ref, merged_ref, out_ref, scale_ref, grads, ordered
    ):
        @pl.when(pl.program_id(0) == 0)
        def _():
            whole = jnp.sum(sums_ref[...], axis=0)
            scale = lax.rsqrt(whole[0:1] / width + EPS)
            slope = scale**3 * whole[1:2] / width
            line = lax.broadcasted_iota(jnp.int32, (8, total), 0)
            both = jnp.where(line == 0, scale, slope)
            scale_ref[...] = both
            columns_of = jnp.transpose(both)
            grads[...] = (
                columns_of[:, 0:1] * weighted_ref[...]
                - embed_ref[...].astype(F32) * columns_of[:, 1:2]
            ).astype(BF16)
            for i in range(groups):
                ordered[pl.ds(i * rows, rows), :] = grads[
                    pl.ds(pl.multiple_of(owner_ref[i] * rows, rows), rows), :
                ]

        out_ref[...] = lax.dot_general(
            merged_ref[...], ordered[...], (((0,), (0,)), ((), ())), preferred_element_type=F32
        )

    return pl.pallas_call(
        kernel,
        grid=(bands,),
        out_shape=(
            jax.ShapeDtypeStruct((height, columns), F32),
            jax.ShapeDtypeStruct((8, total), F32),
        ),
        in_specs=[
            SMEM,
            pl.BlockSpec(sums.shape, lambda g: (0, 0, 0)),
            pl.BlockSpec(embedded.shape, lambda g: (0, 0)),
            pl.BlockSpec(weighted.shape, lambda g: (0, 0)),
            pl.BlockSpec((total, band), lambda g: (0, g)),
        ],
        out_specs=[
            pl.BlockSpec((band, columns), lambda g: (g, 0)),
            pl.BlockSpec((8, total), lambda g: (0, 0)),
        ],
        scratch_shapes=[pltpu.VMEM((total, columns), BF16), pltpu.VMEM((total, columns), BF16)],
        compiler_params=pltpu.CompilerParams(dimension_semantics=("arbitrary",)),
        name="finish",
    )(owners, sums, embedded, weighted, merged)


def text_norm(parts, index, text, gain):
    tokens, width = text.shape
    step = 32 if tokens % 32 == 0 else tokens
    block = width // parts

    def kernel(index_ref, text_ref, gain_ref, out_ref, scratch):
        values = text_ref[...].astype(F32)
        scale = lax.rsqrt(jnp.mean(values * values, axis=-1, keepdims=True) + EPS)
        scratch[...] = (values * scale * gain_ref[...]).astype(BF16)
        for k in range(parts):
            start = pl.multiple_of((index_ref[0] + k) % parts * block, block)
            out_ref[k] = scratch[:, pl.ds(start, block)]

    return pl.pallas_call(
        kernel,
        grid=(tokens // step,),
        out_shape=jax.ShapeDtypeStruct((parts, tokens, block), BF16),
        in_specs=[
            SMEM,
            pl.BlockSpec((step, width), lambda g: (g, 0)),
            pl.BlockSpec((1, width), lambda g: (0, 0)),
        ],
        out_specs=pl.BlockSpec((parts, step, block), lambda g: (0, g, 0)),
        scratch_shapes=[pltpu.VMEM((step, width), BF16)],
        name="text_norm",
    )(index, text, gain)


def on_device(
    patches,
    vit_norm_gain,
    vit_qkv,
    vit_out,
    merger,
    text_embed,
    lang_norm_gain,
    key_weight,
    key_cotangent,
    image_grid,
    image_start,
):
    parts = lax.axis_size("dp")
    groups = lax.axis_size("ctx")
    own_part = lax.axis_index("dp")
    own = lax.axis_index("ctx")
    tokens, width = text_embed.shape[1:]
    vit_width = patches.shape[2]
    capacity = patches.shape[1] // 4
    key_width = key_weight.shape[1]
    feature_cols = merger.shape[1]

    info = jnp.concatenate([image_grid[0].T, image_start], axis=0)
    infos = jnp.stack(gather_dp(info))
    grid_rows, grid_cols, start_pos = infos[:, 0], infos[:, 1], infos[:, 2]
    counts = grid_rows * grid_cols
    target_range = start_pos // tokens
    group_index = jnp.arange(groups, dtype=jnp.int32)
    slot_index = jnp.arange(capacity, dtype=jnp.int32)
    own_counts = jnp.sum(jnp.where(group_index[None] == own, counts, 0), axis=1)

    row = jnp.arange(4 * capacity, dtype=jnp.int32)
    source_row = (row % capacity) * 4 + row // capacity
    order_rows = (source_row[:, None] == row[None, :]).astype(BF16)
    own_rows = dot(order_rows, patches[0]).astype(BF16)
    images = gather_dp(own_rows)
    part_index = own_part.astype(jnp.int32).reshape(1)
    mine, sent = project(parts, part_index, images, vit_norm_gain.reshape(1, -1), vit_qkv)
    received = [shift(sent[k - 1], k) for k in range(1, parts)]
    places = max(1, 4 // parts)
    pieces = max(1, parts // 4)
    piece_width = vit_width // pieces
    scalars = jnp.concatenate([part_index, own_counts])
    hidden_rows, sent = attend(parts, places, scalars, mine, received, images, vit_out)
    for k in range(1, parts):
        hidden_rows = hidden_rows + shift(sent[k - 1], k).astype(F32)
    merged = layer_norm(hidden_rows).astype(BF16)
    keeping = slot_index[None, :] < own_counts[:, None]
    merged = jnp.where(
        keeping[:, None, :, None], merged.reshape(parts, places, capacity, vit_width), 0
    )
    merged = lax.dynamic_slice_in_dim(merged, (own_part % pieces) * piece_width, piece_width, 3)
    merged = jnp.swapaxes(merged, 1, 2).reshape(parts * capacity, places * piece_width)
    merged_pieces, owners = gather_pieces(merged)

    gain_line = lang_norm_gain.reshape(1, -1)
    text_blocks = text_norm(parts, part_index, text_embed[0], gain_line)
    part_features = width // parts
    text_rows = [text_blocks[0]] + [shift(text_blocks[k], k) for k in range(1, parts)]
    text_keys = dot(jnp.concatenate(text_rows, axis=0), key_weight).reshape(parts, tokens, -1)
    key_proj = text_keys[0]
    for k in range(1, parts):
        key_proj = key_proj + shift(text_keys[k].astype(BF16), -k).astype(F32)

    own_start = own * feature_cols
    holder_part = own_start // part_features
    candidate = lax.dynamic_slice_in_dim(key_weight, own_start % part_features, feature_cols, 0)
    key_rows = jnp.where(own_part == holder_part, candidate, jnp.zeros_like(candidate))
    held_by = [g * feature_cols // part_features for g in range(groups)]
    for k in range(1, parts):
        pairs = [
            (held_by[g] * groups + g, (held_by[g] + k) % parts * groups + g) for g in range(groups)
        ]
        key_rows = key_rows + lax.ppermute(candidate, ("dp", "ctx"), pairs)
    own_gain = lax.dynamic_slice_in_dim(lang_norm_gain, own_start, feature_cols, 0).reshape(1, -1)

    own_range = target_range[0] == own
    image_first = jnp.sum(jnp.where(own_range, start_pos[0], 0))
    own_cols = jnp.sum(jnp.where(own_range, grid_cols[0], 0))
    image_count = jnp.sum(jnp.where(own_range, counts[0], 0))
    local_index = jnp.arange(tokens, dtype=jnp.int32)
    inner_index = local_index - (image_first - own * tokens)
    image_mask = (inner_index >= 0) & (inner_index < image_count)
    selector = (inner_index[:, None] == slot_index[None, :]) & (slot_index < image_count)[None, :]
    global_index = own * tokens + local_index
    inner_safe = jnp.clip(inner_index, 0, capacity - 1)
    pos_t = jnp.where(image_mask, image_first, global_index)
    pos_h = jnp.where(image_mask, image_first + inner_safe // own_cols, global_index)
    pos_w = jnp.where(image_mask, image_first + inner_safe % own_cols, global_index)
    cosine, sines = rope_tables(pos_t, pos_h, pos_w)
    grad_key = rotate(
        key_cotangent[0].astype(F32).reshape(tokens, key_width // HD, HD), cosine, -sines
    ).reshape(tokens, -1)
    grad_image_key = dot(selector.T.astype(F32), grad_key, precision=HIGHEST).astype(BF16)
    grads = jnp.concatenate(gather_dp(grad_image_key), axis=0)
    grads, _ = gather_ctx(grads)
    grads = grads.reshape(groups, parts, capacity, key_width)
    routing = (target_range[:, :, None] == owners[None, None, :]).astype(BF16)
    grads = jnp.einsum("roi,irkw->orkw", routing, grads, preferred_element_type=F32).astype(BF16)
    weighted = (
        lax.dot_general(
            grads.reshape(-1, key_width),
            key_rows,
            (((1,), (1,)), ((), ())),
            preferred_element_type=F32,
        )
        * own_gain
    )

    merged_all, embed_part, embed_sent = embed(parts * capacity, groups, merged_pieces, merger)
    embed_sent = embed_sent.reshape(groups, parts, capacity, feature_cols)
    received = [
        jnp.roll(shift(embed_sent, k), k, axis=1).reshape(-1, feature_cols)
        for k in range(1, parts)
    ]
    block_owner = (owners[:, None] == group_index[None, :]).astype(jnp.int32)
    block_range = jnp.sum(block_owner * target_range[0][None, :], axis=-1)
    embedded, sums, outgoing = features(
        parts, groups, owners, block_range, embed_part, received, weighted, own_gain, key_rows
    )
    sums = lax.all_to_all(sums, "ctx", 0, 0, tiled=True)
    arrived = lax.all_to_all(outgoing, "ctx", 0, 0, tiled=True)
    merger_grad, scales = finish(
        groups, float(width), owners, sums, embedded, weighted, merged_all
    )

    image_scale = jnp.sum(
        jnp.where(
            (target_range[0] == own)[:, None],
            scales[0].reshape(groups, parts, capacity)[:, 0],
            0.0,
        ),
        axis=0,
    )
    image_keys = jnp.sum(arrived.astype(F32), axis=0) * image_scale[:, None]
    placed = dot(selector.astype(F32), image_keys, precision=HIGHEST)
    key_proj = jnp.where(image_mask[:, None], placed, key_proj)
    rotated = (
        rotate(key_proj.reshape(tokens, key_width // HD, HD), cosine, sines)
        .reshape(tokens, -1)
        .astype(BF16)
    )
    return (rotated[None], merger_grad)


def solution(mesh):
    return jax.shard_map(
        on_device,
        mesh=mesh,
        in_specs=(
            P("dp", "ctx", None),
            P(),
            P("dp", None),
            P("dp", None),
            P("dp", "ctx"),
            P("dp", "ctx", None),
            P(),
            P("dp", None),
            P("dp", "ctx", None),
            P("dp", None, None),
            P("dp", None),
        ),
        out_specs=(P("dp", "ctx", None), P("dp", "ctx")),
        check_vma=False,
    )
```

time: 172 us -> 148 us (0.86)
  Pallas kernels: 0 us -> 29.7 us
  matrix products: 25.5 us -> 7.11 us
  local copies, waits for them, and re-layouts: 28.1 us -> 10.1 us
  blocking collectives: 28.7 us -> 11.4 us
  other arithmetic: 22 us -> 15.4 us
  starting transfers between devices: 28.1 us -> 32.5 us
  waiting for transfers between devices: 34 us -> 36.8 us
    pallas_call x0 -> x6, Pallas kernels: none -> 29.7 us  [the longest x4 17.8 us: call(): pl.pallas_call(kernel, out_shape=outs, in_specs=[SMEM] * scalars + [VMEM]...]
    all_gather x1 -> x0, blocking collectives: 28.7 us -> none  [on_device(): grads = lax.all_gather(grads, 'ctx', axis=0, tiled=True)]
    all_to_all x0 -> x1, blocking collectives: none -> 11.4 us  [on_device(): sums = lax.all_to_all(sums, 'ctx', 0, 0, tiled=True)]
    ppermute x4 -> x12, starting transfers between devices: 6.08 us -> 16.7 us  [xor_gather(): lax.ppermute(joined, 'ctx', [(i, i ^ stride) for i in range(size)])]
    dot_general x5 -> x1, matrix products: 9.02 us -> 0.43 us  [on_device(): jnp.einsum('roi,irkw->orkw', routing, grads, preferred_element_type=F32)]
    dot_general x11 -> x4, matrix products: 13.8 us -> 5.21 us  [dot(): return jnp.dot(a, b, preferred_element_type=F32, **kw)]
    dynamic_slice x3 -> x0, local copies, waits for them, and re-layouts: 6.45 us -> none  [the longest x1 3.3 us: head_weights(): lax.dynamic_index_in_dim(qkv_blocks, index, 2, keepdims=False)]
    unnamed x52, local copies, waits for them, and re-layouts: 8.32 us -> 2.72 us
  transfers between devices with their start and end apart: 15 -> 22, of which waited for: 7 -> 10; matrix products, arithmetic and copies ran while one was open for 42% -> 20% of each run, Pallas kernels for 0% -> 20%
where the time goes in v2:
time: 148 us; the launch traced here: 147 us
  waiting for transfers between devices  36.8 us (25%)
  starting transfers between devices  32.5 us (22%)
  Pallas kernels  29.7 us (20%)
  other arithmetic  15.4 us (10%)
  blocking collectives  11.4 us (8%)
  local copies, waits for them, and re-layouts  10.1 us (7%)
  matrix products  7.11 us (5%)
  between operations  3.79 us (3%)
    ppermute x8, waiting for transfers between devices, shift(): return lax.ppermute(x, 'dp', [(i, (i + k) % size) for i in range(size)])  21.6 us
    pallas_call x4, Pallas kernels, call(): pl.pallas_call(kernel, out_shape=outs, in_specs=[SMEM] * scalars + [VMEM]...  17.8 us
    ppermute x12, starting transfers between devices, xor_gather(): lax.ppermute(joined, 'ctx', [(i, i ^ stride) for i in range(size)])  16.7 us
    ppermute x12, waiting for transfers between devices, xor_gather(): lax.ppermute(joined, 'ctx', [(i, i ^ stride) for i in range(size)])  15.2 us
    all_to_all x1, blocking collectives, on_device(): sums = lax.all_to_all(sums, 'ctx', 0, 0, tiled=True)  11.4 us
    ppermute x8, starting transfers between devices, shift(): return lax.ppermute(x, 'dp', [(i, (i + k) % size) for i in range(size)])  8.31 us
    pallas_call x1, Pallas kernels, finish(): pl.pallas_call(kernel, grid=(bands,), out_shape=(jax.ShapeDtypeStruct((he...  7.4 us
    dot_general x4, matrix products, dot(): return jnp.dot(a, b, preferred_element_type=F32, **kw)  5.21 us
  transfers between devices with their start and end apart: 22, of which 10 were waited for; matrix products, arithmetic and copies ran while one was open for 20% of the time, Pallas kernels for 20%

profile of v2, /device:TPU:0, one launch (start us, length us, event | category | flops | bytes accessed | tf_op | source)
XLA Modules:
  0.0 146.8 jit_solution(14736428005992241508)
XLA Ops:
  1.4 3.0 %collective-permute-start = (s32[3,16]{1,0:T(4,128)S(1)}, s32[3,16]{1,0:T(4,128)S(1)}, u32[]{:S(2)}, u32[]{:S(2)}) collective-permute-start(s32[3,16]{1,0:T(4,128)S(1)} %get-tuple-element.58), channel_id=1, source_target_pairs={{0,16},{16,0},{1,17},{17,1},{2,18},{18,2},{3,19},{19,3},{4,20},{20... | collective-permute-start | bytes 584 | tf_op jit(solution)/shard_map/ppermute | solution.py:62
  5.9 3.8 %collective-permute-start.18 = (bf16[512,512]{1,0:T(8,128)(2,1)S(1)}, bf16[512,512]{1,0:T(8,128)(2,1)S(1)}, u32[]{:S(2)}, u32[]{:S(2)}) collective-permute-start(bf16[512,512]{1,0:T(8,128)(2,1)S(1)} %constant_dynamic-slice_fusion), channel_id=1, source_target_pairs={{0,16},{1,17},{2,18},{3,19},{4,20},{5,21},{6,22},{7,23},{24,8},{25... | collective-permute-start | bytes 1572872 | tf_op jit(solution)/shard_map/ppermute | solution.py:473
  9.7 4.5 %text_norm.1 = bf16[2,128,4096]{2,1,0:T(8,128)(2,1)} custom-call(s32[1]{0:T(128)} %bitcast.9.index_ref, bf16[128,8192]{1,0:T(8,128)(2,1)} %bitcast.68, f32[1,8192]{1,0:T(1,128)} %bitcast.74), custom_call_target="tpu_custom_call" | custom-call | tf_op jit(solution)/shard_map/text_norm/pallas_call | solution.py:384
  14.2 2.8 %slice_bitcast_fusion.1 = (bf16[128,4096]{1,0:T(8,128)(2,1)S(1)}, bf16[128,4096]{1,0:T(8,128)(2,1)}) fusion(bf16[2,128,4096]{2,1,0:T(8,128)(2,1)} %text_norm.1), kind=kLoop, calls=%fused_computation.10 | loop fusion | bytes 4194304 | tf_op jit(solution)/shard_map/squeeze | solution.py:458
  18.6 1.3 fusion.34
  24.5 1.4 add_select_fusion.1
  28.3 2.0 %collective-permute-start.13 = (bf16[16,512]{1,0:T(8,128)(2,1)S(1)}, bf16[16,512]{1,0:T(8,128)(2,1)S(1)}, u32[]{:S(2)}, u32[]{:S(2)}) collective-permute-start(bf16[16,512]{1,0:T(8,128)(2,1)S(1)} %get-tuple-element.61), channel_id=1, source_target_pairs={{0,16},{16,0},{1,17},{17,1},{2,18},{18,2},{3,19},{19,3},{4,20},{20... | collective-permute-start | bytes 49160 | tf_op jit(solution)/shard_map/ppermute | solution.py:62
  31.6 3.8 %project.1 = (f32[2,64,960]{2,1,0:T(8,128)}, bf16[1,2,64,960]{3,2,1,0:T(8,128)(2,1)}) custom-call(s32[1]{0:T(128)} %bitcast.9.index_ref, bf16[64,1280]{1,0:T(8,128)(2,1)} %copy-done.4, bf16[64,1280]{1,0:T(8,128)(2,1)} %copy-done.11, f32[1,1280]{1,0:T(1,128)} %reshape.433.refs_2_, bf16[640,1920]{1,0:T(8,128)(2,1)} %refs_3_.1), custom_call_target="tpu_custom_call" | custom-call | tf_op jit(solution)/shard_map/project/pallas_call | solution.py:114
  35.4 9.4 %collective-permute-done.13 = bf16[16,512]{1,0:T(8,128)(2,1)S(1)} collective-permute-done((bf16[16,512]{1,0:T(8,128)(2,1)S(1)}, bf16[16,512]{1,0:T(8,128)(2,1)S(1)}, u32[]{:S(2)}, u32[]{:S(2)}) %collective-permute-start.13) | collective-permute-done | bytes 16416 | tf_op jit(solution)/shard_map/ppermute | solution.py:62
  44.8 3.6 %collective-permute-start.14 = (bf16[32,512]{1,0:T(8,128)(2,1)S(1)}, bf16[32,512]{1,0:T(8,128)(2,1)S(1)}, u32[]{:S(2)}, u32[]{:S(2)}) collective-permute-start(bf16[32,512]{1,0:T(8,128)(2,1)S(1)} %pad_maximum_fusion.11), channel_id=1, source_target_pairs={{0,8},{1,9},{2,10},{3,11},{4,12},{5,13},{6,14},{7,15},{8,0},{9,1},... | collective-permute-start | bytes 98312 | tf_op jit(solution)/shard_map/ppermute | solution.py:80
  49.0 1.4 collective-permute-done.14
  50.4 1.5 %collective-permute-start.15 = (bf16[64,512]{1,0:T(8,128)(2,1)S(1)}, bf16[64,512]{1,0:T(8,128)(2,1)S(1)}, u32[]{:S(2)}, u32[]{:S(2)}) collective-permute-start(bf16[64,512]{1,0:T(8,128)(2,1)S(1)} %pad_maximum_fusion.10), channel_id=1, source_target_pairs={{0,4},{1,5},{2,6},{3,7},{4,0},{5,1},{6,2},{7,3},{8,12},{9,13},{10,... | collective-permute-start | bytes 196616 | tf_op jit(solution)/shard_map/ppermute | solution.py:80
  52.6 3.5 %attend.1 = (f32[2,32,1280]{2,1,0:T(8,128)}, bf16[1,2,32,1280]{3,2,1,0:T(8,128)(2,1)}) custom-call(s32[3]{0:T(128)} %pad_add_fusion.3.scalar_ref, f32[2,64,960]{2,1,0:T(8,128)} %get-tuple-element.14.refs_0_, bf16[2,64,960]{2,1,0:T(8,128)(2,1)} %copy-done.12, bf16[64,1280]{1,0:T(8,128)(2,1)} %copy-done.4, bf16[64,1280]{1,0:T(8,128)(2,1)} %copy-done.11, ...), custom_call_target="tpu_custom_call" | custom-call | tf_op jit(solution)/shard_map/attend/pallas_call | solution.py:114
  56.1 1.8 %collective-permute-start.3 = (bf16[2,32,1280]{2,1,0:T(8,128)(2,1)}, bf16[2,32,1280]{2,1,0:T(8,128)(2,1)S(1)}, u32[]{:S(2)}, u32[]{:S(2)}) collective-permute-start(bf16[2,32,1280]{2,1,0:T(8,128)(2,1)} %bitcast.83), channel_id=1, source_target_pairs={{0,16},{16,0},{1,17},{17,1},{2,18},{18,2},{3,19},{19,3},{4,20},{20... | collective-permute-start | bytes 491528 | tf_op jit(solution)/shard_map/ppermute | solution.py:62
  58.5 1.6 %collective-permute-start.16 = (bf16[128,512]{1,0:T(8,128)(2,1)S(1)}, bf16[128,512]{1,0:T(8,128)(2,1)S(1)}, u32[]{:S(2)}, u32[]{:S(2)}) collective-permute-start(bf16[128,512]{1,0:T(8,128)(2,1)S(1)} %pad_maximum_fusion.8), channel_id=1, source_target_pairs={{0,2},{1,3},{2,0},{3,1},{4,6},{5,7},{6,4},{7,5},{8,10},{9,11},{10,... | collective-permute-start | bytes 393224 | tf_op jit(solution)/shard_map/ppermute | solution.py:80
  60.1 1.5 %collective-permute-done.3 = bf16[2,32,1280]{2,1,0:T(8,128)(2,1)S(1)} collective-permute-done((bf16[2,32,1280]{2,1,0:T(8,128)(2,1)}, bf16[2,32,1280]{2,1,0:T(8,128)(2,1)S(1)}, u32[]{:S(2)}, u32[]{:S(2)}) %collective-permute-start.3) | collective-permute-done | bytes 163872 | tf_op jit(solution)/shard_map/ppermute | solution.py:62
  65.9 1.6 %collective-permute-start.8 = (bf16[32,1280]{1,0:T(8,128)(2,1)S(1)}, bf16[32,1280]{1,0:T(8,128)(2,1)S(1)}, u32[]{:S(2)}, u32[]{:S(2)}) collective-permute-start(bf16[32,1280]{1,0:T(8,128)(2,1)S(1)} %get-tuple-element.40.refs_5_), channel_id=1, source_target_pairs={{0,2},{1,3},{2,0},{3,1},{4,6},{5,7},{6,4},{7,5},{8,10},{9,11},{10,... | collective-permute-start | bytes 245768 | tf_op jit(solution)/shard_map/ppermute | solution.py:80
  67.5 3.2 %collective-permute-start.4 = (bf16[32,1280]{1,0:T(8,128)(2,1)S(1)}, bf16[32,1280]{1,0:T(8,128)(2,1)S(1)}, u32[]{:S(2)}, u32[]{:S(2)}) collective-permute-start(bf16[32,1280]{1,0:T(8,128)(2,1)S(1)} %get-tuple-element.41.refs_0_), channel_id=1, source_target_pairs={{0,8},{1,9},{2,10},{3,11},{4,12},{5,13},{6,14},{7,15},{8,0},{9,1},... | collective-permute-start | bytes 245768 | tf_op jit(solution)/shard_map/ppermute | solution.py:80
  70.7 2.9 %collective-permute-start.9 = (bf16[64,1280]{1,0:T(8,128)(2,1)S(1)}, bf16[64,1280]{1,0:T(8,128)(2,1)S(1)}, u32[]{:S(2)}, u32[]{:S(2)}) collective-permute-start(bf16[64,1280]{1,0:T(8,128)(2,1)S(1)} %pad_maximum_fusion.7), channel_id=1, source_target_pairs={{0,8},{1,9},{2,10},{3,11},{4,12},{5,13},{6,14},{7,15},{8,0},{9,1},... | collective-permute-start | bytes 491528 | tf_op jit(solution)/shard_map/ppermute | solution.py:80
  74.6 4.0 %collective-permute-done.9.refs_7_ = bf16[64,1280]{1,0:T(8,128)(2,1)S(1)} collective-permute-done((bf16[64,1280]{1,0:T(8,128)(2,1)S(1)}, bf16[64,1280]{1,0:T(8,128)(2,1)S(1)}, u32[]{:S(2)}, u32[]{:S(2)}) %collective-permute-start.9) | collective-permute-done | bytes 163872 | tf_op jit(solution)/shard_map/ppermute | solution.py:80
  78.7 3.4 %collective-permute-done.5.refs_2_ = bf16[64,1280]{1,0:T(8,128)(2,1)S(1)} collective-permute-done((bf16[64,1280]{1,0:T(8,128)(2,1)S(1)}, bf16[64,1280]{1,0:T(8,128)(2,1)S(1)}, u32[]{:S(2)}, u32[]{:S(2)}) %collective-permute-start.5) | collective-permute-done | bytes 163872 | tf_op jit(solution)/shard_map/ppermute | solution.py:80
  82.1 1.6 %collective-permute-start.6 = (bf16[128,1280]{1,0:T(8,128)(2,1)S(1)}, bf16[128,1280]{1,0:T(8,128)(2,1)S(1)}, u32[]{:S(2)}, u32[]{:S(2)}) collective-permute-start(bf16[128,1280]{1,0:T(8,128)(2,1)S(1)} %pad_maximum_fusion.3), channel_id=1, source_target_pairs={{0,2},{1,3},{2,0},{3,1},{4,6},{5,7},{6,4},{7,5},{8,10},{9,11},{10,... | collective-permute-start | bytes 983048 | tf_op jit(solution)/shard_map/ppermute | solution.py:80
  83.8 3.1 %collective-permute-done.10.refs_8_ = bf16[128,1280]{1,0:T(8,128)(2,1)S(1)} collective-permute-done((bf16[128,1280]{1,0:T(8,128)(2,1)S(1)}, bf16[128,1280]{1,0:T(8,128)(2,1)S(1)}, u32[]{:S(2)}, u32[]{:S(2)}) %collective-permute-start.10) | collective-permute-done | bytes 327712 | tf_op jit(solution)/shard_map/ppermute | solution.py:80
  87.0 2.3 %collective-permute-done.6.refs_3_ = bf16[128,1280]{1,0:T(8,128)(2,1)S(1)} collective-permute-done((bf16[128,1280]{1,0:T(8,128)(2,1)S(1)}, bf16[128,1280]{1,0:T(8,128)(2,1)S(1)}, u32[]{:S(2)}, u32[]{:S(2)}) %collective-permute-start.6) | collective-permute-done | bytes 327712 | tf_op jit(solution)/shard_map/ppermute | solution.py:80
  91.6 5.9 %embed.1 = (bf16[512,2560]{1,0:T(8,128)(2,1)}, f32[512,512]{1,0:T(8,128)}, bf16[512,512]{1,0:T(8,128)(2,1)}) custom-call(bf16[32,1280]{1,0:T(8,128)(2,1)} %copy-done.3, bf16[32,1280]{1,0:T(8,128)(2,1)} %copy-done.10, bf16[64,1280]{1,0:T(8,128)(2,1)} %copy-done.6, bf16[128,1280]{1,0:T(8,128)(2,1)} %copy-done.8, ...), custom_call_target="tpu_custom_call" | custom-call | tf_op jit(solution)/shard_map/embed/pallas_call | solution.py:114
  99.6 1.5 %convolution_multiply_fusion.refs_2_.weighted_ref = f32[512,512]{1,0:T(8,128)} fusion(bf16[512,512]{1,0:T(8,128)(2,1)S(1)} %bitcast.66, bf16[512,512]{1,0:T(8,128)(2,1)S(1)} %select_add_fusion.refs_4_, f32[512]{0:T(512)S(1)} %dynamic_slice.8), kind=kOutput, calls=%fused_computation.5 | convolution fusion | flops 268697600 | bytes 2099200 | tf_op jit(solution)/shard_map/dot_general | solution.py:500
  101.0 10.7 %collective-permute-done.12 = bf16[16,2,16,512]{3,2,1,0:T(8,128)(2,1)S(1)} collective-permute-done((bf16[16,2,16,512]{3,2,1,0:T(8,128)(2,1)}, bf16[16,2,16,512]{3,2,1,0:T(8,128)(2,1)S(1)}, u32[]{:S(2)}, u32[]{:S(2)}) %collective-permute-start.12) | collective-permute-done | bytes 524320 | tf_op jit(solution)/shard_map/ppermute | solution.py:62
  112.6 4.6 %features.1 = (bf16[512,512]{1,0:T(8,128)(2,1)}, f32[16,2,512]{2,1,0:T(2,128)}, bf16[16,16,512]{2,1,0:T(8,128)(2,1)}) custom-call(s32[16]{0:T(128)} %copy-done.16, s32[16]{0:T(128)} %select_reduce_fusion.1.holder_ref, f32[512,512]{1,0:T(8,128)} %get-tuple-element.18.refs_0_, bf16[512,512]{1,0:T(8,128)(2,1)} %bitcast.67, ...), custom_call_target="tpu_custom_call" | custom-call | tf_op jit(solution)/shard_map/features/pallas_call | solution.py:114
  117.3 11.4 %all_to_all.10.sums_ref = f32[16,2,512]{2,1,0:T(2,128)} all-to-all(f32[16,2,512]{2,1,0:T(2,128)} %get-tuple-element.21), channel_id=1, replica_groups=mesh['dp'=2,'ctx'=16] {'ctx'}, dimensions={0} | all-to-all | bytes 131072 | tf_op jit(solution)/shard_map/all_to_all | solution.py:520
  128.7 3.7 %all-to-all-start = ((bf16[16,16,512]{2,1,0:T(8,128)(2,1)}), bf16[16,16,512]{2,1,0:T(8,128)(2,1)S(1)}, u32[]{:S(2)}, u32[]{:S(2)}) async-start(bf16[16,16,512]{2,1,0:T(8,128)(2,1)} %get-tuple-element.20), calls=%async_computation | async-start | bytes 524288 | tf_op jit(solution)/shard_map/all_to_all | solution.py:521
  132.4 3.8 %fusion = f32[256,512]{1,0:T(8,128)S(1)} fusion(bf16[4096,512]{1,0:T(8,128)(2,1)} %param.19, bf16[128,4096]{1,0:T(8,128)(2,1)} %collective-permute-done.19, bf16[128,4096]{1,0:T(8,128)(2,1)S(1)} %get-tuple-element.32), kind=kOutput, calls=%fused_computation.1 | convolution fusion | flops 1077936128 | bytes 6815744 | tf_op jit(solution)/shard_map/dot_general | solution.py:27
  136.7 7.4 %finish.1 = (f32[2560,512]{1,0:T(8,128)}, f32[8,512]{1,0:T(8,128)}) custom-call(s32[16]{0:T(128)} %copy-done.16, f32[16,2,512]{2,1,0:T(2,128)} %all_to_all.10.sums_ref, bf16[512,512]{1,0:T(8,128)(2,1)} %get-tuple-element.22.embed_ref, f32[512,512]{1,0:T(8,128)} %convolution_multiply_fusion.refs_2_.weighted_ref, bf16[512,2560]{1,0:T(8,128)(2,1)} %get-tuple-element.23.merged_ref), custom_call_target="tpu_custom_call" | custom-call | tf_op jit(solution)/shard_map/finish/pallas_call | solution.py:347
  (135 shorter events, 25.3 us)
Async XLA Ops:
  1.4 17.2 %collective-permute-start = (s32[3,16]{1,0:T(4,128)S(1)}, s32[3,16]{1,0:T(4,128)S(1)}, u32[]{:S(2)}, u32[]{:S(2)}) collective-permute-start(s32[3,16]{1,0:T(4,128)S(1)} %get-tuple-element.58), channel_id=1, source_target_pairs={{0,16},{16,0},{1,17},{17,1},{2,18},{18,2},{3,19},{19,3},{4,20},{20... | collective-permute-start | bytes 584 | tf_op jit(solution)/shard_map/ppermute | solution.py:62
  4.6 9.6 %copy-start.4 = (bf16[64,1280]{1,0:T(8,128)(2,1)}, bf16[64,1280]{1,0:T(8,128)(2,1)S(1)}, u32[]{:S(2)}) copy-start(bf16[64,1280]{1,0:T(8,128)(2,1)S(1)} %convolution_convert_fusion.refs_0_.refs_2_) | copy-start | bytes 491524
  4.6 26.3 %collective-permute-start.1 = (bf16[64,1280]{1,0:T(8,128)(2,1)S(1)}, bf16[64,1280]{1,0:T(8,128)(2,1)S(1)}, u32[]{:S(2)}, u32[]{:S(2)}) collective-permute-start(bf16[64,1280]{1,0:T(8,128)(2,1)S(1)} %convolution_convert_fusion.refs_0_.refs_2_), channel_id=1, source_target_pairs={{0,16},{16,0},{1,17},{17,1},{2,18},{18,2},{3,19},{19,3},{4,20},{20... | collective-permute-start | bytes 491528 | tf_op jit(solution)/shard_map/ppermute | solution.py:62
  5.9 92.4 %collective-permute-start.18 = (bf16[512,512]{1,0:T(8,128)(2,1)S(1)}, bf16[512,512]{1,0:T(8,128)(2,1)S(1)}, u32[]{:S(2)}, u32[]{:S(2)}) collective-permute-start(bf16[512,512]{1,0:T(8,128)(2,1)S(1)} %constant_dynamic-slice_fusion), channel_id=1, source_target_pairs={{0,16},{1,17},{2,18},{3,19},{4,20},{5,21},{6,22},{7,23},{24,8},{25... | collective-permute-start | bytes 1572872 | tf_op jit(solution)/shard_map/ppermute | solution.py:473
  17.0 115.4 %collective-permute-start.19 = (bf16[128,4096]{1,0:T(8,128)(2,1)}, bf16[128,4096]{1,0:T(8,128)(2,1)}, u32[]{:S(2)}, u32[]{:S(2)}) collective-permute-start(bf16[128,4096]{1,0:T(8,128)(2,1)} %get-tuple-element.33), channel_id=1, source_target_pairs={{0,16},{16,0},{1,17},{17,1},{2,18},{18,2},{3,19},{19,3},{4,20},{20... | collective-permute-start | bytes 3145736 | tf_op jit(solution)/shard_map/ppermute | solution.py:62
  17.1 73.1 %copy-start.16 = (s32[16]{0:T(128)}, s32[16]{0:T(128)S(1)}, u32[]{:S(2)}) copy-start(s32[16]{0:T(128)S(1)} %broadcast_xor_fusion.owner_ref) | copy-start | bytes 196
  17.9 81.7 %copy-start.14 = (f32[512]{0:T(512)}, f32[512]{0:T(512)S(1)}, u32[]{:S(2)}) copy-start(f32[512]{0:T(512)S(1)} %dynamic_slice.8) | copy-start | bytes 6148
  28.3 16.5 %collective-permute-start.13 = (bf16[16,512]{1,0:T(8,128)(2,1)S(1)}, bf16[16,512]{1,0:T(8,128)(2,1)S(1)}, u32[]{:S(2)}, u32[]{:S(2)}) collective-permute-start(bf16[16,512]{1,0:T(8,128)(2,1)S(1)} %get-tuple-element.61), channel_id=1, source_target_pairs={{0,16},{16,0},{1,17},{17,1},{2,18},{18,2},{3,19},{19,3},{4,20},{20... | collective-permute-start | bytes 49160 | tf_op jit(solution)/shard_map/ppermute | solution.py:62
  35.4 16.5 %collective-permute-start.2 = (bf16[2,64,960]{2,1,0:T(8,128)(2,1)}, bf16[2,64,960]{2,1,0:T(8,128)(2,1)S(1)}, u32[]{:S(2)}, u32[]{:S(2)}) collective-permute-start(bf16[2,64,960]{2,1,0:T(8,128)(2,1)} %bitcast.82), channel_id=1, source_target_pairs={{0,16},{16,0},{1,17},{17,1},{2,18},{18,2},{3,19},{19,3},{4,20},{20... | collective-permute-start | bytes 737288 | tf_op jit(solution)/shard_map/ppermute | solution.py:62
  44.8 5.6 %collective-permute-start.14 = (bf16[32,512]{1,0:T(8,128)(2,1)S(1)}, bf16[32,512]{1,0:T(8,128)(2,1)S(1)}, u32[]{:S(2)}, u32[]{:S(2)}) collective-permute-start(bf16[32,512]{1,0:T(8,128)(2,1)S(1)} %pad_maximum_fusion.11), channel_id=1, source_target_pairs={{0,8},{1,9},{2,10},{3,11},{4,12},{5,13},{6,14},{7,15},{8,0},{9,1},... | collective-permute-start | bytes 98312 | tf_op jit(solution)/shard_map/ppermute | solution.py:80
  50.4 8.1 %collective-permute-start.15 = (bf16[64,512]{1,0:T(8,128)(2,1)S(1)}, bf16[64,512]{1,0:T(8,128)(2,1)S(1)}, u32[]{:S(2)}, u32[]{:S(2)}) collective-permute-start(bf16[64,512]{1,0:T(8,128)(2,1)S(1)} %pad_maximum_fusion.10), channel_id=1, source_target_pairs={{0,4},{1,5},{2,6},{3,7},{4,0},{5,1},{6,2},{7,3},{8,12},{9,13},{10,... | collective-permute-start | bytes 196616 | tf_op jit(solution)/shard_map/ppermute | solution.py:80
  56.1 5.5 %collective-permute-start.3 = (bf16[2,32,1280]{2,1,0:T(8,128)(2,1)}, bf16[2,32,1280]{2,1,0:T(8,128)(2,1)S(1)}, u32[]{:S(2)}, u32[]{:S(2)}) collective-permute-start(bf16[2,32,1280]{2,1,0:T(8,128)(2,1)} %bitcast.83), channel_id=1, source_target_pairs={{0,16},{16,0},{1,17},{17,1},{2,18},{18,2},{3,19},{19,3},{4,20},{20... | collective-permute-start | bytes 491528 | tf_op jit(solution)/shard_map/ppermute | solution.py:62
  58.5 9.0 %copy-start.22 = (bf16[256,512]{1,0:T(8,128)(2,1)S(1)}, bf16[256,512]{1,0:T(8,128)(2,1)}, u32[]{:S(2)}) copy-start(bf16[256,512]{1,0:T(8,128)(2,1)} %get-tuple-element.46) | copy-start | bytes 786436
  58.5 25.1 %collective-permute-start.16 = (bf16[128,512]{1,0:T(8,128)(2,1)S(1)}, bf16[128,512]{1,0:T(8,128)(2,1)S(1)}, u32[]{:S(2)}, u32[]{:S(2)}) collective-permute-start(bf16[128,512]{1,0:T(8,128)(2,1)S(1)} %pad_maximum_fusion.8), channel_id=1, source_target_pairs={{0,2},{1,3},{2,0},{3,1},{4,6},{5,7},{6,4},{7,5},{8,10},{9,11},{10,... | collective-permute-start | bytes 393224 | tf_op jit(solution)/shard_map/ppermute | solution.py:80
  65.9 23.4 %copy-start.2 = (bf16[32,1280]{1,0:T(8,128)(2,1)}, bf16[32,1280]{1,0:T(8,128)(2,1)S(1)}, u32[]{:S(2)}) copy-start(bf16[32,1280]{1,0:T(8,128)(2,1)S(1)} %get-tuple-element.40.refs_5_) | copy-start | bytes 245764
  65.9 23.4 %copy-start.3 = (bf16[32,1280]{1,0:T(8,128)(2,1)}, bf16[32,1280]{1,0:T(8,128)(2,1)S(1)}, u32[]{:S(2)}) copy-start(bf16[32,1280]{1,0:T(8,128)(2,1)S(1)} %get-tuple-element.41.refs_0_) | copy-start | bytes 245764
  65.9 4.8 %collective-permute-start.8 = (bf16[32,1280]{1,0:T(8,128)(2,1)S(1)}, bf16[32,1280]{1,0:T(8,128)(2,1)S(1)}, u32[]{:S(2)}, u32[]{:S(2)}) collective-permute-start(bf16[32,1280]{1,0:T(8,128)(2,1)S(1)} %get-tuple-element.40.refs_5_), channel_id=1, source_target_pairs={{0,2},{1,3},{2,0},{3,1},{4,6},{5,7},{6,4},{7,5},{8,10},{9,11},{10,... | collective-permute-start | bytes 245768 | tf_op jit(solution)/shard_map/ppermute | solution.py:80
  67.5 6.6 %collective-permute-start.4 = (bf16[32,1280]{1,0:T(8,128)(2,1)S(1)}, bf16[32,1280]{1,0:T(8,128)(2,1)S(1)}, u32[]{:S(2)}, u32[]{:S(2)}) collective-permute-start(bf16[32,1280]{1,0:T(8,128)(2,1)S(1)} %get-tuple-element.41.refs_0_), channel_id=1, source_target_pairs={{0,8},{1,9},{2,10},{3,11},{4,12},{5,13},{6,14},{7,15},{8,0},{9,1},... | collective-permute-start | bytes 245768 | tf_op jit(solution)/shard_map/ppermute | solution.py:80
  70.7 18.6 %copy-start.9 = (bf16[32,1280]{1,0:T(8,128)(2,1)}, bf16[32,1280]{1,0:T(8,128)(2,1)S(1)}, u32[]{:S(2)}) copy-start(bf16[32,1280]{1,0:T(8,128)(2,1)S(1)} %collective-permute-done.8.refs_6_) | copy-start | bytes 245764
  70.7 7.8 %collective-permute-start.9 = (bf16[64,1280]{1,0:T(8,128)(2,1)S(1)}, bf16[64,1280]{1,0:T(8,128)(2,1)S(1)}, u32[]{:S(2)}, u32[]{:S(2)}) collective-permute-start(bf16[64,1280]{1,0:T(8,128)(2,1)S(1)} %pad_maximum_fusion.7), channel_id=1, source_target_pairs={{0,8},{1,9},{2,10},{3,11},{4,12},{5,13},{6,14},{7,15},{8,0},{9,1},... | collective-permute-start | bytes 491528 | tf_op jit(solution)/shard_map/ppermute | solution.py:80
  74.1 15.2 %copy-start.10 = (bf16[32,1280]{1,0:T(8,128)(2,1)}, bf16[32,1280]{1,0:T(8,128)(2,1)S(1)}, u32[]{:S(2)}) copy-start(bf16[32,1280]{1,0:T(8,128)(2,1)S(1)} %collective-permute-done.4.refs_1_) | copy-start | bytes 245764
  74.1 7.9 %collective-permute-start.5 = (bf16[64,1280]{1,0:T(8,128)(2,1)S(1)}, bf16[64,1280]{1,0:T(8,128)(2,1)S(1)}, u32[]{:S(2)}, u32[]{:S(2)}) collective-permute-start(bf16[64,1280]{1,0:T(8,128)(2,1)S(1)} %pad_maximum_fusion.6), channel_id=1, source_target_pairs={{0,4},{1,5},{2,6},{3,7},{4,0},{5,1},{6,2},{7,3},{8,12},{9,13},{10,... | collective-permute-start | bytes 491528 | tf_op jit(solution)/shard_map/ppermute | solution.py:80
  78.6 10.8 %copy-start.5 = (bf16[64,1280]{1,0:T(8,128)(2,1)}, bf16[64,1280]{1,0:T(8,128)(2,1)S(1)}, u32[]{:S(2)}) copy-start(bf16[64,1280]{1,0:T(8,128)(2,1)S(1)} %collective-permute-done.9.refs_7_) | copy-start | bytes 491524
  78.6 8.2 %collective-permute-start.10 = (bf16[128,1280]{1,0:T(8,128)(2,1)S(1)}, bf16[128,1280]{1,0:T(8,128)(2,1)S(1)}, u32[]{:S(2)}, u32[]{:S(2)}) collective-permute-start(bf16[128,1280]{1,0:T(8,128)(2,1)S(1)} %pad_maximum_fusion.4), channel_id=1, source_target_pairs={{0,4},{1,5},{2,6},{3,7},{4,0},{5,1},{6,2},{7,3},{8,12},{9,13},{10,... | collective-permute-start | bytes 983048 | tf_op jit(solution)/shard_map/ppermute | solution.py:80
  82.1 7.1 %collective-permute-start.6 = (bf16[128,1280]{1,0:T(8,128)(2,1)S(1)}, bf16[128,1280]{1,0:T(8,128)(2,1)S(1)}, u32[]{:S(2)}, u32[]{:S(2)}) collective-permute-start(bf16[128,1280]{1,0:T(8,128)(2,1)S(1)} %pad_maximum_fusion.3), channel_id=1, source_target_pairs={{0,2},{1,3},{2,0},{3,1},{4,6},{5,7},{6,4},{7,5},{8,10},{9,11},{10,... | collective-permute-start | bytes 983048 | tf_op jit(solution)/shard_map/ppermute | solution.py:80
  83.7 6.5 %collective-permute-start.17 = (bf16[256,512]{1,0:T(8,128)(2,1)S(1)}, bf16[256,512]{1,0:T(8,128)(2,1)S(1)}, u32[]{:S(2)}, u32[]{:S(2)}) collective-permute-start(bf16[256,512]{1,0:T(8,128)(2,1)S(1)} %get-tuple-element.42), channel_id=1, source_target_pairs={{0,1},{1,0},{2,3},{3,2},{4,5},{5,4},{6,7},{7,6},{8,9},{9,8},{10,11... | collective-permute-start | bytes 786440 | tf_op jit(solution)/shard_map/ppermute | solution.py:80
  86.9 4.1 %collective-permute-start.11 = (bf16[256,1280]{1,0:T(8,128)(2,1)S(1)}, bf16[256,1280]{1,0:T(8,128)(2,1)}, u32[]{:S(2)}, u32[]{:S(2)}) collective-permute-start(bf16[256,1280]{1,0:T(8,128)(2,1)S(1)} %pad_maximum_fusion.1), channel_id=1, source_target_pairs={{0,1},{1,0},{2,3},{3,2},{4,5},{5,4},{6,7},{7,6},{8,9},{9,8},{10,11... | collective-permute-start | bytes 1966088 | tf_op jit(solution)/shard_map/ppermute | solution.py:80
  89.3 2.3 %collective-permute-start.7 = (bf16[256,1280]{1,0:T(8,128)(2,1)S(1)}, bf16[256,1280]{1,0:T(8,128)(2,1)}, u32[]{:S(2)}, u32[]{:S(2)}) collective-permute-start(bf16[256,1280]{1,0:T(8,128)(2,1)S(1)} %pad_maximum_fusion), channel_id=1, source_target_pairs={{0,1},{1,0},{2,3},{3,2},{4,5},{5,4},{6,7},{7,6},{8,9},{9,8},{10,11... | collective-permute-start | bytes 1966088 | tf_op jit(solution)/shard_map/ppermute | solution.py:80
  97.6 14.2 %collective-permute-start.12 = (bf16[16,2,16,512]{3,2,1,0:T(8,128)(2,1)}, bf16[16,2,16,512]{3,2,1,0:T(8,128)(2,1)S(1)}, u32[]{:S(2)}, u32[]{:S(2)}) collective-permute-start(bf16[16,2,16,512]{3,2,1,0:T(8,128)(2,1)} %bitcast.81), channel_id=1, source_target_pairs={{0,16},{16,0},{1,17},{17,1},{2,18},{18,2},{3,19},{19,3},{4,20},{20... | collective-permute-start | bytes 1572872 | tf_op jit(solution)/shard_map/ppermute | solution.py:62
  99.5 13.1 %copy-start.1 = (bf16[512,512]{1,0:T(8,128)(2,1)}, bf16[512,512]{1,0:T(8,128)(2,1)S(1)}, u32[]{:S(2)}) copy-start(bf16[512,512]{1,0:T(8,128)(2,1)S(1)} %select_add_fusion.refs_4_) | copy-start | bytes 1572868
  128.7 16.3 %all-to-all-start = ((bf16[16,16,512]{2,1,0:T(8,128)(2,1)}), bf16[16,16,512]{2,1,0:T(8,128)(2,1)S(1)}, u32[]{:S(2)}, u32[]{:S(2)}) async-start(bf16[16,16,512]{2,1,0:T(8,128)(2,1)} %get-tuple-element.20), calls=%async_computation | async-start | bytes 524288 | tf_op jit(solution)/shard_map/all_to_all | solution.py:521
  136.2 9.2 %collective-permute-start.20 = (bf16[128,512]{1,0:T(8,128)(2,1)S(1)}, bf16[128,512]{1,0:T(8,128)(2,1)S(1)}, u32[]{:S(2)}, u32[]{:S(2)}) collective-permute-start(bf16[128,512]{1,0:T(8,128)(2,1)S(1)} %slice.137), channel_id=1, source_target_pairs={{0,16},{16,0},{1,17},{17,1},{2,18},{18,2},{3,19},{19,3},{4,20},{20... | collective-permute-start | bytes 393224 | tf_op jit(solution)/shard_map/ppermute | solution.py:62
  (14 other events, 63.0 us)

commit v3 on v2

v3 whole, which is shorter than its diff:
```python
import math

import jax
import jax.numpy as jnp
from jax import lax
from jax.experimental import pallas as pl
from jax.experimental.pallas import tpu as pltpu
from jax.sharding import PartitionSpec as P


VHD = 80
HD = 128
EPS = 1e-06
THETA = 1000000.0
HIGHEST = lax.Precision.HIGHEST
BF16 = jnp.bfloat16
barrier = lax.optimization_barrier
F32 = jnp.float32


def layer_norm(values):
    average = jnp.mean(values, axis=-1, keepdims=True)
    centered = values - average
    variance = jnp.mean(centered * centered, axis=-1, keepdims=True)
    return centered * lax.rsqrt(variance + EPS)


def dot(a, b, **kw):
    return jnp.dot(a, b, preferred_element_type=F32, **kw)


def shift(x, k):
    size = lax.axis_size("dp")
    return lax.ppermute(x, "dp", [(i, (i + k) % size) for i in range(size)])


def gather_dp(x):
    return [x] + [shift(x, k) for k in range(1, lax.axis_size("dp"))]


def strides_of(size):
    return [1 << b for b in reversed(range(size.bit_length() - 1))]


def xor_gather(x, strides):
    size = lax.axis_size("ctx")
    pieces = [x]
    offsets = [[0]]
    for stride in strides:
        known = [o for piece in offsets for o in piece]
        joined = pieces[0] if len(pieces) == 1 else jnp.concatenate(pieces, axis=0)
        pieces.append(lax.ppermute(joined, "ctx", [(i, i ^ stride) for i in range(size)]))
        offsets.append([o ^ stride for o in known])
    return pieces, offsets


def gather_halves(x):
    size = lax.axis_size("ctx")
    own = lax.axis_index("ctx")
    if size & (size - 1) or size < 8:
        return [lax.all_gather(x, "ctx", axis=0, tiled=True)], jnp.arange(size, dtype=jnp.int32)
    strides = strides_of(size)
    middle = x.shape[1] // 2
    left, offsets = xor_gather(x[:, :middle], strides[:-1])
    right, others = xor_gather(x[:, middle:], strides[-2:-1] + strides[:-2])
    order = [o for piece in offsets for o in piece]
    rows = x.shape[0]
    found = {
        o: piece[j * rows : (j + 1) * rows]
        for piece, known in zip(right, others)
        for j, o in enumerate(known)
    }
    low = jnp.concatenate(
        [jnp.concatenate(left, axis=0), jnp.concatenate([found[o] for o in order], axis=0)], axis=1
    )
    high = lax.ppermute(low, "ctx", [(i, i ^ 1) for i in range(size)])
    order = order + [o ^ 1 for o in order]
    return [low, high], own ^ jnp.asarray(order, jnp.int32)


def find_image(own, tokens, grid_ref, start_ref, groups):
    zero = jnp.int32(0)
    first, cols, count, owner = zero, zero, zero, zero
    for o in range(groups):
        start = start_ref[0, o]
        here = (start >= own * tokens) & (start < (own + 1) * tokens)
        first = jnp.where(here, start, first)
        cols = jnp.where(here, grid_ref[0, o, 1], cols)
        count = jnp.where(here, grid_ref[0, o, 0] * grid_ref[0, o, 1], count)
        owner = jnp.where(here, o, owner)
    return first, cols, count, owner


SMEM = pl.BlockSpec(memory_space=pltpu.SMEM)
VMEM = pl.BlockSpec(memory_space=pltpu.VMEM)


def call(kernel, outs, ins, scalars=0, scratch=()):
    return pl.pallas_call(
        kernel,
        out_shape=outs,
        in_specs=[SMEM] * scalars + [VMEM] * (len(ins) - scalars),
        out_specs=[VMEM] * len(outs),
        scratch_shapes=list(scratch),
    )(*ins)


def project(parts, index, images, gain, weight):
    rows, _ = images[0].shape
    depth, columns = weight.shape
    third = columns // 3
    block = third // parts

    def kernel(index_ref, *refs):
        image_refs = refs[:parts]
        gain_ref, weight_ref, mine_ref, sent_ref = refs[parts:]
        own = index_ref[0]
        pieces = []
        for r in range(parts):
            normed = layer_norm(image_refs[r][...].astype(F32)) * gain_ref[...]
            piece = normed[:, :depth]
            for b in range(1, parts):
                piece = jnp.where(own == b, normed[:, b * depth : (b + 1) * depth], piece)
            pieces.append(piece.astype(BF16))
        product = dot(jnp.concatenate(pieces, axis=0), weight_ref[...])
        for b in range(parts):
            heads = jnp.concatenate(
                [product[:, j * third + b * block : j * third + (b + 1) * block] for j in range(3)],
                axis=1,
            )

            @pl.when(own == b)
            def _():
                mine_ref[...] = heads.reshape(parts, rows, 3 * block)

            for k in range(1, parts):

                @pl.when((own + k) % parts == b)
                def _():
                    for r in range(parts):
                        sent_ref[k - 1, (r + k) % parts] = heads[r * rows : (r + 1) * rows].astype(
                            BF16
                        )

    return call(
        kernel,
        (
            jax.ShapeDtypeStruct((parts, rows, 3 * block), F32),
            jax.ShapeDtypeStruct((parts - 1, parts, rows, 3 * block), BF16),
        ),
        (index, *images, gain, weight),
        scalars=1,
    )


def attend(parts, places, scalars, mine, received, images, out_weight):
    rows, width = images[0].shape
    capacity = rows // 4
    block = out_weight.shape[0]
    heads = block // VHD
    taken = places * capacity

    def kernel(scalar_ref, *refs):
        mine_ref = refs[0]
        received_refs = refs[1:parts]
        image_refs = refs[parts : 2 * parts]
        weight_ref, hidden_ref, sent_ref, scratch = refs[2 * parts :]
        own = scalar_ref[0]
        lane = lax.broadcasted_iota(jnp.int32, (rows, block), 1)
        key_slot = lax.broadcasted_iota(jnp.int32, (heads * rows, rows), 1) % capacity
        attended = []
        for r in range(parts):
            total = mine_ref[r]
            for ref in received_refs:
                total = total + ref[r].astype(F32)
            total = total.astype(BF16)
            queries = total[:, :block]
            keys = total[:, block : 2 * block]
            contents = total[:, 2 * block :]
            in_head = [(lane >= h * VHD) & (lane < (h + 1) * VHD) for h in range(heads)]
            stacked = jnp.concatenate(
                [jnp.where(inside, queries, jnp.zeros_like(queries)) for inside in in_head], axis=0
            )
            scores = lax.dot_general(
                stacked, keys, (((1,), (1,)), ((), ())), preferred_element_type=F32
            ) / math.sqrt(VHD)
            alive = (key_slot < scalar_ref[1 + r]).astype(F32)
            weights = jnp.exp(scores) * alive
            probability = (weights / jnp.sum(weights, axis=-1, keepdims=True)).astype(BF16)
            spread = dot(probability, contents)
            picked = jnp.where(in_head[0], spread[:rows], 0.0)
            for h in range(1, heads):
                picked = picked + jnp.where(in_head[h], spread[h * rows : (h + 1) * rows], 0.0)
            attended.append(picked.astype(BF16))
        product = dot(jnp.concatenate(attended, axis=0), weight_ref[...])
        scratch[...] = product.reshape(parts, rows, width)

        def start(index):
            return pl.multiple_of((index * 4 // parts) * capacity, capacity)

        for r in range(parts):
            at = pl.ds(start(own), taken)
            hidden_ref[r] = scratch[r, at, :] + image_refs[r][at, :].astype(F32)
            for k in range(1, parts):
                at = pl.ds(start((own + k) % parts), taken)
                sent_ref[k - 1, (r + k) % parts] = scratch[r, at, :].astype(BF16)

    return call(
        kernel,
        (
            jax.ShapeDtypeStruct((parts, taken, width), F32),
            jax.ShapeDtypeStruct((parts - 1, parts, taken, width), BF16),
        ),
        (scalars, mine, *received, *images, out_weight),
        scalars=1,
        scratch=[pltpu.VMEM((parts, rows, width), F32)],
    )


def features(parts, groups, owners, holders, own_parts, received, weighted, gain, key_rows):
    total = sum(p.shape[0] for p in own_parts)
    columns = own_parts[0].shape[1]
    rows = total // groups
    capacity = rows // parts
    key_width = key_rows.shape[1]
    chunks = len(own_parts)
    per_chunk = groups // chunks
    flat = [r for group in received for r in group]

    def kernel(owner_ref, holder_ref, *refs):
        part_refs = refs[:chunks]
        received_refs = refs[chunks : chunks + len(flat)]
        weighted_ref, gain_ref, key_ref, embed_ref, sums_ref, keys_ref = refs[chunks + len(flat) :]
        picked = []
        for i in range(groups):
            chunk, base = i // per_chunk, (i % per_chunk) * rows
            block = part_refs[chunk][base : base + rows, :]
            for k in range(1, parts):
                ref = received_refs[chunk * (parts - 1) + k - 1]
                block = block + jnp.concatenate(
                    [
                        ref[pl.ds(base + (r - k) % parts * capacity, capacity), :].astype(F32)
                        for r in range(parts)
                    ],
                    axis=0,
                )
            block = block.astype(BF16)
            picked.append((block[:capacity].astype(F32) * gain_ref[...]).astype(BF16))
            embed_ref[pl.ds(pl.multiple_of(owner_ref[i] * rows, rows), rows), :] = block
        values = embed_ref[...].astype(F32)
        ones = jnp.ones((8, columns), F32)
        contract = (((1,), (1,)), ((), ()))
        squares = lax.dot_general(
            ones, values * values, contract, precision=HIGHEST, preferred_element_type=F32
        )
        products = lax.dot_general(
            ones, values * weighted_ref[...], contract, precision=HIGHEST, preferred_element_type=F32
        )
        for i in range(groups):
            sums_ref[i, :, 0:total] = squares[0:1]
            sums_ref[i, :, total : 2 * total] = products[0:1]
        terms = dot(jnp.concatenate(picked, axis=0), key_ref[...]).astype(BF16)
        for i in range(groups):
            keys_ref[holder_ref[i]] = terms[i * capacity : (i + 1) * capacity]

    return call(
        kernel,
        (
            jax.ShapeDtypeStruct((total, columns), BF16),
            jax.ShapeDtypeStruct((groups, 1, 2 * total), F32),
            jax.ShapeDtypeStruct((groups, capacity, key_width), BF16),
        ),
        (owners, holders, *own_parts, *flat, weighted, gain, key_rows),
        scalars=2,
    )


def finish(groups, width, owners, sums, embedded, weighted, merged):
    total, columns = embedded.shape
    rows = total // groups
    chunks = len(merged)
    chunk = total // chunks
    height = merged[0].shape[1]
    bands = 5 if height % (5 * 128) == 0 else 1
    band = height // bands

    def kernel(owner_ref, sums_ref, embed_ref, weighted_ref, *refs):
        merged_refs = refs[:chunks]
        out_ref, scale_ref, grads, ordered = refs[chunks:]

        @pl.when(pl.program_id(0) == 0)
        def _():
            whole = jnp.sum(sums_ref[...], axis=0)
            scale = lax.rsqrt(whole[:, :total] / width + EPS)
            slope = scale**3 * whole[:, total:] / width
            line = lax.broadcasted_iota(jnp.int32, (8, total), 0)
            both = jnp.where(line == 0, scale, slope)
            scale_ref[...] = both
            columns_of = jnp.transpose(both)
            grads[...] = (
                columns_of[:, 0:1] * weighted_ref[...]
                - embed_ref[...].astype(F32) * columns_of[:, 1:2]
            ).astype(BF16)
            for i in range(groups):
                ordered[pl.ds(i * rows, rows), :] = grads[
                    pl.ds(pl.multiple_of(owner_ref[i] * rows, rows), rows), :
                ]

        result = None
        for j in range(chunks):
            term = lax.dot_general(
                merged_refs[j][...],
                ordered[j * chunk : (j + 1) * chunk, :],
                (((0,), (0,)), ((), ())),
                preferred_element_type=F32,
            )
            result = term if result is None else result + term
        out_ref[...] = result

    return pl.pallas_call(
        kernel,
        grid=(bands,),
        out_shape=(
            jax.ShapeDtypeStruct((height, columns), F32),
            jax.ShapeDtypeStruct((8, total), F32),
        ),
        in_specs=[
            SMEM,
            pl.BlockSpec(sums.shape, lambda g: (0, 0, 0)),
            pl.BlockSpec(embedded.shape, lambda g: (0, 0)),
            pl.BlockSpec(weighted.shape, lambda g: (0, 0)),
        ]
        + [pl.BlockSpec((chunk, band), lambda g: (0, g))] * chunks,
        out_specs=[
            pl.BlockSpec((band, columns), lambda g: (g, 0)),
            pl.BlockSpec((8, total), lambda g: (0, 0)),
        ],
        scratch_shapes=[pltpu.VMEM((total, columns), BF16), pltpu.VMEM((total, columns), BF16)],
        compiler_params=pltpu.CompilerParams(dimension_semantics=("arbitrary",)),
        name="finish",
    )(owners, sums, embedded, weighted, *merged)


def merge(parts, places, counts, hidden, received):
    taken, width = hidden.shape[1:]
    capacity = taken // places

    def kernel(count_ref, *refs):
        hidden_ref, received_refs, out_ref = refs[0], refs[1:-1], refs[-1]
        slot = lax.broadcasted_iota(jnp.int32, (capacity, width), 0)
        for r in range(parts):
            total = hidden_ref[r]
            for ref in received_refs:
                total = total + ref[r].astype(F32)
            normed = layer_norm(total).astype(BF16)
            for p in range(places):
                kept = normed[p * capacity : (p + 1) * capacity]
                kept = jnp.where(slot < count_ref[r], kept, jnp.zeros_like(kept))
                out_ref[r * capacity : (r + 1) * capacity, p * width : (p + 1) * width] = kept

    return call(
        kernel,
        (jax.ShapeDtypeStruct((parts * capacity, places * width), BF16),),
        (counts, hidden, *received),
        scalars=1,
    )[0]


def angle_table(tokens, groups, capacity, index, grid, start):
    half = HD // 2
    first_cut = HD // 8
    second_cut = first_cut + 3 * HD // 16
    inverse = THETA ** (-(2.0 * (jnp.arange(HD, dtype=jnp.int32) % half).astype(F32)) / HD)

    def kernel(index_ref, grid_ref, start_ref, inverse_ref, out_ref):
        own = index_ref[1]
        first, cols, count, _ = find_image(own, tokens, grid_ref, start_ref, groups)
        line = lax.broadcasted_iota(jnp.int32, (tokens, HD), 0) + own * tokens
        frequency = lax.broadcasted_iota(jnp.int32, (tokens, HD), 1) % half
        inner = line - first
        row = jnp.zeros_like(inner)
        for j in range(1, capacity):
            row = row + (inner >= j * cols).astype(jnp.int32)
        offset = jnp.where(frequency < second_cut, row, inner - row * cols)
        offset = jnp.where(frequency < first_cut, 0, offset)
        inside = (inner >= 0) & (inner < count)
        chosen = jnp.where(inside, first + offset, line)
        out_ref[...] = chosen.astype(F32) * inverse_ref[...]

    return call(
        kernel,
        (jax.ShapeDtypeStruct((tokens, HD), F32),),
        (index, grid, start, inverse.reshape(1, -1)),
        scalars=3,
    )[0]


def place_rows(tokens, own, first, count, shape, axis):
    token = lax.broadcasted_iota(jnp.int32, shape, axis)
    slot = lax.broadcasted_iota(jnp.int32, shape, 1 - axis)
    return ((token + own * tokens - first == slot) & (slot < count)).astype(F32)


def turn(values, cosine, sines):
    heads = []
    for h in range(values.shape[1] // HD):
        head = values[:, h * HD : (h + 1) * HD]
        heads.append(head * cosine + pltpu.roll(head, HD // 2, 1) * sines)
    return jnp.concatenate(heads, axis=1)


def image_grads(tokens, groups, capacity, index, grid, start, cotangent, cosine, sines):
    width = cotangent.shape[1]

    def kernel(index_ref, grid_ref, start_ref, cotangent_ref, cosine_ref, sine_ref, out_ref):
        own = index_ref[1]
        first, _, count, _ = find_image(own, tokens, grid_ref, start_ref, groups)
        lane = lax.broadcasted_iota(jnp.int32, (tokens, HD), 1)
        signed = jnp.where(lane < HD // 2, sine_ref[...], -sine_ref[...])
        grad = turn(cotangent_ref[...].astype(F32), cosine_ref[...], signed)
        chosen = place_rows(tokens, own, first, count, (capacity, tokens), 1)
        out_ref[...] = dot(chosen, grad, precision=HIGHEST).astype(BF16)

    return call(
        kernel,
        (jax.ShapeDtypeStruct((capacity, width), BF16),),
        (index, grid, start, cotangent, cosine, sines),
        scalars=3,
    )[0]


def keys_out(parts, groups, index, grid, start, text_keys, returned, arrived, scales, cosine, sines):
    tokens, width = returned[0][0].shape[0] * len(returned), text_keys[0].shape[1]
    capacity = arrived.shape[1]
    total = scales.shape[1]
    chunks = len(text_keys)
    chunk = tokens // chunks
    flat = [r for group in returned for r in group]

    def kernel(index_ref, grid_ref, start_ref, *refs):
        text_refs = refs[:chunks]
        returned_refs = refs[chunks : chunks + len(flat)]
        arrived_ref, scale_ref, cosine_ref, sine_ref, out_ref = refs[chunks + len(flat) :]
        own = index_ref[1]
        first, _, count, owner = find_image(own, tokens, grid_ref, start_ref, groups)
        shape = (capacity, total)
        lane = lax.broadcasted_iota(jnp.int32, shape, 1)
        slot = lax.broadcasted_iota(jnp.int32, shape, 0)
        wanted = lane == owner * (parts * capacity) + slot
        scale = jnp.sum(jnp.where(wanted, scale_ref[0:1, :], 0.0), axis=-1, keepdims=True)
        image = jnp.sum(arrived_ref[...].astype(F32), axis=0) * scale
        chosen = place_rows(tokens, own, first, count, (tokens, capacity), 0)
        placed = dot(chosen, image, precision=HIGHEST)
        token = lax.broadcasted_iota(jnp.int32, (tokens, width), 0) + own * tokens
        inside = (token >= first) & (token < first + count)
        lane = lax.broadcasted_iota(jnp.int32, (tokens, HD), 1)
        signed = jnp.where(lane < HD // 2, -sine_ref[...], sine_ref[...])
        rows = []
        for j in range(chunks):
            part = text_refs[j][0:chunk, :]
            for k in range(parts - 1):
                part = part + returned_refs[j * (parts - 1) + k][...].astype(F32)
            rows.append(part)
        keys = jnp.where(inside, placed, jnp.concatenate(rows, axis=0))
        out_ref[...] = turn(keys, cosine_ref[...], signed).astype(BF16)

    return call(
        kernel,
        (jax.ShapeDtypeStruct((tokens, width), BF16),),
        (index, grid, start, *text_keys, *flat, arrived, scales, cosine, sines),
        scalars=3,
    )[0]


def text_norm(parts, chunks, index, text, gain):
    tokens, width = text.shape
    step = 32 if tokens // chunks % 32 == 0 else tokens // chunks
    block = width // parts
    steps = tokens // chunks // step

    def kernel(index_ref, text_ref, gain_ref, *refs):
        out_refs, scratch = refs[:-1], refs[-1]
        values = text_ref[...].astype(F32)
        scale = lax.rsqrt(jnp.mean(values * values, axis=-1, keepdims=True) + EPS)
        scratch[...] = (values * scale * gain_ref[...]).astype(BF16)
        for j in range(chunks):

            @pl.when(pl.program_id(0) // steps == j)
            def _():
                for k in range(parts):
                    start = pl.multiple_of((index_ref[0] + k) % parts * block, block)
                    out_refs[j * parts + k][...] = scratch[:, pl.ds(start, block)]

    def place(j):
        return lambda g: (jnp.clip(g - j * steps, 0, steps - 1), 0)

    flat = pl.pallas_call(
        kernel,
        grid=(tokens // step,),
        out_shape=[jax.ShapeDtypeStruct((tokens // chunks, block), BF16)] * (chunks * parts),
        in_specs=[
            SMEM,
            pl.BlockSpec((step, width), lambda g: (g, 0)),
            pl.BlockSpec((1, width), lambda g: (0, 0)),
        ],
        out_specs=[
            pl.BlockSpec((step, block), place(j)) for j in range(chunks) for _ in range(parts)
        ],
        scratch_shapes=[pltpu.VMEM((step, width), BF16)],
        name="text_norm",
    )(index, text, gain)
    return [flat[j * parts : (j + 1) * parts] for j in range(chunks)]


def on_device(
    patches,
    vit_norm_gain,
    vit_qkv,
    vit_out,
    merger,
    text_embed,
    lang_norm_gain,
    key_weight,
    key_cotangent,
    image_grid,
    image_start,
):
    parts = lax.axis_size("dp")
    groups = lax.axis_size("ctx")
    own_part = lax.axis_index("dp")
    own = lax.axis_index("ctx")
    tokens, width = text_embed.shape[1:]
    vit_width = patches.shape[2]
    capacity = patches.shape[1] // 4
    key_width = key_weight.shape[1]
    feature_cols = merger.shape[1]
    gain_line = lang_norm_gain.reshape(1, -1)
    index = jnp.stack([own_part, own]).astype(jnp.int32)
    others = range(1, parts)

    row = jnp.arange(4 * capacity, dtype=jnp.int32)
    source_row = (row % capacity) * 4 + row // capacity
    order_rows = (source_row[:, None] == row[None, :]).astype(BF16)
    images = gather_dp(dot(order_rows, patches[0]).astype(BF16))

    info = jnp.concatenate([image_grid[0].T, image_start], axis=0)
    infos = jnp.stack(gather_dp(info))
    counts = infos[:, 0] * infos[:, 1]
    target_range = infos[:, 2] // tokens
    group_index = jnp.arange(groups, dtype=jnp.int32)
    own_counts = jnp.sum(jnp.where(group_index[None] == own, counts, 0), axis=1)

    chunks = 2
    text_blocks = text_norm(parts, chunks, index, text_embed[0], gain_line)

    mine, sent = project(parts, index, images, vit_norm_gain.reshape(1, -1), vit_qkv)

    sent, grid, start = barrier((sent, image_grid, image_start))
    received = [shift(sent[k - 1], k) for k in others]
    angles = angle_table(tokens, groups, capacity, index, grid, start)
    cosine, sines = jnp.cos(angles), jnp.sin(angles)
    grads = image_grads(
        tokens, groups, capacity, index, grid, start, key_cotangent[0], cosine, sines
    )
    grads = jnp.concatenate(gather_dp(grads), axis=0)

    places = max(1, 4 // parts)
    pieces = max(1, parts // 4)
    piece_width = vit_width // pieces
    scalars = jnp.concatenate([index[:1], own_counts])
    hidden_rows, sent = attend(parts, places, scalars, mine, received, images, vit_out)
    sent, grads = barrier((sent, grads))
    received = [shift(sent[k - 1], k) for k in others]
    grads = lax.all_to_all(
        jnp.broadcast_to(grads[None], (groups,) + grads.shape), "ctx", 0, 0, tiled=True
    )
    received, text_blocks, key_source = barrier((received, text_blocks, key_weight))
    merged = merge(parts, places, own_counts, hidden_rows, received)
    if pieces > 1:
        merged = lax.dynamic_slice_in_dim(merged, (own_part % pieces) * piece_width, piece_width, 1)
    merged_all, owners = gather_halves(merged)

    part_features = width // parts
    own_start = own * feature_cols
    holder_part = own_start // part_features
    candidate = lax.dynamic_slice_in_dim(key_source, own_start % part_features, feature_cols, 0)
    key_rows = jnp.where(own_part == holder_part, candidate, jnp.zeros_like(candidate))
    held_by = [g * feature_cols // part_features for g in range(groups)]
    for k in others:
        pairs = [
            (held_by[g] * groups + g, (held_by[g] + k) % parts * groups + g) for g in range(groups)
        ]
        key_rows = key_rows + lax.ppermute(candidate, ("dp", "ctx"), pairs)
    own_gain = lax.dynamic_slice_in_dim(lang_norm_gain, own_start, feature_cols, 0).reshape(1, -1)

    def text_terms(blocks):
        rows = [blocks[0]] + [shift(blocks[k], k) for k in others]
        return dot(jnp.concatenate(rows, axis=0), key_weight)

    def text_return(terms):
        size = terms.shape[0] // parts
        return [shift(terms[k * size : (k + 1) * size].astype(BF16), -k) for k in others]

    early_terms = text_terms(text_blocks[0])

    grads = grads.reshape(groups, parts, capacity, key_width)
    routing = (target_range[:, :, None] == group_index[None, None, :]).astype(BF16)
    grads = jnp.einsum("roh,hrkw->orkw", routing, grads, preferred_element_type=F32).astype(BF16)
    weighted = (
        lax.dot_general(
            grads.reshape(-1, key_width),
            key_rows,
            (((1,), (1,)), ((), ())),
            preferred_element_type=F32,
        )
        * own_gain
    )

    embed_parts = [dot(rows, merger) for rows in merged_all]
    received = [[shift(part.astype(BF16), k) for k in others] for part in embed_parts]
    block_owner = (owners[:, None] == group_index[None, :]).astype(jnp.int32)
    block_range = jnp.sum(block_owner * target_range[0][None, :], axis=-1)
    received, late_blocks, early_terms = barrier((received, text_blocks[1], early_terms))
    embedded, sums, outgoing = features(
        parts, groups, owners, block_range, embed_parts, received, weighted, own_gain, key_rows
    )
    sums = lax.all_to_all(sums, "ctx", 0, 0, tiled=True)
    late_terms = text_terms(late_blocks)
    returned = [text_return(early_terms), text_return(late_terms)]
    sums, outgoing = barrier((sums, outgoing))
    arrived = lax.all_to_all(outgoing, "ctx", 0, 0, tiled=True)
    merger_grad, scales = finish(groups, float(width), owners, sums, embedded, weighted, merged_all)
    rotated = keys_out(
        parts,
        groups,
        index,
        image_grid,
        image_start,
        [early_terms, late_terms],
        returned,
        arrived,
        scales,
        cosine,
        sines,
    )
    return (rotated[None], merger_grad)


def solution(mesh):
    return jax.shard_map(
        on_device,
        mesh=mesh,
        in_specs=(
            P("dp", "ctx", None),
            P(),
            P("dp", None),
            P("dp", None),
            P("dp", "ctx"),
            P("dp", "ctx", None),
            P(),
            P("dp", None),
            P("dp", "ctx", None),
            P("dp", None, None),
            P("dp", None),
        ),
        out_specs=(P("dp", "ctx", None), P("dp", "ctx")),
        check_vma=False,
    )
```

time: 148 us -> 154 us (1.041)
  other arithmetic: 15.4 us -> 5.68 us
  starting transfers between devices: 32.5 us -> 39.1 us
  matrix products: 7.11 us -> 13 us
  between operations: 3.79 us -> 0.99 us
  local copies, waits for them, and re-layouts: 10.1 us -> 12.7 us
  Pallas kernels: 29.7 us -> 31.8 us
    ppermute x8 -> x11, waiting for transfers between devices: 21.6 us -> 28 us  [shift(): return lax.ppermute(x, 'dp', [(i, (i + k) % size) for i in range(size)])]
    dot_general x4 -> x5, matrix products: 5.21 us -> 11.2 us  [dot(): return jnp.dot(a, b, preferred_element_type=F32, **kw)]
    all_to_all x0 -> x1, starting transfers between devices: none -> 5.88 us  [on_device(): lax.all_to_all(jnp.broadcast_to(grads[None], (groups,) + grads.shape), 'c...]
    ppermute x12 -> x6, waiting for transfers between devices: 15.2 us -> 9.55 us  [xor_gather(): lax.ppermute(joined, 'ctx', [(i, i ^ stride) for i in range(size)])]
    ppermute x8 -> x11, starting transfers between devices: 8.31 us -> 13.8 us  [shift(): return lax.ppermute(x, 'dp', [(i, (i + k) % size) for i in range(size)])]
    reduce_sum x5 -> x0, other arithmetic: 3.69 us -> none  [the longest x1 1.3 us: on_device(): own_cols = jnp.sum(jnp.where(own_range, grid_cols[0], 0))]
    ppermute x12 -> x6, starting transfers between devices: 16.7 us -> 13.1 us  [xor_gather(): lax.ppermute(joined, 'ctx', [(i, i ^ stride) for i in range(size)])]
    select_n x5 -> x1, other arithmetic: 3.59 us -> 0.01 us  [on_device(): target_range = infos[:, 2] // tokens]
  transfers between devices with their start and end apart: 22 -> 21, of which waited for: 10 -> 9; matrix products, arithmetic and copies ran while one was open for 20% -> 16% of each run, Pallas kernels for 20% -> 13%
where the time goes in v3:
time: 154 us; the launch traced here: 153 us
  starting transfers between devices  39.1 us (25%)
  waiting for transfers between devices  37.5 us (24%)
  Pallas kernels  31.8 us (21%)
  matrix products  13 us (8%)
  local copies, waits for them, and re-layouts  12.7 us (8%)
  blocking collectives  11.8 us (8%)
  other arithmetic  5.68 us (4%)
    ppermute x11, waiting for transfers between devices, shift(): return lax.ppermute(x, 'dp', [(i, (i + k) % size) for i in range(size)])  28 us
    pallas_call x7, Pallas kernels, call(): pl.pallas_call(kernel, out_shape=outs, in_specs=[SMEM] * scalars + [VMEM]...  19.8 us
    ppermute x11, starting transfers between devices, shift(): return lax.ppermute(x, 'dp', [(i, (i + k) % size) for i in range(size)])  13.8 us
    ppermute x6, starting transfers between devices, xor_gather(): lax.ppermute(joined, 'ctx', [(i, i ^ stride) for i in range(size)])  13.1 us
    all_to_all x1, blocking collectives, on_device(): sums = lax.all_to_all(sums, 'ctx', 0, 0, tiled=True)  11.8 us
    dot_general x5, matrix products, dot(): return jnp.dot(a, b, preferred_element_type=F32, **kw)  11.2 us
    ppermute x6, waiting for transfers between devices, xor_gather(): lax.ppermute(joined, 'ctx', [(i, i ^ stride) for i in range(size)])  9.55 us
    pallas_call x1, Pallas kernels, finish(): pl.pallas_call(kernel, grid=(bands,), out_shape=(jax.ShapeDtypeStruct((he...  7.35 us
  transfers between devices with their start and end apart: 21, of which 9 were waited for; matrix products, arithmetic and copies ran while one was open for 16% of the time, Pallas kernels for 13%

profile of v3, /device:TPU:0, one launch (start us, length us, event | category | flops | bytes accessed | tf_op | source)
XLA Modules:
  0.0 152.7 jit_solution(8030593531355420583)
XLA Ops:
  1.5 3.0 %collective-permute-start = (s32[3,16]{1,0:T(4,128)S(1)}, s32[3,16]{1,0:T(4,128)S(1)}, u32[]{:S(2)}, u32[]{:S(2)}) collective-permute-start(s32[3,16]{1,0:T(4,128)S(1)} %get-tuple-element.72), channel_id=1, source_target_pairs={{0,16},{16,0},{1,17},{17,1},{2,18},{18,2},{3,19},{19,3},{4,20},{20... | collective-permute-start | bytes 584 | tf_op jit(solution)/shard_map/ppermute | solution.py:34
  8.3 3.1 %collective-permute-done.1.refs_1_.refs_3_ = bf16[64,1280]{1,0:T(8,128)(2,1)S(1)} collective-permute-done((bf16[64,1280]{1,0:T(8,128)(2,1)S(1)}, bf16[64,1280]{1,0:T(8,128)(2,1)S(1)}, u32[]{:S(2)}, u32[]{:S(2)}) %collective-permute-start.1) | collective-permute-done | bytes 163872 | tf_op jit(solution)/shard_map/ppermute | solution.py:34
  12.0 3.8 %shard_map.131 = (f32[2,64,960]{2,1,0:T(8,128)}, bf16[1,2,64,960]{3,2,1,0:T(8,128)(2,1)}) custom-call(s32[2]{0:T(128)} %pad_add_fusion.2.index_ref, bf16[64,1280]{1,0:T(8,128)(2,1)} %copy-done.2, bf16[64,1280]{1,0:T(8,128)(2,1)} %copy-done.4, f32[1,1280]{1,0:T(1,128)} %reshape.116.refs_2_, bf16[640,1920]{1,0:T(8,128)(2,1)} %refs_3_.1), custom_call_target="tpu_custom_call" | custom-call | tf_op jit(solution)/shard_map/pallas_call | solution.py:99
  18.4 1.7 %fusion.25 = (f32[128,128]{1,0:T(8,128)}, f32[128,128]{1,0:T(8,128)}) fusion(f32[128,128]{1,0:T(8,128)} %shard_map.133), kind=kLoop, calls=%fused_computation.68 | loop fusion | bytes 196608 | tf_op jit(solution)/shard_map/sin | solution.py:561
  20.2 1.9 %shard_map.134 = bf16[16,512]{1,0:T(8,128)(2,1)} custom-call(s32[2]{0:T(128)} %pad_add_fusion.2.index_ref, s32[1,16,2]{2,1,0:T(8,128)} %copy.27.grid_ref, s32[1,16]{1,0:T(1,128)} %start_ref.3, bf16[128,512]{1,0:T(8,128)(2,1)} %bitcast.43, f32[128,128]{1,0:T(8,128)} %get-tuple-element.68.cosine_ref.refs_6_, f32[128,128]{1,0:T(8,128)} %get-tuple-element.67.sine_ref.refs_7_), custom_call_target="tpu_custom_call" | custom-call | tf_op jit(solution)/shard_map/pallas_call | solution.py:99
  22.1 1.7 %collective-permute-start.3 = (bf16[16,512]{1,0:T(8,128)(2,1)}, bf16[16,512]{1,0:T(8,128)(2,1)S(1)}, u32[]{:S(2)}, u32[]{:S(2)}) collective-permute-start(bf16[16,512]{1,0:T(8,128)(2,1)} %shard_map.134), channel_id=1, source_target_pairs={{0,16},{16,0},{1,17},{17,1},{2,18},{18,2},{3,19},{19,3},{4,20},{20... | collective-permute-start | bytes 49160 | tf_op jit(solution)/shard_map/ppermute | solution.py:34
  27.5 3.5 %shard_map.132 = (f32[2,32,1280]{2,1,0:T(8,128)}, bf16[1,2,32,1280]{3,2,1,0:T(8,128)(2,1)}) custom-call(s32[3]{0:T(128)} %pad_add_fusion.3.scalar_ref, f32[2,64,960]{2,1,0:T(8,128)} %get-tuple-element.33.refs_0_, bf16[2,64,960]{2,1,0:T(8,128)(2,1)} %copy-done.8, bf16[64,1280]{1,0:T(8,128)(2,1)} %copy-done.2, bf16[64,1280]{1,0:T(8,128)(2,1)} %copy-done.4, ...), custom_call_target="tpu_custom_call" | custom-call | tf_op jit(solution)/shard_map/pallas_call | solution.py:99
  31.0 1.7 %collective-permute-start.4 = (bf16[2,32,1280]{2,1,0:T(8,128)(2,1)}, bf16[2,32,1280]{2,1,0:T(8,128)(2,1)S(1)}, u32[]{:S(2)}, u32[]{:S(2)}) collective-permute-start(bf16[2,32,1280]{2,1,0:T(8,128)(2,1)} %bitcast.52), channel_id=1, source_target_pairs={{0,16},{16,0},{1,17},{17,1},{2,18},{18,2},{3,19},{19,3},{4,20},{20... | collective-permute-start | bytes 491528 | tf_op jit(solution)/shard_map/ppermute | solution.py:34
  32.7 4.6 %text_norm.1 = (bf16[64,4096]{1,0:T(8,128)(2,1)}, bf16[64,4096]{1,0:T(8,128)(2,1)}, bf16[64,4096]{1,0:T(8,128)(2,1)}, bf16[64,4096]{1,0:T(8,128)(2,1)}) custom-call(s32[2]{0:T(128)} %pad_add_fusion.2.index_ref, bf16[128,8192]{1,0:T(8,128)(2,1)} %bitcast.41, f32[1,8192]{1,0:T(1,128)} %bitcast.45), custom_call_target="tpu_custom_call" | custom-call | tf_op jit(solution)/shard_map/text_norm/pallas_call | solution.py:497
  38.0 1.9 %shard_map.135 = bf16[32,2560]{1,0:T(8,128)(2,1)} custom-call(s32[2]{0:T(128)} %copy-done.15, f32[2,32,1280]{2,1,0:T(8,128)} %get-tuple-element.36.refs_0_, bf16[2,32,1280]{2,1,0:T(8,128)(2,1)} %copy-done.9), custom_call_target="tpu_custom_call" | custom-call | tf_op jit(solution)/shard_map/pallas_call | solution.py:99
  40.9 2.7 %collective-permute-start.5 = (bf16[32,1280]{1,0:T(8,128)(2,1)S(1)}, bf16[32,1280]{1,0:T(8,128)(2,1)S(1)}, u32[]{:S(2)}, u32[]{:S(2)}) collective-permute-start(bf16[32,1280]{1,0:T(8,128)(2,1)S(1)} %get-tuple-element.64), channel_id=1, source_target_pairs={{0,8},{1,9},{2,10},{3,11},{4,12},{5,13},{6,14},{7,15},{8,0},{9,1},... | collective-permute-start | bytes 245768 | tf_op jit(solution)/shard_map/ppermute | solution.py:52
  46.4 1.7 %collective-permute-start.6 = (bf16[64,1280]{1,0:T(8,128)(2,1)S(1)}, bf16[64,1280]{1,0:T(8,128)(2,1)S(1)}, u32[]{:S(2)}, u32[]{:S(2)}) collective-permute-start(bf16[64,1280]{1,0:T(8,128)(2,1)S(1)} %pad_maximum_fusion.3), channel_id=1, source_target_pairs={{0,4},{1,5},{2,6},{3,7},{4,0},{5,1},{6,2},{7,3},{8,12},{9,13},{10,... | collective-permute-start | bytes 491528 | tf_op jit(solution)/shard_map/ppermute | solution.py:52
  48.1 3.7 %collective-permute-start.9 = (bf16[64,1280]{1,0:T(8,128)(2,1)S(1)}, bf16[64,1280]{1,0:T(8,128)(2,1)S(1)}, u32[]{:S(2)}, u32[]{:S(2)}) collective-permute-start(bf16[64,1280]{1,0:T(8,128)(2,1)S(1)} %pad_maximum_fusion.4), channel_id=1, source_target_pairs={{0,8},{1,9},{2,10},{3,11},{4,12},{5,13},{6,14},{7,15},{8,0},{9,1},... | collective-permute-start | bytes 491528 | tf_op jit(solution)/shard_map/ppermute | solution.py:52
  53.7 2.8 %collective-permute-done.9 = bf16[64,1280]{1,0:T(8,128)(2,1)S(1)} collective-permute-done((bf16[64,1280]{1,0:T(8,128)(2,1)S(1)}, bf16[64,1280]{1,0:T(8,128)(2,1)S(1)}, u32[]{:S(2)}, u32[]{:S(2)}) %collective-permute-start.9) | collective-permute-done | bytes 163872 | tf_op jit(solution)/shard_map/ppermute | solution.py:52
  56.4 1.9 %collective-permute-start.10 = (bf16[128,1280]{1,0:T(8,128)(2,1)S(1)}, bf16[128,1280]{1,0:T(8,128)(2,1)S(1)}, u32[]{:S(2)}, u32[]{:S(2)}) collective-permute-start(bf16[128,1280]{1,0:T(8,128)(2,1)S(1)} %pad_maximum_fusion.2), channel_id=1, source_target_pairs={{0,4},{1,5},{2,6},{3,7},{4,0},{5,1},{6,2},{7,3},{8,12},{9,13},{10,... | collective-permute-start | bytes 983048 | tf_op jit(solution)/shard_map/ppermute | solution.py:52
  58.3 5.2 %collective-permute-done.10 = bf16[128,1280]{1,0:T(8,128)(2,1)S(1)} collective-permute-done((bf16[128,1280]{1,0:T(8,128)(2,1)S(1)}, bf16[128,1280]{1,0:T(8,128)(2,1)S(1)}, u32[]{:S(2)}, u32[]{:S(2)}) %collective-permute-start.10) | collective-permute-done | bytes 327712 | tf_op jit(solution)/shard_map/ppermute | solution.py:52
  67.3 5.9 %all-to-all-start = ((bf16[16,32,512]{2,1,0:T(8,128)(2,1)}), bf16[16,32,512]{2,1,0:T(8,128)(2,1)}, u32[]{:S(2)}, u32[]{:S(2)}) async-start(bf16[16,32,512]{2,1,0:T(8,128)(2,1)} %broadcast_in_dim.20), calls=%async_computation | async-start | bytes 1048576 | tf_op jit(solution)/shard_map/all_to_all | solution.py:574
  74.3 2.8 %collective-permute-start.18 = (bf16[512,512]{1,0:T(8,128)(2,1)S(1)}, bf16[512,512]{1,0:T(8,128)(2,1)S(1)}, u32[]{:S(2)}, u32[]{:S(2)}) collective-permute-start(bf16[512,512]{1,0:T(8,128)(2,1)S(1)} %constant_dynamic-slice_fusion), channel_id=1, source_target_pairs={{0,16},{1,17},{2,18},{3,19},{4,20},{5,21},{6,22},{7,23},{24,8},{25... | collective-permute-start | bytes 1572872 | tf_op jit(solution)/shard_map/ppermute | solution.py:593
  77.2 3.0 %fusion.26 = (bf16[256,512]{1,0:T(8,128)(2,1)}, f32[256,512]{1,0:T(8,128)}) fusion(bf16[256,2560]{1,0:T(8,128)(2,1)} %pad_maximum_fusion.refs_0_, bf16[2560,512]{1,0:T(8,128)(2,1)S(1)} %copy-done), kind=kOutput, calls=%fused_computation.69 | convolution fusion | flops 671219712 | bytes 4718592 | tf_op jit(solution)/shard_map/dot_general | solution.py:29
  80.3 2.1 %collective-permute-start.11 = (bf16[256,512]{1,0:T(8,128)(2,1)}, bf16[256,512]{1,0:T(8,128)(2,1)}, u32[]{:S(2)}, u32[]{:S(2)}) collective-permute-start(bf16[256,512]{1,0:T(8,128)(2,1)} %get-tuple-element.73), channel_id=1, source_target_pairs={{0,16},{16,0},{1,17},{17,1},{2,18},{18,2},{3,19},{19,3},{4,20},{20... | collective-permute-start | bytes 786440 | tf_op jit(solution)/shard_map/ppermute | solution.py:34
  82.3 3.1 %fusion.27 = (bf16[256,512]{1,0:T(8,128)(2,1)}, f32[256,512]{1,0:T(8,128)}) fusion(bf16[256,2560]{1,0:T(8,128)(2,1)} %collective-permute-done.12.refs_1_, bf16[2560,512]{1,0:T(8,128)(2,1)S(1)} %copy-done), kind=kOutput, calls=%fused_computation.70 | convolution fusion | flops 671219712 | bytes 4718592 | tf_op jit(solution)/shard_map/dot_general | solution.py:29
  85.6 15.2 %collective-permute-done.14 = bf16[64,4096]{1,0:T(8,128)(2,1)S(1)} collective-permute-done((bf16[64,4096]{1,0:T(8,128)(2,1)}, bf16[64,4096]{1,0:T(8,128)(2,1)S(1)}, u32[]{:S(2)}, u32[]{:S(2)}) %collective-permute-start.14) | collective-permute-done | bytes 524320 | tf_op jit(solution)/shard_map/ppermute | solution.py:34
  103.2 3.1 %collective-permute-done.11.refs_2_ = bf16[256,512]{1,0:T(8,128)(2,1)} collective-permute-done((bf16[256,512]{1,0:T(8,128)(2,1)}, bf16[256,512]{1,0:T(8,128)(2,1)}, u32[]{:S(2)}, u32[]{:S(2)}) %collective-permute-start.11) | collective-permute-done | bytes 262176 | tf_op jit(solution)/shard_map/ppermute | solution.py:34
  106.3 5.0 %collective-permute-done.13.refs_3_ = bf16[256,512]{1,0:T(8,128)(2,1)} collective-permute-done((bf16[256,512]{1,0:T(8,128)(2,1)}, bf16[256,512]{1,0:T(8,128)(2,1)}, u32[]{:S(2)}, u32[]{:S(2)}) %collective-permute-start.13) | collective-permute-done | bytes 262176 | tf_op jit(solution)/shard_map/ppermute | solution.py:34
  111.4 2.5 %collective-permute-start.15 = (bf16[64,4096]{1,0:T(8,128)(2,1)}, bf16[64,4096]{1,0:T(8,128)(2,1)}, u32[]{:S(2)}, u32[]{:S(2)}) collective-permute-start(bf16[64,4096]{1,0:T(8,128)(2,1)} %get-tuple-element.52), channel_id=1, source_target_pairs={{0,16},{16,0},{1,17},{17,1},{2,18},{18,2},{3,19},{19,3},{4,20},{20... | collective-permute-start | bytes 1572872 | tf_op jit(solution)/shard_map/ppermute | solution.py:34
  116.0 4.6 %shard_map.136 = (bf16[512,512]{1,0:T(8,128)(2,1)}, f32[16,1,1024]{2,1,0:T(1,128)}, bf16[16,16,512]{2,1,0:T(8,128)(2,1)}) custom-call(s32[16]{0:T(128)} %copy-done.14, s32[16]{0:T(128)} %select_reduce_fusion.holder_ref, f32[256,512]{1,0:T(8,128)} %get-tuple-element.74.refs_0_, f32[256,512]{1,0:T(8,128)} %get-tuple-element.76.refs_1_, ...), custom_call_target="tpu_custom_call" | custom-call | tf_op jit(solution)/shard_map/pallas_call | solution.py:99
  120.6 11.8 %all_to_all.15.sums_ref = f32[16,1,1024]{2,1,0:T(1,128)} all-to-all(f32[16,1,1024]{2,1,0:T(1,128)} %get-tuple-element.57), channel_id=1, replica_groups=mesh['dp'=2,'ctx'=16] {'ctx'}, dimensions={0} | all-to-all | bytes 131072 | tf_op jit(solution)/shard_map/all_to_all | solution.py:627
  132.4 3.5 %all-to-all-start.2 = ((bf16[16,16,512]{2,1,0:T(8,128)(2,1)}), bf16[16,16,512]{2,1,0:T(8,128)(2,1)S(1)}, u32[]{:S(2)}, u32[]{:S(2)}) async-start(bf16[16,16,512]{2,1,0:T(8,128)(2,1)} %get-tuple-element.59), calls=%async_computation.2 | async-start | bytes 524288 | tf_op jit(solution)/shard_map/all_to_all | solution.py:631
  136.0 2.1 %collective-permute-start.16 = (bf16[64,512]{1,0:T(8,128)(2,1)S(1)}, bf16[64,512]{1,0:T(8,128)(2,1)S(1)}, u32[]{:S(2)}, u32[]{:S(2)}) collective-permute-start(bf16[64,512]{1,0:T(8,128)(2,1)S(1)} %slice.79), channel_id=1, source_target_pairs={{0,16},{16,0},{1,17},{17,1},{2,18},{18,2},{3,19},{19,3},{4,20},{20... | collective-permute-start | bytes 196616 | tf_op jit(solution)/shard_map/ppermute | solution.py:34
  138.1 3.2 %fusion.5.refs_1_ = f32[128,512]{1,0:T(8,128)S(1)} fusion(bf16[4096,512]{1,0:T(8,128)(2,1)} %param.19, bf16[64,4096]{1,0:T(8,128)(2,1)} %collective-permute-done.15, bf16[64,4096]{1,0:T(8,128)(2,1)} %get-tuple-element.51), kind=kOutput, calls=%fused_computation.9 | convolution fusion | flops 538968064 | bytes 5505024 | tf_op jit(solution)/shard_map/dot_general | solution.py:29
  142.1 7.4 %finish.1 = (f32[2560,512]{1,0:T(8,128)}, f32[8,512]{1,0:T(8,128)}) custom-call(s32[16]{0:T(128)} %copy-done.14, f32[16,1,1024]{2,1,0:T(1,128)} %all_to_all.15.sums_ref, bf16[512,512]{1,0:T(8,128)(2,1)} %get-tuple-element.61.embed_ref, f32[512,512]{1,0:T(8,128)} %convolution_multiply_fusion.refs_4_.weighted_ref, bf16[256,2560]{1,0:T(8,128)(2,1)} %pad_maximum_fusion.refs_0_, ...), custom_call_target="tpu_custom_call" | custom-call | tf_op jit(solution)/shard_map/finish/pallas_call | solution.py:320
  150.2 2.4 %shard_map.137 = bf16[128,512]{1,0:T(8,128)(2,1)} custom-call(s32[2]{0:T(128)} %pad_add_fusion.2.index_ref, s32[1,16,2]{2,1,0:T(8,128)} %copy.30.grid_ref, s32[1,16]{1,0:T(1,128)} %start_ref.3, f32[128,512]{1,0:T(8,128)} %copy-done.5, f32[128,512]{1,0:T(8,128)} %copy-done.6, bf16[64,512]{1,0:T(8,128)(2,1)} %copy-done.10, bf16[64,512]{1,0:T(8,128)(2,1)} %copy-done.11, ...), custom_call_target="tpu_custom_call" | custom-call | tf_op jit(solution)/shard_map/pallas_call | solution.py:99
  (101 shorter events, 29.0 us)
Async XLA Ops:
  0.6 76.6 %copy-start = (bf16[2560,512]{1,0:T(8,128)(2,1)S(1)}, bf16[2560,512]{1,0:T(8,128)(2,1)}, u32[]{:S(2)}) copy-start(bf16[2560,512]{1,0:T(8,128)(2,1)} %param.16) | copy-start | bytes 7864324
  0.6 15.2 %copy-start.13 = (s32[1,16,2]{1,2,0:T(2,128)S(1)}, s32[1,16,2]{1,2,0:T(2,128)}, u32[]{:S(2)}) copy-start(s32[1,16,2]{1,2,0:T(2,128)} %param.21) | copy-start | bytes 388
  1.5 6.7 %collective-permute-start = (s32[3,16]{1,0:T(4,128)S(1)}, s32[3,16]{1,0:T(4,128)S(1)}, u32[]{:S(2)}, u32[]{:S(2)}) collective-permute-start(s32[3,16]{1,0:T(4,128)S(1)} %get-tuple-element.72), channel_id=1, source_target_pairs={{0,16},{16,0},{1,17},{17,1},{2,18},{18,2},{3,19},{19,3},{4,20},{20... | collective-permute-start | bytes 584 | tf_op jit(solution)/shard_map/ppermute | solution.py:34
  5.7 5.7 %collective-permute-start.1 = (bf16[64,1280]{1,0:T(8,128)(2,1)S(1)}, bf16[64,1280]{1,0:T(8,128)(2,1)S(1)}, u32[]{:S(2)}, u32[]{:S(2)}) collective-permute-start(bf16[64,1280]{1,0:T(8,128)(2,1)S(1)} %convolution_convert_fusion.refs_0_.refs_2_), channel_id=1, source_target_pairs={{0,16},{16,0},{1,17},{17,1},{2,18},{18,2},{3,19},{19,3},{4,20},{20... | collective-permute-start | bytes 491528 | tf_op jit(solution)/shard_map/ppermute | solution.py:34
  8.3 29.0 %copy-start.15 = (s32[2]{0:T(128)}, s32[2]{0:T(128)S(1)}, u32[]{:S(2)}) copy-start(s32[2]{0:T(128)S(1)} %select_reduce_fusion.1.count_ref) | copy-start | bytes 28
  16.5 10.2 %collective-permute-start.2 = (bf16[2,64,960]{2,1,0:T(8,128)(2,1)}, bf16[2,64,960]{2,1,0:T(8,128)(2,1)S(1)}, u32[]{:S(2)}, u32[]{:S(2)}) collective-permute-start(bf16[2,64,960]{2,1,0:T(8,128)(2,1)} %bitcast.51), channel_id=1, source_target_pairs={{0,16},{16,0},{1,17},{17,1},{2,18},{18,2},{3,19},{19,3},{4,20},{20... | collective-permute-start | bytes 737288 | tf_op jit(solution)/shard_map/ppermute | solution.py:34
  22.1 3.9 %collective-permute-start.3 = (bf16[16,512]{1,0:T(8,128)(2,1)}, bf16[16,512]{1,0:T(8,128)(2,1)S(1)}, u32[]{:S(2)}, u32[]{:S(2)}) collective-permute-start(bf16[16,512]{1,0:T(8,128)(2,1)} %shard_map.134), channel_id=1, source_target_pairs={{0,16},{16,0},{1,17},{17,1},{2,18},{18,2},{3,19},{19,3},{4,20},{20... | collective-permute-start | bytes 49160 | tf_op jit(solution)/shard_map/ppermute | solution.py:34
  31.0 6.4 %collective-permute-start.4 = (bf16[2,32,1280]{2,1,0:T(8,128)(2,1)}, bf16[2,32,1280]{2,1,0:T(8,128)(2,1)S(1)}, u32[]{:S(2)}, u32[]{:S(2)}) collective-permute-start(bf16[2,32,1280]{2,1,0:T(8,128)(2,1)} %bitcast.52), channel_id=1, source_target_pairs={{0,16},{16,0},{1,17},{17,1},{2,18},{18,2},{3,19},{19,3},{4,20},{20... | collective-permute-start | bytes 491528 | tf_op jit(solution)/shard_map/ppermute | solution.py:34
  40.9 5.5 %collective-permute-start.5 = (bf16[32,1280]{1,0:T(8,128)(2,1)S(1)}, bf16[32,1280]{1,0:T(8,128)(2,1)S(1)}, u32[]{:S(2)}, u32[]{:S(2)}) collective-permute-start(bf16[32,1280]{1,0:T(8,128)(2,1)S(1)} %get-tuple-element.64), channel_id=1, source_target_pairs={{0,8},{1,9},{2,10},{3,11},{4,12},{5,13},{6,14},{7,15},{8,0},{9,1},... | collective-permute-start | bytes 245768 | tf_op jit(solution)/shard_map/ppermute | solution.py:52
  43.5 4.6 %collective-permute-start.8 = (bf16[32,1280]{1,0:T(8,128)(2,1)S(1)}, bf16[32,1280]{1,0:T(8,128)(2,1)S(1)}, u32[]{:S(2)}, u32[]{:S(2)}) collective-permute-start(bf16[32,1280]{1,0:T(8,128)(2,1)S(1)} %get-tuple-element.66), channel_id=1, source_target_pairs={{0,2},{1,3},{2,0},{3,1},{4,6},{5,7},{6,4},{7,5},{8,10},{9,11},{10,... | collective-permute-start | bytes 245768 | tf_op jit(solution)/shard_map/ppermute | solution.py:52
  46.4 5.7 %collective-permute-start.6 = (bf16[64,1280]{1,0:T(8,128)(2,1)S(1)}, bf16[64,1280]{1,0:T(8,128)(2,1)S(1)}, u32[]{:S(2)}, u32[]{:S(2)}) collective-permute-start(bf16[64,1280]{1,0:T(8,128)(2,1)S(1)} %pad_maximum_fusion.3), channel_id=1, source_target_pairs={{0,4},{1,5},{2,6},{3,7},{4,0},{5,1},{6,2},{7,3},{8,12},{9,13},{10,... | collective-permute-start | bytes 491528 | tf_op jit(solution)/shard_map/ppermute | solution.py:52
  48.1 17.5 %copy-start.17 = (s32[16]{0:T(128)S(1)}, s32[16]{0:T(128)}, u32[]{:S(2)}) copy-start(s32[16]{0:T(128)} %constant.109.clone) | copy-start | bytes 196
  48.1 8.3 %collective-permute-start.9 = (bf16[64,1280]{1,0:T(8,128)(2,1)S(1)}, bf16[64,1280]{1,0:T(8,128)(2,1)S(1)}, u32[]{:S(2)}, u32[]{:S(2)}) collective-permute-start(bf16[64,1280]{1,0:T(8,128)(2,1)S(1)} %pad_maximum_fusion.4), channel_id=1, source_target_pairs={{0,8},{1,9},{2,10},{3,11},{4,12},{5,13},{6,14},{7,15},{8,0},{9,1},... | collective-permute-start | bytes 491528 | tf_op jit(solution)/shard_map/ppermute | solution.py:52
  52.1 11.6 %collective-permute-start.7 = (bf16[128,1280]{1,0:T(8,128)(2,1)S(1)}, bf16[128,1280]{1,0:T(8,128)(2,1)S(1)}, u32[]{:S(2)}, u32[]{:S(2)}) collective-permute-start(bf16[128,1280]{1,0:T(8,128)(2,1)S(1)} %pad_maximum_fusion.1), channel_id=1, source_target_pairs={{0,2},{1,3},{2,0},{3,1},{4,6},{5,7},{6,4},{7,5},{8,10},{9,11},{10,... | collective-permute-start | bytes 983048 | tf_op jit(solution)/shard_map/ppermute | solution.py:52
  56.4 7.1 %collective-permute-start.10 = (bf16[128,1280]{1,0:T(8,128)(2,1)S(1)}, bf16[128,1280]{1,0:T(8,128)(2,1)S(1)}, u32[]{:S(2)}, u32[]{:S(2)}) collective-permute-start(bf16[128,1280]{1,0:T(8,128)(2,1)S(1)} %pad_maximum_fusion.2), channel_id=1, source_target_pairs={{0,4},{1,5},{2,6},{3,7},{4,0},{5,1},{6,2},{7,3},{8,12},{9,13},{10,... | collective-permute-start | bytes 983048 | tf_op jit(solution)/shard_map/ppermute | solution.py:52
  64.9 17.4 %collective-permute-start.12 = (bf16[256,2560]{1,0:T(8,128)(2,1)}, bf16[256,2560]{1,0:T(8,128)(2,1)}, u32[]{:S(2)}, u32[]{:S(2)}) collective-permute-start(bf16[256,2560]{1,0:T(8,128)(2,1)} %pad_maximum_fusion.refs_0_), channel_id=1, source_target_pairs={{0,1},{1,0},{2,3},{3,2},{4,5},{5,4},{6,7},{7,6},{8,9},{9,8},{10,11... | collective-permute-start | bytes 3932168 | tf_op jit(solution)/shard_map/ppermute | solution.py:76
  65.6 48.8 %copy-start.12 = (f32[512]{0:T(512)}, f32[512]{0:T(512)S(1)}, u32[]{:S(2)}) copy-start(f32[512]{0:T(512)S(1)} %dynamic_slice.7) | copy-start | bytes 6148
  65.7 14.6 %copy-start.14 = (s32[16]{0:T(128)}, s32[16]{0:T(128)S(1)}, u32[]{:S(2)}) copy-start(s32[16]{0:T(128)S(1)} %broadcast_xor_fusion.owner_ref) | copy-start | bytes 196
  67.3 34.4 %all-to-all-start = ((bf16[16,32,512]{2,1,0:T(8,128)(2,1)}), bf16[16,32,512]{2,1,0:T(8,128)(2,1)}, u32[]{:S(2)}, u32[]{:S(2)}) async-start(bf16[16,32,512]{2,1,0:T(8,128)(2,1)} %broadcast_in_dim.20), calls=%async_computation | async-start | bytes 1048576 | tf_op jit(solution)/shard_map/all_to_all | solution.py:574
  74.3 27.2 %collective-permute-start.18 = (bf16[512,512]{1,0:T(8,128)(2,1)S(1)}, bf16[512,512]{1,0:T(8,128)(2,1)S(1)}, u32[]{:S(2)}, u32[]{:S(2)}) collective-permute-start(bf16[512,512]{1,0:T(8,128)(2,1)S(1)} %constant_dynamic-slice_fusion), channel_id=1, source_target_pairs={{0,16},{1,17},{2,18},{3,19},{4,20},{5,21},{6,22},{7,23},{24,8},{25... | collective-permute-start | bytes 1572872 | tf_op jit(solution)/shard_map/ppermute | solution.py:593
  77.1 23.6 %collective-permute-start.14 = (bf16[64,4096]{1,0:T(8,128)(2,1)}, bf16[64,4096]{1,0:T(8,128)(2,1)S(1)}, u32[]{:S(2)}, u32[]{:S(2)}) collective-permute-start(bf16[64,4096]{1,0:T(8,128)(2,1)} %get-tuple-element.49), channel_id=1, source_target_pairs={{0,16},{16,0},{1,17},{17,1},{2,18},{18,2},{3,19},{19,3},{4,20},{20... | collective-permute-start | bytes 1572872 | tf_op jit(solution)/shard_map/ppermute | solution.py:34
  80.3 20.5 %copy-start.7 = (bf16[4096,512]{1,0:T(8,128)(2,1)S(1)}, bf16[4096,512]{1,0:T(8,128)(2,1)}, u32[]{:S(2)}) copy-start(bf16[4096,512]{1,0:T(8,128)(2,1)} %param.19) | copy-start | bytes 12582916
  80.3 20.5 %copy-start.16 = (bf16[64,4096]{1,0:T(8,128)(2,1)S(1)}, bf16[64,4096]{1,0:T(8,128)(2,1)}, u32[]{:S(2)}) copy-start(bf16[64,4096]{1,0:T(8,128)(2,1)} %get-tuple-element.48) | copy-start | bytes 1572868
  80.3 26.1 %collective-permute-start.11 = (bf16[256,512]{1,0:T(8,128)(2,1)}, bf16[256,512]{1,0:T(8,128)(2,1)}, u32[]{:S(2)}, u32[]{:S(2)}) collective-permute-start(bf16[256,512]{1,0:T(8,128)(2,1)} %get-tuple-element.73), channel_id=1, source_target_pairs={{0,16},{16,0},{1,17},{17,1},{2,18},{18,2},{3,19},{19,3},{4,20},{20... | collective-permute-start | bytes 786440 | tf_op jit(solution)/shard_map/ppermute | solution.py:34
  85.4 26.0 %collective-permute-start.13 = (bf16[256,512]{1,0:T(8,128)(2,1)}, bf16[256,512]{1,0:T(8,128)(2,1)}, u32[]{:S(2)}, u32[]{:S(2)}) collective-permute-start(bf16[256,512]{1,0:T(8,128)(2,1)} %get-tuple-element.75), channel_id=1, source_target_pairs={{0,16},{16,0},{1,17},{17,1},{2,18},{18,2},{3,19},{19,3},{4,20},{20... | collective-permute-start | bytes 786440 | tf_op jit(solution)/shard_map/ppermute | solution.py:34
  101.5 34.5 %copy-start.5 = (f32[128,512]{1,0:T(8,128)}, f32[128,512]{1,0:T(8,128)S(1)}, u32[]{:S(2)}) copy-start(f32[128,512]{1,0:T(8,128)S(1)} %fusion.1.refs_0_) | copy-start | bytes 786436
  101.7 14.3 %copy-start.1 = (bf16[512,512]{1,0:T(8,128)(2,1)}, bf16[512,512]{1,0:T(8,128)(2,1)S(1)}, u32[]{:S(2)}) copy-start(bf16[512,512]{1,0:T(8,128)(2,1)S(1)} %select_add_fusion.refs_6_) | copy-start | bytes 1572868
  111.4 26.7 %collective-permute-start.15 = (bf16[64,4096]{1,0:T(8,128)(2,1)}, bf16[64,4096]{1,0:T(8,128)(2,1)}, u32[]{:S(2)}, u32[]{:S(2)}) collective-permute-start(bf16[64,4096]{1,0:T(8,128)(2,1)} %get-tuple-element.52), channel_id=1, source_target_pairs={{0,16},{16,0},{1,17},{17,1},{2,18},{18,2},{3,19},{19,3},{4,20},{20... | collective-permute-start | bytes 1572872 | tf_op jit(solution)/shard_map/ppermute | solution.py:34
  132.4 17.1 %all-to-all-start.2 = ((bf16[16,16,512]{2,1,0:T(8,128)(2,1)}), bf16[16,16,512]{2,1,0:T(8,128)(2,1)S(1)}, u32[]{:S(2)}, u32[]{:S(2)}) async-start(bf16[16,16,512]{2,1,0:T(8,128)(2,1)} %get-tuple-element.59), calls=%async_computation.2 | async-start | bytes 524288 | tf_op jit(solution)/shard_map/all_to_all | solution.py:631
  136.0 13.5 %collective-permute-start.16 = (bf16[64,512]{1,0:T(8,128)(2,1)S(1)}, bf16[64,512]{1,0:T(8,128)(2,1)S(1)}, u32[]{:S(2)}, u32[]{:S(2)}) collective-permute-start(bf16[64,512]{1,0:T(8,128)(2,1)S(1)} %slice.79), channel_id=1, source_target_pairs={{0,16},{16,0},{1,17},{17,1},{2,18},{18,2},{3,19},{19,3},{4,20},{20... | collective-permute-start | bytes 196616 | tf_op jit(solution)/shard_map/ppermute | solution.py:34
  141.3 8.2 %copy-start.6 = (f32[128,512]{1,0:T(8,128)}, f32[128,512]{1,0:T(8,128)S(1)}, u32[]{:S(2)}) copy-start(f32[128,512]{1,0:T(8,128)S(1)} %fusion.5.refs_1_) | copy-start | bytes 786436
  141.4 8.1 %collective-permute-start.17 = (bf16[64,512]{1,0:T(8,128)(2,1)S(1)}, bf16[64,512]{1,0:T(8,128)(2,1)S(1)}, u32[]{:S(2)}, u32[]{:S(2)}) collective-permute-start(bf16[64,512]{1,0:T(8,128)(2,1)S(1)} %slice.78), channel_id=1, source_target_pairs={{0,16},{16,0},{1,17},{17,1},{2,18},{18,2},{3,19},{19,3},{4,20},{20... | collective-permute-start | bytes 196616 | tf_op jit(solution)/shard_map/ppermute | solution.py:34
  (7 other events, 9.8 us)

commit v4 on v3

--- a/solution.py
+++ b/solution.py
@@ -230,7 +230,9 @@
     def kernel(owner_ref, holder_ref, *refs):
         part_refs = refs[:chunks]
         received_refs = refs[chunks : chunks + len(flat)]
-        weighted_ref, gain_ref, key_ref, embed_ref, sums_ref, keys_ref = refs[chunks + len(flat) :]
+        weighted_ref, gain_ref, key_ref, embed_ref, sums_ref, keys_ref, squared, multiplied = refs[
+            chunks + len(flat) :
+        ]
         picked = []
         for i in range(groups):
             chunk, base = i // per_chunk, (i % per_chunk) * rows
@@ -246,19 +248,25 @@
                 )
             block = block.astype(BF16)
             picked.append((block[:capacity].astype(F32) * gain_ref[...]).astype(BF16))
-            embed_ref[pl.ds(pl.multiple_of(owner_ref[i] * rows, rows), rows), :] = block
-        values = embed_ref[...].astype(F32)
+            embed_ref[pl.ds(i * rows, rows), :] = block
+            values = block.astype(F32)
+            at = pl.ds(pl.multiple_of(owner_ref[i] * rows, rows), rows)
+            squared[at, :] = values * values
+            multiplied[at, :] = values * weighted_ref[pl.ds(i * rows, rows), :]
         ones = jnp.ones((8, columns), F32)
-        contract = (((1,), (1,)), ((), ()))
-        squares = lax.dot_general(
-            ones, values * values, contract, precision=HIGHEST, preferred_element_type=F32
-        )
-        products = lax.dot_general(
-            ones, values * weighted_ref[...], contract, precision=HIGHEST, preferred_element_type=F32
-        )
+        both = [
+            lax.dot_general(
+                ones,
+                ref[...],
+                (((1,), (1,)), ((), ())),
+                precision=HIGHEST,
+                preferred_element_type=F32,
+            )[0:1]
+            for ref in (squared, multiplied)
+        ]
         for i in range(groups):
-            sums_ref[i, :, 0:total] = squares[0:1]
-            sums_ref[i, :, total : 2 * total] = products[0:1]
+            sums_ref[i, :, 0:total] = both[0]
+            sums_ref[i, :, total : 2 * total] = both[1]
         terms = dot(jnp.concatenate(picked, axis=0), key_ref[...]).astype(BF16)
         for i in range(groups):
             keys_ref[holder_ref[i]] = terms[i * capacity : (i + 1) * capacity]
@@ -272,81 +280,43 @@
         ),
         (owners, holders, *own_parts, *flat, weighted, gain, key_rows),
         scalars=2,
-    )
-
-
-def finish(groups, width, owners, sums, embedded, weighted, merged):
-    total, columns = embedded.shape
+        scratch=[pltpu.VMEM((total, columns), F32), pltpu.VMEM((total, columns), F32)],
+    )
+
+
+def norm_scales(groups, width, owners, sums):
+    total = sums.shape[2] // 2
     rows = total // groups
-    chunks = len(merged)
-    chunk = total // chunks
-    height = merged[0].shape[1]
-    bands = 5 if height % (5 * 128) == 0 else 1
-    band = height // bands
-
-    def kernel(owner_ref, sums_ref, embed_ref, weighted_ref, *refs):
-        merged_refs = refs[:chunks]
-        out_ref, scale_ref, grads, ordered = refs[chunks:]
-
-        @pl.when(pl.program_id(0) == 0)
-        def _():
-            whole = jnp.sum(sums_ref[...], axis=0)
-            scale = lax.rsqrt(whole[:, :total] / width + EPS)
-            slope = scale**3 * whole[:, total:] / width
-            line = lax.broadcasted_iota(jnp.int32, (8, total), 0)
-            both = jnp.where(line == 0, scale, slope)
-            scale_ref[...] = both
-            columns_of = jnp.transpose(both)
-            grads[...] = (
-                columns_of[:, 0:1] * weighted_ref[...]
-                - embed_ref[...].astype(F32) * columns_of[:, 1:2]
-            ).astype(BF16)
-            for i in range(groups):
-                ordered[pl.ds(i * rows, rows), :] = grads[
-                    pl.ds(pl.multiple_of(owner_ref[i] * rows, rows), rows), :
-                ]
-
-        result = None
-        for j in range(chunks):
-            term = lax.dot_general(
-                merged_refs[j][...],
-                ordered[j * chunk : (j + 1) * chunk, :],
-                (((0,), (0,)), ((), ())),
-                preferred_element_type=F32,
-            )
-            result = term if result is None else result + term
-        out_ref[...] = result
-
-    return pl.pallas_call(
-        kernel,
-        grid=(bands,),
-        out_shape=(
-            jax.ShapeDtypeStruct((height, columns), F32),
-            jax.ShapeDtypeStruct((8, total), F32),
-        ),
-        in_specs=[
-            SMEM,
-            pl.BlockSpec(sums.shape, lambda g: (0, 0, 0)),
-            pl.BlockSpec(embedded.shape, lambda g: (0, 0)),
-            pl.BlockSpec(weighted.shape, lambda g: (0, 0)),
-        ]
-        + [pl.BlockSpec((chunk, band), lambda g: (0, g))] * chunks,
-        out_specs=[
-            pl.BlockSpec((band, columns), lambda g: (g, 0)),
-            pl.BlockSpec((8, total), lambda g: (0, 0)),
-        ],
-        scratch_shapes=[pltpu.VMEM((total, columns), BF16), pltpu.VMEM((total, columns), BF16)],
-        compiler_params=pltpu.CompilerParams(dimension_semantics=("arbitrary",)),
-        name="finish",
-    )(owners, sums, embedded, weighted, *merged)
-
-
-def merge(parts, places, counts, hidden, received):
+
+    def kernel(owner_ref, sums_ref, scale_ref, columns_ref, turned):
+        whole = jnp.sum(sums_ref[...], axis=0)
+        scale = lax.rsqrt(whole[:, :total] / width + EPS)
+        slope = scale**3 * whole[:, total:] / width
+        line = lax.broadcasted_iota(jnp.int32, (8, total), 0)
+        both = jnp.where(line == 0, scale, slope)
+        scale_ref[...] = both
+        turned[...] = jnp.transpose(both)
+        for i in range(groups):
+            columns_ref[pl.ds(i * rows, rows), :] = turned[
+                pl.ds(pl.multiple_of(owner_ref[i] * rows, rows), rows), :
+            ]
+
+    return call(
+        kernel,
+        (jax.ShapeDtypeStruct((8, total), F32), jax.ShapeDtypeStruct((total, 8), F32)),
+        (owners, sums),
+        scalars=1,
+        scratch=[pltpu.VMEM((total, 8), F32)],
+    )
+
+
+def merge(parts, places, counts, hidden, received, extra):
     taken, width = hidden.shape[1:]
     capacity = taken // places
+    main = places * width
 
     def kernel(count_ref, *refs):
-        hidden_ref, received_refs, out_ref = refs[0], refs[1:-1], refs[-1]
+        hidden_ref, received_refs, extra_ref, out_ref = refs[0], refs[1:-2], refs[-2], refs[-1]
         slot = lax.broadcasted_iota(jnp.int32, (capacity, width), 0)
         for r in range(parts):
             total = hidden_ref[r]
@@ -357,11 +327,12 @@
                 kept = normed[p * capacity : (p + 1) * capacity]
                 kept = jnp.where(slot < count_ref[r], kept, jnp.zeros_like(kept))
                 out_ref[r * capacity : (r + 1) * capacity, p * width : (p + 1) * width] = kept
-
-    return call(
-        kernel,
-        (jax.ShapeDtypeStruct((parts * capacity, places * width), BF16),),
-        (counts, hidden, *received),
+        out_ref[:, main:] = extra_ref[...]
+
+    return call(
+        kernel,
+        (jax.ShapeDtypeStruct((parts * capacity, main + extra.shape[1]), BF16),),
+        (counts, hidden, *received, extra),
         scalars=1,
     )[0]
 
@@ -569,16 +540,15 @@
     piece_width = vit_width // pieces
     scalars = jnp.concatenate([index[:1], own_counts])
     hidden_rows, sent = attend(parts, places, scalars, mine, received, images, vit_out)
-    sent, grads = barrier((sent, grads))
     received = [shift(sent[k - 1], k) for k in others]
-    grads = lax.all_to_all(
-        jnp.broadcast_to(grads[None], (groups,) + grads.shape), "ctx", 0, 0, tiled=True
-    )
     received, text_blocks, key_source = barrier((received, text_blocks, key_weight))
-    merged = merge(parts, places, own_counts, hidden_rows, received)
+    merged = merge(parts, places, own_counts, hidden_rows, received, grads)
     if pieces > 1:
-        merged = lax.dynamic_slice_in_dim(merged, (own_part % pieces) * piece_width, piece_width, 1)
+        taken = lax.dynamic_slice_in_dim(merged, (own_part % pieces) * piece_width, piece_width, 1)
+        merged = jnp.concatenate([taken, grads], axis=1)
     merged_all, owners = gather_halves(merged)
+    main = places * piece_width
+    grads = jnp.concatenate([rows[:, main:] for rows in merged_all], axis=0)
 
     part_features = width // parts
     own_start = own * feature_cols
@@ -604,8 +574,10 @@
     early_terms = text_terms(text_blocks[0])
 
     grads = grads.reshape(groups, parts, capacity, key_width)
-    routing = (target_range[:, :, None] == group_index[None, None, :]).astype(BF16)
-    grads = jnp.einsum("roh,hrkw->orkw", routing, grads, preferred_element_type=F32).astype(BF16)
+    block_owner = (owners[:, None] == group_index[None, :]).astype(jnp.int32)
+    block_range = jnp.sum(block_owner[None] * target_range[:, None, :], axis=-1)
+    routing = (block_range[:, :, None] == owners[None, None, :]).astype(BF16)
+    grads = jnp.einsum("roi,irkw->orkw", routing, grads, preferred_element_type=F32).astype(BF16)
     weighted = (
         lax.dot_general(
             grads.reshape(-1, key_width),
@@ -616,20 +588,23 @@
         * own_gain
     )
 
-    embed_parts = [dot(rows, merger) for rows in merged_all]
+    embed_parts = [dot(rows[:, :main], merger) for rows in merged_all]
+    joined = jnp.concatenate([rows[:, :main] for rows in merged_all], axis=0)
     received = [[shift(part.astype(BF16), k) for k in others] for part in embed_parts]
-    block_owner = (owners[:, None] == group_index[None, :]).astype(jnp.int32)
-    block_range = jnp.sum(block_owner * target_range[0][None, :], axis=-1)
-    received, late_blocks, early_terms = barrier((received, text_blocks[1], early_terms))
+    received, late_blocks = barrier((received, text_blocks[1]))
     embedded, sums, outgoing = features(
-        parts, groups, owners, block_range, embed_parts, received, weighted, own_gain, key_rows
+        parts, groups, owners, block_range[0], embed_parts, received, weighted, own_gain, key_rows
     )
     sums = lax.all_to_all(sums, "ctx", 0, 0, tiled=True)
     late_terms = text_terms(late_blocks)
+    arrived = lax.all_to_all(outgoing, "ctx", 0, 0, tiled=True)
     returned = [text_return(early_terms), text_return(late_terms)]
-    sums, outgoing = barrier((sums, outgoing))
-    arrived = lax.all_to_all(outgoing, "ctx", 0, 0, tiled=True)
-    merger_grad, scales = finish(groups, float(width), owners, sums, embedded, weighted, merged_all)
+    scales, columns = norm_scales(groups, float(width), owners, sums)
+    grad_embedded = columns[:, 0:1] * weighted - embedded.astype(F32) * columns[:, 1:2]
+    grad_embedded = grad_embedded.astype(BF16)
+    merger_grad = lax.dot_general(
+        joined, grad_embedded, (((0,), (0,)), ((), ())), preferred_element_type=F32
+    )
     rotated = keys_out(
         parts,
         groups,

time: 154 us -> 155 us (level)
  blocking collectives: 11.8 us -> 0 us
  local copies, waits for them, and re-layouts: 12.7 us -> 20.3 us
  matrix products: 13 us -> 19.6 us
  Pallas kernels: 31.8 us -> 26.6 us
  waiting for transfers between devices: 37.5 us -> 39.3 us
    all_to_all x1 -> x0, blocking collectives: 11.8 us -> none  [on_device(): sums = lax.all_to_all(sums, 'ctx', 0, 0, tiled=True)]
    ppermute x1, waiting for transfers between devices: 0.01 us -> 11.5 us  [on_device(): key_rows = key_rows + lax.ppermute(candidate, ('dp', 'ctx'), pairs)]
    ppermute x11, waiting for transfers between devices: 28 us -> 16.5 us  [shift(): return lax.ppermute(x, 'dp', [(i, (i + k) % size) for i in range(size)])]
    slice x0 -> x5, local copies, waits for them, and re-layouts: none -> 8.38 us  [the longest x2 4.93 us: on_device(): embed_parts = [dot(rows[:, :main], merger) for rows in merged_all]]
    pallas_call x1 -> x0, Pallas kernels: 7.35 us -> none  [finish(): pl.pallas_call(kernel, grid=(bands,), out_shape=(jax.ShapeDtypeStruct((he...]
    dot_general x1 -> x2, matrix products: 0.34 us -> 4.48 us  [the longest x1 4.05 us: on_device(): lax.dot_general(joined, grad_embedded, (((0,), (0,)), ((), ())), preferre...]
    all_to_all x1, starting transfers between devices: 3.53 us -> 6.02 us  [on_device(): arrived = lax.all_to_all(outgoing, 'ctx', 0, 0, tiled=True)]
    dot_general x5, matrix products: 11.2 us -> 13.7 us  [dot(): return jnp.dot(a, b, preferred_element_type=F32, **kw)]
  transfers between devices with their start and end apart: 21 -> 21, of which waited for: 9 -> 10; matrix products, arithmetic and copies ran while one was open for 16% -> 26% of each run, Pallas kernels for 13% -> 12%
where the time goes in v4:
time: 155 us; the launch traced here: 153 us
  starting transfers between devices  39.6 us (26%)
  waiting for transfers between devices  39.3 us (25%)
  Pallas kernels  26.6 us (17%)
  local copies, waits for them, and re-layouts  20.3 us (13%)
  matrix products  19.6 us (13%)
  other arithmetic  6.94 us (4%)
    pallas_call x8, Pallas kernels, call(): pl.pallas_call(kernel, out_shape=outs, in_specs=[SMEM] * scalars + [VMEM]...  21.9 us
    ppermute x11, waiting for transfers between devices, shift(): return lax.ppermute(x, 'dp', [(i, (i + k) % size) for i in range(size)])  16.5 us
    dot_general x5, matrix products, dot(): return jnp.dot(a, b, preferred_element_type=F32, **kw)  13.7 us
    ppermute x6, starting transfers between devices, xor_gather(): lax.ppermute(joined, 'ctx', [(i, i ^ stride) for i in range(size)])  12.9 us
    ppermute x11, starting transfers between devices, shift(): return lax.ppermute(x, 'dp', [(i, (i + k) % size) for i in range(size)])  12.5 us
    ppermute x1, waiting for transfers between devices, on_device(): key_rows = key_rows + lax.ppermute(candidate, ('dp', 'ctx'), pairs)  11.5 us
    ppermute x6, waiting for transfers between devices, xor_gather(): lax.ppermute(joined, 'ctx', [(i, i ^ stride) for i in range(size)])  11.3 us
    all_to_all x1, starting transfers between devices, on_device(): arrived = lax.all_to_all(outgoing, 'ctx', 0, 0, tiled=True)  6.02 us
  transfers between devices with their start and end apart: 21, of which 10 were waited for; matrix products, arithmetic and copies ran while one was open for 26% of the time, Pallas kernels for 12%

profile of v4, /device:TPU:0, one launch (start us, length us, event | category | flops | bytes accessed | tf_op | source)
XLA Modules:
  0.0 153.4 jit_solution(1572308572442077998)
XLA Ops:
  1.5 3.0 %collective-permute-start = (s32[3,16]{1,0:T(4,128)S(1)}, s32[3,16]{1,0:T(4,128)S(1)}, u32[]{:S(2)}, u32[]{:S(2)}) collective-permute-start(s32[3,16]{1,0:T(4,128)S(1)} %get-tuple-element.64), channel_id=1, source_target_pairs={{0,16},{16,0},{1,17},{17,1},{2,18},{18,2},{3,19},{19,3},{4,20},{20... | collective-permute-start | bytes 584 | tf_op jit(solution)/shard_map/ppermute | solution.py:34
  8.1 3.2 %collective-permute-done.1.refs_1_.refs_3_ = bf16[64,1280]{1,0:T(8,128)(2,1)S(1)} collective-permute-done((bf16[64,1280]{1,0:T(8,128)(2,1)S(1)}, bf16[64,1280]{1,0:T(8,128)(2,1)S(1)}, u32[]{:S(2)}, u32[]{:S(2)}) %collective-permute-start.1) | collective-permute-done | bytes 163872 | tf_op jit(solution)/shard_map/ppermute | solution.py:34
  12.0 3.8 %shard_map.131 = (f32[2,64,960]{2,1,0:T(8,128)}, bf16[1,2,64,960]{3,2,1,0:T(8,128)(2,1)}) custom-call(s32[2]{0:T(128)} %pad_add_fusion.2.index_ref, bf16[64,1280]{1,0:T(8,128)(2,1)} %copy-done.4, bf16[64,1280]{1,0:T(8,128)(2,1)} %copy-done.8, f32[1,1280]{1,0:T(1,128)} %reshape.107.refs_2_, bf16[640,1920]{1,0:T(8,128)(2,1)} %refs_3_.1), custom_call_target="tpu_custom_call" | custom-call | tf_op jit(solution)/shard_map/pallas_call | solution.py:99
  19.2 3.7 %collective-permute-done.2.refs_1_ = bf16[2,64,960]{2,1,0:T(8,128)(2,1)S(1)} collective-permute-done((bf16[2,64,960]{2,1,0:T(8,128)(2,1)}, bf16[2,64,960]{2,1,0:T(8,128)(2,1)S(1)}, u32[]{:S(2)}, u32[]{:S(2)}) %collective-permute-start.2) | collective-permute-done | bytes 245792 | tf_op jit(solution)/shard_map/ppermute | solution.py:34
  23.7 3.5 %shard_map.132 = (f32[2,32,1280]{2,1,0:T(8,128)}, bf16[1,2,32,1280]{3,2,1,0:T(8,128)(2,1)}) custom-call(s32[3]{0:T(128)} %pad_add_fusion.3.scalar_ref, f32[2,64,960]{2,1,0:T(8,128)} %get-tuple-element.28.refs_0_, bf16[2,64,960]{2,1,0:T(8,128)(2,1)} %copy-done.14, bf16[64,1280]{1,0:T(8,128)(2,1)} %copy-done.4, bf16[64,1280]{1,0:T(8,128)(2,1)} %copy-done.8, ...), custom_call_target="tpu_custom_call" | custom-call | tf_op jit(solution)/shard_map/pallas_call | solution.py:99
  29.5 1.9 %shard_map.134 = bf16[16,512]{1,0:T(8,128)(2,1)} custom-call(s32[2]{0:T(128)} %pad_add_fusion.2.index_ref, s32[1,16,2]{2,1,0:T(8,128)} %copy.24.grid_ref, s32[1,16]{1,0:T(1,128)} %start_ref.3, bf16[128,512]{1,0:T(8,128)(2,1)} %bitcast.40, f32[128,128]{1,0:T(8,128)} %get-tuple-element.60.cosine_ref.refs_6_, f32[128,128]{1,0:T(8,128)} %get-tuple-element.59.sine_ref.refs_7_), custom_call_target="tpu_custom_call" | custom-call | tf_op jit(solution)/shard_map/pallas_call | solution.py:99
  32.8 4.7 %text_norm.1 = (bf16[64,4096]{1,0:T(8,128)(2,1)}, bf16[64,4096]{1,0:T(8,128)(2,1)}, bf16[64,4096]{1,0:T(8,128)(2,1)}, bf16[64,4096]{1,0:T(8,128)(2,1)}) custom-call(s32[2]{0:T(128)} %pad_add_fusion.2.index_ref, bf16[128,8192]{1,0:T(8,128)(2,1)} %bitcast.38, f32[1,8192]{1,0:T(1,128)} %bitcast.42), custom_call_target="tpu_custom_call" | custom-call | tf_op jit(solution)/shard_map/text_norm/pallas_call | solution.py:468
  39.6 2.0 %shard_map.135 = bf16[32,3072]{1,0:T(8,128)(2,1)} custom-call(s32[2]{0:T(128)} %copy-done.21, f32[2,32,1280]{2,1,0:T(8,128)} %get-tuple-element.38.refs_0_, bf16[2,32,1280]{2,1,0:T(8,128)(2,1)} %copy-done.15, bf16[32,512]{1,0:T(8,128)(2,1)} %pad_maximum_fusion.6.refs_2_), custom_call_target="tpu_custom_call" | custom-call | tf_op jit(solution)/shard_map/pallas_call | solution.py:99
  42.5 2.7 %collective-permute-start.6 = (bf16[32,1536]{1,0:T(8,128)(2,1)S(1)}, bf16[32,1536]{1,0:T(8,128)(2,1)S(1)}, u32[]{:S(2)}, u32[]{:S(2)}) collective-permute-start(bf16[32,1536]{1,0:T(8,128)(2,1)S(1)} %get-tuple-element.56), channel_id=1, source_target_pairs={{0,8},{1,9},{2,10},{3,11},{4,12},{5,13},{6,14},{7,15},{8,0},{9,1},... | collective-permute-start | bytes 294920 | tf_op jit(solution)/shard_map/ppermute | solution.py:52
  48.2 1.7 %collective-permute-start.7 = (bf16[64,1536]{1,0:T(8,128)(2,1)S(1)}, bf16[64,1536]{1,0:T(8,128)(2,1)S(1)}, u32[]{:S(2)}, u32[]{:S(2)}) collective-permute-start(bf16[64,1536]{1,0:T(8,128)(2,1)S(1)} %pad_maximum_fusion.4), channel_id=1, source_target_pairs={{0,4},{1,5},{2,6},{3,7},{4,0},{5,1},{6,2},{7,3},{8,12},{9,13},{10,... | collective-permute-start | bytes 589832 | tf_op jit(solution)/shard_map/ppermute | solution.py:52
  50.0 3.7 %collective-permute-start.10 = (bf16[64,1536]{1,0:T(8,128)(2,1)S(1)}, bf16[64,1536]{1,0:T(8,128)(2,1)S(1)}, u32[]{:S(2)}, u32[]{:S(2)}) collective-permute-start(bf16[64,1536]{1,0:T(8,128)(2,1)S(1)} %pad_maximum_fusion.5), channel_id=1, source_target_pairs={{0,8},{1,9},{2,10},{3,11},{4,12},{5,13},{6,14},{7,15},{8,0},{9,1},... | collective-permute-start | bytes 589832 | tf_op jit(solution)/shard_map/ppermute | solution.py:52
  55.8 3.2 %collective-permute-done.10 = bf16[64,1536]{1,0:T(8,128)(2,1)S(1)} collective-permute-done((bf16[64,1536]{1,0:T(8,128)(2,1)S(1)}, bf16[64,1536]{1,0:T(8,128)(2,1)S(1)}, u32[]{:S(2)}, u32[]{:S(2)}) %collective-permute-start.10) | collective-permute-done | bytes 196640 | tf_op jit(solution)/shard_map/ppermute | solution.py:52
  60.7 6.1 %collective-permute-done.11 = bf16[128,1536]{1,0:T(8,128)(2,1)S(1)} collective-permute-done((bf16[128,1536]{1,0:T(8,128)(2,1)S(1)}, bf16[128,1536]{1,0:T(8,128)(2,1)S(1)}, u32[]{:S(2)}, u32[]{:S(2)}) %collective-permute-start.11) | collective-permute-done | bytes 393248 | tf_op jit(solution)/shard_map/ppermute | solution.py:52
  71.7 2.5 %collective-permute-start.18 = (bf16[512,512]{1,0:T(8,128)(2,1)S(1)}, bf16[512,512]{1,0:T(8,128)(2,1)S(1)}, u32[]{:S(2)}, u32[]{:S(2)}) collective-permute-start(bf16[512,512]{1,0:T(8,128)(2,1)S(1)} %constant_dynamic-slice_fusion), channel_id=1, source_target_pairs={{0,16},{1,17},{2,18},{3,19},{4,20},{5,21},{6,22},{7,23},{24,8},{25... | collective-permute-start | bytes 1572872 | tf_op jit(solution)/shard_map/ppermute | solution.py:563
  74.9 11.5 %collective-permute-done.18 = bf16[512,512]{1,0:T(8,128)(2,1)S(1)} collective-permute-done((bf16[512,512]{1,0:T(8,128)(2,1)S(1)}, bf16[512,512]{1,0:T(8,128)(2,1)S(1)}, u32[]{:S(2)}, u32[]{:S(2)}) %collective-permute-start.18) | collective-permute-done | bytes 524320 | tf_op jit(solution)/shard_map/ppermute | solution.py:563
  88.8 3.0 %fusion.40 = (bf16[256,512]{1,0:T(8,128)(2,1)S(1)}, f32[256,512]{1,0:T(8,128)}) fusion(bf16[2560,512]{1,0:T(8,128)(2,1)S(1)} %copy-done, bf16[256,3072]{1,0:T(8,128)(2,1)} %pad_maximum_fusion), kind=kOutput, calls=%fused_computation.87 | convolution fusion | flops 671219712 | bytes 4718592 | tf_op jit(solution)/shard_map/dot_general | solution.py:29
  91.8 2.5 %collective-permute-start.12 = (bf16[256,512]{1,0:T(8,128)(2,1)S(1)}, bf16[256,512]{1,0:T(8,128)(2,1)S(1)}, u32[]{:S(2)}, u32[]{:S(2)}) collective-permute-start(bf16[256,512]{1,0:T(8,128)(2,1)S(1)} %get-tuple-element.65), channel_id=1, source_target_pairs={{0,16},{16,0},{1,17},{17,1},{2,18},{18,2},{3,19},{19,3},{4,20},{20... | collective-permute-start | bytes 786440 | tf_op jit(solution)/shard_map/ppermute | solution.py:34
  94.3 3.0 %fusion.41 = (bf16[256,512]{1,0:T(8,128)(2,1)S(1)}, f32[256,512]{1,0:T(8,128)}) fusion(bf16[2560,512]{1,0:T(8,128)(2,1)S(1)} %copy-done, bf16[256,3072]{1,0:T(8,128)(2,1)} %collective-permute-done.13), kind=kOutput, calls=%fused_computation.88 | convolution fusion | flops 671219712 | bytes 4718592 | tf_op jit(solution)/shard_map/dot_general | solution.py:29
  99.0 4.3 %collective-permute-done.12.refs_2_ = bf16[256,512]{1,0:T(8,128)(2,1)S(1)} collective-permute-done((bf16[256,512]{1,0:T(8,128)(2,1)S(1)}, bf16[256,512]{1,0:T(8,128)(2,1)S(1)}, u32[]{:S(2)}, u32[]{:S(2)}) %collective-permute-start.12) | collective-permute-done | bytes 262176 | tf_op jit(solution)/shard_map/ppermute | solution.py:34
  103.3 5.2 %collective-permute-done.14.refs_3_ = bf16[256,512]{1,0:T(8,128)(2,1)S(1)} collective-permute-done((bf16[256,512]{1,0:T(8,128)(2,1)S(1)}, bf16[256,512]{1,0:T(8,128)(2,1)S(1)}, u32[]{:S(2)}, u32[]{:S(2)}) %collective-permute-start.14) | collective-permute-done | bytes 262176 | tf_op jit(solution)/shard_map/ppermute | solution.py:34
  108.4 2.5 %collective-permute-start.15 = (bf16[64,4096]{1,0:T(8,128)(2,1)}, bf16[64,4096]{1,0:T(8,128)(2,1)}, u32[]{:S(2)}, u32[]{:S(2)}) collective-permute-start(bf16[64,4096]{1,0:T(8,128)(2,1)} %get-tuple-element.45), channel_id=1, source_target_pairs={{0,16},{16,0},{1,17},{17,1},{2,18},{18,2},{3,19},{19,3},{4,20},{20... | collective-permute-start | bytes 1572872 | tf_op jit(solution)/shard_map/ppermute | solution.py:34
  112.4 4.9 %shard_map.136 = (bf16[512,512]{1,0:T(8,128)(2,1)}, f32[16,1,1024]{2,1,0:T(1,128)}, bf16[16,16,512]{2,1,0:T(8,128)(2,1)}) custom-call(s32[16]{0:T(128)} %copy-done.20, s32[16]{0:T(128)} %slice_bitcast_fusion.holder_ref, f32[256,512]{1,0:T(8,128)} %get-tuple-element.66.refs_0_, f32[256,512]{1,0:T(8,128)} %get-tuple-element.68.refs_1_, ...), custom_call_target="tpu_custom_call" | custom-call | tf_op jit(solution)/shard_map/pallas_call | solution.py:99
  117.3 5.8 %all-to-all-start.1 = ((f32[16,1,1024]{2,1,0:T(1,128)}), f32[16,1,1024]{2,1,0:T(1,128)S(1)}, u32[]{:S(2)}, u32[]{:S(2)}) async-start(f32[16,1,1024]{2,1,0:T(1,128)} %get-tuple-element.50), calls=%async_computation.1 | async-start | bytes 131072 | tf_op jit(solution)/shard_map/all_to_all | solution.py:598
  123.1 3.2 %fusion.5.refs_0_ = f32[128,512]{1,0:T(8,128)S(1)} fusion(bf16[4096,512]{1,0:T(8,128)(2,1)} %param.19, bf16[64,4096]{1,0:T(8,128)(2,1)} %collective-permute-done.4, bf16[64,4096]{1,0:T(8,128)(2,1)} %get-tuple-element.36), kind=kOutput, calls=%fused_computation.9 | convolution fusion | flops 538968064 | bytes 5505024 | tf_op jit(solution)/shard_map/dot_general | solution.py:29
  126.3 2.1 %collective-permute-start.16 = (bf16[64,512]{1,0:T(8,128)(2,1)S(1)}, bf16[64,512]{1,0:T(8,128)(2,1)S(1)}, u32[]{:S(2)}, u32[]{:S(2)}) collective-permute-start(bf16[64,512]{1,0:T(8,128)(2,1)S(1)} %slice.115), channel_id=1, source_target_pairs={{0,16},{16,0},{1,17},{17,1},{2,18},{18,2},{3,19},{19,3},{4,20},{20... | collective-permute-start | bytes 196616 | tf_op jit(solution)/shard_map/ppermute | solution.py:34
  128.4 2.5 %slice.92 = bf16[256,2560]{1,0:T(8,128)(2,1)} slice(bf16[256,3072]{1,0:T(8,128)(2,1)} %pad_maximum_fusion), slice={[0:256], [0:2560]} | slice | bytes 2621440 | tf_op jit(solution)/shard_map/slice | solution.py:591
  130.9 2.5 %slice.93 = bf16[256,2560]{1,0:T(8,128)(2,1)} slice(bf16[256,3072]{1,0:T(8,128)(2,1)} %collective-permute-done.13), slice={[0:256], [0:2560]} | slice | bytes 2621440 | tf_op jit(solution)/shard_map/slice | solution.py:591
  133.3 6.0 %all-to-all-start = ((bf16[16,16,512]{2,1,0:T(8,128)(2,1)}), bf16[16,16,512]{2,1,0:T(8,128)(2,1)S(1)}, u32[]{:S(2)}, u32[]{:S(2)}) async-start(bf16[16,16,512]{2,1,0:T(8,128)(2,1)} %get-tuple-element.49), calls=%async_computation | async-start | bytes 524288 | tf_op jit(solution)/shard_map/all_to_all | solution.py:600
  139.4 1.7 %shard_map.137 = (f32[8,512]{1,0:T(8,128)}, f32[512,8]{1,0:T(8,128)}) custom-call(s32[16]{0:T(128)} %copy-done.20, f32[16,1,1024]{2,1,0:T(1,128)} %copy-done.13), custom_call_target="tpu_custom_call" | custom-call | tf_op jit(solution)/shard_map/pallas_call | solution.py:99
  142.5 3.4 %fusion.9.refs_1_ = f32[128,512]{1,0:T(8,128)S(1)} fusion(bf16[4096,512]{1,0:T(8,128)(2,1)} %param.19, bf16[64,4096]{1,0:T(8,128)(2,1)} %collective-permute-done.15, bf16[64,4096]{1,0:T(8,128)(2,1)} %get-tuple-element.44), kind=kOutput, calls=%fused_computation.13 | convolution fusion | flops 538968064 | bytes 5505024 | tf_op jit(solution)/shard_map/dot_general | solution.py:29
  146.2 4.1 %fusion = f32[2560,512]{1,0:T(8,128)} fusion(bf16[256,2560]{1,0:T(8,128)(2,1)S(1)} %copy-done.6, bf16[256,2560]{1,0:T(8,128)(2,1)S(1)} %copy-done.5, bf16[512,512]{1,0:T(8,128)(2,1)S(1)} %copy-done.22, f32[512,512]{1,0:T(8,128)S(1)} %copy-done.2, f32[512]{0:T(512)S(1)} %get-tuple-element.55, f32[512]{0:T(512)S(1)} %get-tuple-element.54), kind=kOutput, calls=%fused_computation | convolution fusion | flops 1348730880 | bytes 9441280 | tf_op jit(solution)/shard_map/dot_general | solution.py:605
  151.0 2.4 %shard_map.138 = bf16[128,512]{1,0:T(8,128)(2,1)} custom-call(s32[2]{0:T(128)} %pad_add_fusion.2.index_ref, s32[1,16,2]{2,1,0:T(8,128)} %copy.27.grid_ref, s32[1,16]{1,0:T(1,128)} %start_ref.3, f32[128,512]{1,0:T(8,128)} %copy-done.9, f32[128,512]{1,0:T(8,128)} %copy-done.10, bf16[64,512]{1,0:T(8,128)(2,1)} %copy-done.16, bf16[64,512]{1,0:T(8,128)(2,1)} %copy-done.17, ...), custom_call_target="tpu_custom_call" | custom-call | tf_op jit(solution)/shard_map/pallas_call | solution.py:99
  (117 shorter events, 36.3 us)
Async XLA Ops:
  0.6 88.2 %copy-start = (bf16[2560,512]{1,0:T(8,128)(2,1)S(1)}, bf16[2560,512]{1,0:T(8,128)(2,1)}, u32[]{:S(2)}) copy-start(bf16[2560,512]{1,0:T(8,128)(2,1)} %param.16) | copy-start | bytes 7864324
  0.6 16.3 %copy-start.19 = (s32[1,16,2]{1,2,0:T(2,128)S(1)}, s32[1,16,2]{1,2,0:T(2,128)}, u32[]{:S(2)}) copy-start(s32[1,16,2]{1,2,0:T(2,128)} %param.21) | copy-start | bytes 388
  1.5 14.6 %collective-permute-start = (s32[3,16]{1,0:T(4,128)S(1)}, s32[3,16]{1,0:T(4,128)S(1)}, u32[]{:S(2)}, u32[]{:S(2)}) collective-permute-start(s32[3,16]{1,0:T(4,128)S(1)} %get-tuple-element.64), channel_id=1, source_target_pairs={{0,16},{16,0},{1,17},{17,1},{2,18},{18,2},{3,19},{19,3},{4,20},{20... | collective-permute-start | bytes 584 | tf_op jit(solution)/shard_map/ppermute | solution.py:34
  5.6 5.7 %copy-start.4 = (bf16[64,1280]{1,0:T(8,128)(2,1)}, bf16[64,1280]{1,0:T(8,128)(2,1)S(1)}, u32[]{:S(2)}) copy-start(bf16[64,1280]{1,0:T(8,128)(2,1)S(1)} %convolution_convert_fusion.refs_0_.refs_2_) | copy-start | bytes 491524
  5.7 5.7 %collective-permute-start.1 = (bf16[64,1280]{1,0:T(8,128)(2,1)S(1)}, bf16[64,1280]{1,0:T(8,128)(2,1)S(1)}, u32[]{:S(2)}, u32[]{:S(2)}) collective-permute-start(bf16[64,1280]{1,0:T(8,128)(2,1)S(1)} %convolution_convert_fusion.refs_0_.refs_2_), channel_id=1, source_target_pairs={{0,16},{16,0},{1,17},{17,1},{2,18},{18,2},{3,19},{19,3},{4,20},{20... | collective-permute-start | bytes 491528 | tf_op jit(solution)/shard_map/ppermute | solution.py:34
  15.8 7.1 %collective-permute-start.2 = (bf16[2,64,960]{2,1,0:T(8,128)(2,1)}, bf16[2,64,960]{2,1,0:T(8,128)(2,1)S(1)}, u32[]{:S(2)}, u32[]{:S(2)}) collective-permute-start(bf16[2,64,960]{2,1,0:T(8,128)(2,1)} %bitcast.48), channel_id=1, source_target_pairs={{0,16},{16,0},{1,17},{17,1},{2,18},{18,2},{3,19},{19,3},{4,20},{20... | collective-permute-start | bytes 737288 | tf_op jit(solution)/shard_map/ppermute | solution.py:34
  16.3 22.7 %copy-start.21 = (s32[2]{0:T(128)}, s32[2]{0:T(128)S(1)}, u32[]{:S(2)}) copy-start(s32[2]{0:T(128)S(1)} %select_reduce_fusion.count_ref) | copy-start | bytes 28
  27.2 11.8 %collective-permute-start.3 = (bf16[2,32,1280]{2,1,0:T(8,128)(2,1)}, bf16[2,32,1280]{2,1,0:T(8,128)(2,1)S(1)}, u32[]{:S(2)}, u32[]{:S(2)}) collective-permute-start(bf16[2,32,1280]{2,1,0:T(8,128)(2,1)} %bitcast.49), channel_id=1, source_target_pairs={{0,16},{16,0},{1,17},{17,1},{2,18},{18,2},{3,19},{19,3},{4,20},{20... | collective-permute-start | bytes 491528 | tf_op jit(solution)/shard_map/ppermute | solution.py:34
  31.4 6.2 %collective-permute-start.5 = (bf16[16,512]{1,0:T(8,128)(2,1)}, bf16[16,512]{1,0:T(8,128)(2,1)S(1)}, u32[]{:S(2)}, u32[]{:S(2)}) collective-permute-start(bf16[16,512]{1,0:T(8,128)(2,1)} %shard_map.134), channel_id=1, source_target_pairs={{0,16},{16,0},{1,17},{17,1},{2,18},{18,2},{3,19},{19,3},{4,20},{20... | collective-permute-start | bytes 49160 | tf_op jit(solution)/shard_map/ppermute | solution.py:34
  42.5 5.7 %collective-permute-start.6 = (bf16[32,1536]{1,0:T(8,128)(2,1)S(1)}, bf16[32,1536]{1,0:T(8,128)(2,1)S(1)}, u32[]{:S(2)}, u32[]{:S(2)}) collective-permute-start(bf16[32,1536]{1,0:T(8,128)(2,1)S(1)} %get-tuple-element.56), channel_id=1, source_target_pairs={{0,8},{1,9},{2,10},{3,11},{4,12},{5,13},{6,14},{7,15},{8,0},{9,1},... | collective-permute-start | bytes 294920 | tf_op jit(solution)/shard_map/ppermute | solution.py:52
  45.2 4.8 %collective-permute-start.9 = (bf16[32,1536]{1,0:T(8,128)(2,1)S(1)}, bf16[32,1536]{1,0:T(8,128)(2,1)S(1)}, u32[]{:S(2)}, u32[]{:S(2)}) collective-permute-start(bf16[32,1536]{1,0:T(8,128)(2,1)S(1)} %get-tuple-element.58), channel_id=1, source_target_pairs={{0,2},{1,3},{2,0},{3,1},{4,6},{5,7},{6,4},{7,5},{8,10},{9,11},{10,... | collective-permute-start | bytes 294920 | tf_op jit(solution)/shard_map/ppermute | solution.py:52
  48.2 5.9 %collective-permute-start.7 = (bf16[64,1536]{1,0:T(8,128)(2,1)S(1)}, bf16[64,1536]{1,0:T(8,128)(2,1)S(1)}, u32[]{:S(2)}, u32[]{:S(2)}) collective-permute-start(bf16[64,1536]{1,0:T(8,128)(2,1)S(1)} %pad_maximum_fusion.4), channel_id=1, source_target_pairs={{0,4},{1,5},{2,6},{3,7},{4,0},{5,1},{6,2},{7,3},{8,12},{9,13},{10,... | collective-permute-start | bytes 589832 | tf_op jit(solution)/shard_map/ppermute | solution.py:52
  50.0 9.0 %collective-permute-start.10 = (bf16[64,1536]{1,0:T(8,128)(2,1)S(1)}, bf16[64,1536]{1,0:T(8,128)(2,1)S(1)}, u32[]{:S(2)}, u32[]{:S(2)}) collective-permute-start(bf16[64,1536]{1,0:T(8,128)(2,1)S(1)} %pad_maximum_fusion.5), channel_id=1, source_target_pairs={{0,8},{1,9},{2,10},{3,11},{4,12},{5,13},{6,14},{7,15},{8,0},{9,1},... | collective-permute-start | bytes 589832 | tf_op jit(solution)/shard_map/ppermute | solution.py:52
  54.2 16.5 %copy-start.23 = (s32[16]{0:T(128)S(1)}, s32[16]{0:T(128)}, u32[]{:S(2)}) copy-start(s32[16]{0:T(128)} %constant.108.clone) | copy-start | bytes 196
  54.2 12.8 %collective-permute-start.8 = (bf16[128,1536]{1,0:T(8,128)(2,1)S(1)}, bf16[128,1536]{1,0:T(8,128)(2,1)S(1)}, u32[]{:S(2)}, u32[]{:S(2)}) collective-permute-start(bf16[128,1536]{1,0:T(8,128)(2,1)S(1)} %pad_maximum_fusion.2), channel_id=1, source_target_pairs={{0,2},{1,3},{2,0},{3,1},{4,6},{5,7},{6,4},{7,5},{8,10},{9,11},{10,... | collective-permute-start | bytes 1179656 | tf_op jit(solution)/shard_map/ppermute | solution.py:52
  59.0 7.8 %collective-permute-start.11 = (bf16[128,1536]{1,0:T(8,128)(2,1)S(1)}, bf16[128,1536]{1,0:T(8,128)(2,1)S(1)}, u32[]{:S(2)}, u32[]{:S(2)}) collective-permute-start(bf16[128,1536]{1,0:T(8,128)(2,1)S(1)} %pad_maximum_fusion.3), channel_id=1, source_target_pairs={{0,4},{1,5},{2,6},{3,7},{4,0},{5,1},{6,2},{7,3},{8,12},{9,13},{10,... | collective-permute-start | bytes 1179656 | tf_op jit(solution)/shard_map/ppermute | solution.py:52
  69.2 25.1 %collective-permute-start.13 = (bf16[256,3072]{1,0:T(8,128)(2,1)}, bf16[256,3072]{1,0:T(8,128)(2,1)}, u32[]{:S(2)}, u32[]{:S(2)}) collective-permute-start(bf16[256,3072]{1,0:T(8,128)(2,1)} %pad_maximum_fusion), channel_id=1, source_target_pairs={{0,1},{1,0},{2,3},{3,2},{4,5},{5,4},{6,7},{7,6},{8,9},{9,8},{10,11... | collective-permute-start | bytes 4718600 | tf_op jit(solution)/shard_map/ppermute | solution.py:76
  70.6 40.3 %copy-start.18 = (f32[512]{0:T(512)}, f32[512]{0:T(512)S(1)}, u32[]{:S(2)}) copy-start(f32[512]{0:T(512)S(1)} %dynamic_slice.7) | copy-start | bytes 6148
  70.6 27.7 %copy-start.20 = (s32[16]{0:T(128)}, s32[16]{0:T(128)S(1)}, u32[]{:S(2)}) copy-start(s32[16]{0:T(128)S(1)} %broadcast_xor_fusion.owner_ref) | copy-start | bytes 196
  71.7 14.7 %collective-permute-start.18 = (bf16[512,512]{1,0:T(8,128)(2,1)S(1)}, bf16[512,512]{1,0:T(8,128)(2,1)S(1)}, u32[]{:S(2)}, u32[]{:S(2)}) collective-permute-start(bf16[512,512]{1,0:T(8,128)(2,1)S(1)} %constant_dynamic-slice_fusion), channel_id=1, source_target_pairs={{0,16},{1,17},{2,18},{3,19},{4,20},{5,21},{6,22},{7,23},{24,8},{25... | collective-permute-start | bytes 1572872 | tf_op jit(solution)/shard_map/ppermute | solution.py:563
  74.9 48.1 %collective-permute-start.4 = (bf16[64,4096]{1,0:T(8,128)(2,1)}, bf16[64,4096]{1,0:T(8,128)(2,1)}, u32[]{:S(2)}, u32[]{:S(2)}) collective-permute-start(bf16[64,4096]{1,0:T(8,128)(2,1)} %get-tuple-element.37), channel_id=1, source_target_pairs={{0,16},{16,0},{1,17},{17,1},{2,18},{18,2},{3,19},{19,3},{4,20},{20... | collective-permute-start | bytes 1572872 | tf_op jit(solution)/shard_map/ppermute | solution.py:34
  87.6 23.3 %copy-start.1 = (bf16[512,512]{1,0:T(8,128)(2,1)}, bf16[512,512]{1,0:T(8,128)(2,1)S(1)}, u32[]{:S(2)}) copy-start(bf16[512,512]{1,0:T(8,128)(2,1)S(1)} %select_add_fusion.refs_6_) | copy-start | bytes 1572868
  91.8 11.5 %collective-permute-start.12 = (bf16[256,512]{1,0:T(8,128)(2,1)S(1)}, bf16[256,512]{1,0:T(8,128)(2,1)S(1)}, u32[]{:S(2)}, u32[]{:S(2)}) collective-permute-start(bf16[256,512]{1,0:T(8,128)(2,1)S(1)} %get-tuple-element.65), channel_id=1, source_target_pairs={{0,16},{16,0},{1,17},{17,1},{2,18},{18,2},{3,19},{19,3},{4,20},{20... | collective-permute-start | bytes 786440 | tf_op jit(solution)/shard_map/ppermute | solution.py:34
  97.3 11.2 %collective-permute-start.14 = (bf16[256,512]{1,0:T(8,128)(2,1)S(1)}, bf16[256,512]{1,0:T(8,128)(2,1)S(1)}, u32[]{:S(2)}, u32[]{:S(2)}) collective-permute-start(bf16[256,512]{1,0:T(8,128)(2,1)S(1)} %get-tuple-element.67), channel_id=1, source_target_pairs={{0,16},{16,0},{1,17},{17,1},{2,18},{18,2},{3,19},{19,3},{4,20},{20... | collective-permute-start | bytes 786440 | tf_op jit(solution)/shard_map/ppermute | solution.py:34
  103.3 9.1 %copy-start.11 = (bf16[256,512]{1,0:T(8,128)(2,1)}, bf16[256,512]{1,0:T(8,128)(2,1)S(1)}, u32[]{:S(2)}) copy-start(bf16[256,512]{1,0:T(8,128)(2,1)S(1)} %collective-permute-done.12.refs_2_) | copy-start | bytes 786436
  108.4 34.1 %collective-permute-start.15 = (bf16[64,4096]{1,0:T(8,128)(2,1)}, bf16[64,4096]{1,0:T(8,128)(2,1)}, u32[]{:S(2)}, u32[]{:S(2)}) collective-permute-start(bf16[64,4096]{1,0:T(8,128)(2,1)} %get-tuple-element.45), channel_id=1, source_target_pairs={{0,16},{16,0},{1,17},{17,1},{2,18},{18,2},{3,19},{19,3},{4,20},{20... | collective-permute-start | bytes 1572872 | tf_op jit(solution)/shard_map/ppermute | solution.py:34
  117.3 16.1 %all-to-all-start.1 = ((f32[16,1,1024]{2,1,0:T(1,128)}), f32[16,1,1024]{2,1,0:T(1,128)S(1)}, u32[]{:S(2)}, u32[]{:S(2)}) async-start(f32[16,1,1024]{2,1,0:T(1,128)} %get-tuple-element.50), calls=%async_computation.1 | async-start | bytes 131072 | tf_op jit(solution)/shard_map/all_to_all | solution.py:598
  126.3 7.0 %copy-start.9 = (f32[128,512]{1,0:T(8,128)}, f32[128,512]{1,0:T(8,128)S(1)}, u32[]{:S(2)}) copy-start(f32[128,512]{1,0:T(8,128)S(1)} %fusion.5.refs_0_) | copy-start | bytes 786436
  126.3 23.9 %collective-permute-start.16 = (bf16[64,512]{1,0:T(8,128)(2,1)S(1)}, bf16[64,512]{1,0:T(8,128)(2,1)S(1)}, u32[]{:S(2)}, u32[]{:S(2)}) collective-permute-start(bf16[64,512]{1,0:T(8,128)(2,1)S(1)} %slice.115), channel_id=1, source_target_pairs={{0,16},{16,0},{1,17},{17,1},{2,18},{18,2},{3,19},{19,3},{4,20},{20... | collective-permute-start | bytes 196616 | tf_op jit(solution)/shard_map/ppermute | solution.py:34
  133.3 6.0 %copy-start.13 = (f32[16,1,1024]{2,1,0:T(1,128)}, f32[16,1,1024]{2,1,0:T(1,128)S(1)}, u32[]{:S(2)}) copy-start(f32[16,1,1024]{2,1,0:T(1,128)S(1)} %all-to-all-done.1.sums_ref) | copy-start | bytes 196612
  133.3 16.9 %all-to-all-start = ((bf16[16,16,512]{2,1,0:T(8,128)(2,1)}), bf16[16,16,512]{2,1,0:T(8,128)(2,1)S(1)}, u32[]{:S(2)}, u32[]{:S(2)}) async-start(bf16[16,16,512]{2,1,0:T(8,128)(2,1)} %get-tuple-element.49), calls=%async_computation | async-start | bytes 524288 | tf_op jit(solution)/shard_map/all_to_all | solution.py:600
  145.9 4.5 %collective-permute-start.17 = (bf16[64,512]{1,0:T(8,128)(2,1)S(1)}, bf16[64,512]{1,0:T(8,128)(2,1)S(1)}, u32[]{:S(2)}, u32[]{:S(2)}) collective-permute-start(bf16[64,512]{1,0:T(8,128)(2,1)S(1)} %slice.114), channel_id=1, source_target_pairs={{0,16},{16,0},{1,17},{17,1},{2,18},{18,2},{3,19},{19,3},{4,20},{20... | collective-permute-start | bytes 196616 | tf_op jit(solution)/shard_map/ppermute | solution.py:34
  (13 other events, 27.5 us)

commit v5 on v4

--- a/solution.py
+++ b/solution.py
@@ -54,28 +54,31 @@
     return pieces, offsets
 
 
-def gather_halves(x):
+def gather_halves(left, right, main):
     size = lax.axis_size("ctx")
     own = lax.axis_index("ctx")
+    middle, rows = left.shape[1], left.shape[0]
     if size & (size - 1) or size < 8:
-        return [lax.all_gather(x, "ctx", axis=0, tiled=True)], jnp.arange(size, dtype=jnp.int32)
+        x = jnp.concatenate([left, right], axis=1)
+        x = lax.all_gather(x, "ctx", axis=0, tiled=True)
+        return [x[:, :main]], [x[:, main:]], jnp.arange(size, dtype=jnp.int32)
     strides = strides_of(size)
-    middle = x.shape[1] // 2
-    left, offsets = xor_gather(x[:, :middle], strides[:-1])
-    right, others = xor_gather(x[:, middle:], strides[-2:-1] + strides[:-2])
+    lefts, offsets = xor_gather(left, strides[:-1])
+    rights, others = xor_gather(right, strides[-2:-1] + strides[:-2])
     order = [o for piece in offsets for o in piece]
-    rows = x.shape[0]
     found = {
         o: piece[j * rows : (j + 1) * rows]
-        for piece, known in zip(right, others)
+        for piece, known in zip(rights, others)
         for j, o in enumerate(known)
     }
-    low = jnp.concatenate(
-        [jnp.concatenate(left, axis=0), jnp.concatenate([found[o] for o in order], axis=0)], axis=1
-    )
-    high = lax.ppermute(low, "ctx", [(i, i ^ 1) for i in range(size)])
+    rights = jnp.concatenate([found[o] for o in order], axis=0)
+    low = jnp.concatenate([jnp.concatenate(lefts, axis=0), rights[:, : main - middle]], axis=1)
+    rest = rights[:, main - middle :]
+    pairs = [(i, i ^ 1) for i in range(size)]
+    lows = [low, lax.ppermute(low, "ctx", pairs)]
+    rests = [rest, lax.ppermute(rest, "ctx", pairs)]
     order = order + [o ^ 1 for o in order]
-    return [low, high], own ^ jnp.asarray(order, jnp.int32)
+    return lows, rests, own ^ jnp.asarray(order, jnp.int32)
 
 
 def find_image(own, tokens, grid_ref, start_ref, groups):
@@ -225,12 +228,13 @@
     key_width = key_rows.shape[1]
     chunks = len(own_parts)
     per_chunk = groups // chunks
+    sum_rows = -(-6 * (total // key_width) // 8) * 8
     flat = [r for group in received for r in group]
 
     def kernel(owner_ref, holder_ref, *refs):
         part_refs = refs[:chunks]
         received_refs = refs[chunks : chunks + len(flat)]
-        weighted_ref, gain_ref, key_ref, embed_ref, sums_ref, keys_ref, squared, multiplied = refs[
+        weighted_ref, gain_ref, key_ref, embed_ref, keys_ref, squared, multiplied = refs[
             chunks + len(flat) :
         ]
         picked = []
@@ -264,19 +268,24 @@
             )[0:1]
             for ref in (squared, multiplied)
         ]
-        for i in range(groups):
-            sums_ref[i, :, 0:total] = both[0]
-            sums_ref[i, :, total : 2 * total] = both[1]
+        lines = []
+        for _ in range(3):
+            rounded = [v.astype(BF16).astype(F32) for v in both]
+            both = [v - w for v, w in zip(both, rounded)]
+            for v in rounded:
+                lines += [v[:, j : j + key_width] for j in range(0, total, key_width)]
+        lines += [jnp.zeros_like(lines[0])] * (sum_rows - len(lines))
+        lines = jnp.concatenate(lines, axis=0).astype(BF16)
         terms = dot(jnp.concatenate(picked, axis=0), key_ref[...]).astype(BF16)
         for i in range(groups):
-            keys_ref[holder_ref[i]] = terms[i * capacity : (i + 1) * capacity]
+            keys_ref[holder_ref[i], 0:capacity] = terms[i * capacity : (i + 1) * capacity]
+            keys_ref[i, capacity:] = lines
 
     return call(
         kernel,
         (
             jax.ShapeDtypeStruct((total, columns), BF16),
-            jax.ShapeDtypeStruct((groups, 1, 2 * total), F32),
-            jax.ShapeDtypeStruct((groups, capacity, key_width), BF16),
+            jax.ShapeDtypeStruct((groups, capacity + sum_rows, key_width), BF16),
         ),
         (owners, holders, *own_parts, *flat, weighted, gain, key_rows),
         scalars=2,
@@ -284,14 +293,23 @@
     )
 
 
-def norm_scales(groups, width, owners, sums):
-    total = sums.shape[2] // 2
-    rows = total // groups
+def norm_scales(parts, groups, width, owners, arrived, capacity):
+    rows = parts * capacity
+    total = groups * rows
+    lines = total // arrived.shape[2]
 
     def kernel(owner_ref, sums_ref, scale_ref, columns_ref, turned):
-        whole = jnp.sum(sums_ref[...], axis=0)
-        scale = lax.rsqrt(whole[:, :total] / width + EPS)
-        slope = scale**3 * whole[:, total:] / width
+        summed = jnp.sum(sums_ref[:, capacity:, :].astype(F32), axis=0)
+
+        def whole(q):
+            pieces = []
+            for j in range(lines):
+                at = [(2 * p + q) * lines + j for p in range(3)]
+                pieces.append(sum(summed[r : r + 1] for r in at))
+            return jnp.concatenate(pieces, axis=1)
+
+        scale = lax.rsqrt(whole(0) / width + EPS)
+        slope = scale**3 * whole(1) / width
         line = lax.broadcasted_iota(jnp.int32, (8, total), 0)
         both = jnp.where(line == 0, scale, slope)
         scale_ref[...] = both
@@ -304,37 +322,53 @@
     return call(
         kernel,
         (jax.ShapeDtypeStruct((8, total), F32), jax.ShapeDtypeStruct((total, 8), F32)),
-        (owners, sums),
+        (owners, arrived),
         scalars=1,
         scratch=[pltpu.VMEM((total, 8), F32)],
     )
 
 
-def merge(parts, places, counts, hidden, received, extra):
+def merge(parts, places, counts, hidden, received, extras):
     taken, width = hidden.shape[1:]
     capacity = taken // places
     main = places * width
+    middle = (main + extras[0].shape[1]) // 256 * 128
+    rest = main + extras[0].shape[1] - middle
+    count = len(received)
 
     def kernel(count_ref, *refs):
-        hidden_ref, received_refs, extra_ref, out_ref = refs[0], refs[1:-2], refs[-2], refs[-1]
+        hidden_ref, received_refs = refs[0], refs[1 : 1 + count]
+        extra_refs, left_ref, right_ref = refs[1 + count : -2], refs[-2], refs[-1]
+
+        def put(rows, column, values):
+            split = min(max(middle - column, 0), values.shape[1])
+            if split:
+                left_ref[rows, column : column + split] = values[:, :split]
+            if split < values.shape[1]:
+                begin = column + split - middle
+                right_ref[rows, begin : begin + values.shape[1] - split] = values[:, split:]
+
         slot = lax.broadcasted_iota(jnp.int32, (capacity, width), 0)
         for r in range(parts):
+            rows = pl.ds(r * capacity, capacity)
             total = hidden_ref[r]
             for ref in received_refs:
                 total = total + ref[r].astype(F32)
             normed = layer_norm(total).astype(BF16)
             for p in range(places):
                 kept = normed[p * capacity : (p + 1) * capacity]
-                kept = jnp.where(slot < count_ref[r], kept, jnp.zeros_like(kept))
-                out_ref[r * capacity : (r + 1) * capacity, p * width : (p + 1) * width] = kept
-        out_ref[:, main:] = extra_ref[...]
-
-    return call(
-        kernel,
-        (jax.ShapeDtypeStruct((parts * capacity, main + extra.shape[1]), BF16),),
-        (counts, hidden, *received, extra),
+                put(rows, p * width, jnp.where(slot < count_ref[r], kept, jnp.zeros_like(kept)))
+            put(rows, main, extra_refs[r][...])
+
+    return call(
+        kernel,
+        (
+            jax.ShapeDtypeStruct((parts * capacity, middle), BF16),
+            jax.ShapeDtypeStruct((parts * capacity, rest), BF16),
+        ),
+        (counts, hidden, *received, *extras),
         scalars=1,
-    )[0]
+    )
 
 
 def angle_table(tokens, groups, capacity, index, grid, start):
@@ -401,11 +435,11 @@
 
 
 def keys_out(parts, groups, index, grid, start, text_keys, returned, arrived, scales, cosine, sines):
-    tokens, width = returned[0][0].shape[0] * len(returned), text_keys[0].shape[1]
-    capacity = arrived.shape[1]
+    tokens, width = cosine.shape[0], text_keys[0].shape[1]
     total = scales.shape[1]
+    capacity = total // (parts * groups)
     chunks = len(text_keys)
-    chunk = tokens // chunks
+    sizes = [t.shape[0] // parts for t in text_keys]
     flat = [r for group in returned for r in group]
 
     def kernel(index_ref, grid_ref, start_ref, *refs):
@@ -419,7 +453,7 @@
         slot = lax.broadcasted_iota(jnp.int32, shape, 0)
         wanted = lane == owner * (parts * capacity) + slot
         scale = jnp.sum(jnp.where(wanted, scale_ref[0:1, :], 0.0), axis=-1, keepdims=True)
-        image = jnp.sum(arrived_ref[...].astype(F32), axis=0) * scale
+        image = jnp.sum(arrived_ref[:, 0:capacity, :].astype(F32), axis=0) * scale
         chosen = place_rows(tokens, own, first, count, (tokens, capacity), 0)
         placed = dot(chosen, image, precision=HIGHEST)
         token = lax.broadcasted_iota(jnp.int32, (tokens, width), 0) + own * tokens
@@ -428,7 +462,7 @@
         signed = jnp.where(lane < HD // 2, -sine_ref[...], sine_ref[...])
         rows = []
         for j in range(chunks):
-            part = text_refs[j][0:chunk, :]
+            part = text_refs[j][0 : sizes[j], :]
             for k in range(parts - 1):
                 part = part + returned_refs[j * (parts - 1) + k][...].astype(F32)
             rows.append(part)
@@ -443,44 +477,46 @@
     )[0]
 
 
-def text_norm(parts, chunks, index, text, gain):
+def text_norm(parts, sizes, index, text, gain):
     tokens, width = text.shape
-    step = 32 if tokens // chunks % 32 == 0 else tokens // chunks
+    step = math.gcd(32, *sizes)
     block = width // parts
-    steps = tokens // chunks // step
+    steps = [size // step for size in sizes]
+    begins = [sum(steps[:j]) for j in range(len(steps))]
 
     def kernel(index_ref, text_ref, gain_ref, *refs):
         out_refs, scratch = refs[:-1], refs[-1]
         values = text_ref[...].astype(F32)
         scale = lax.rsqrt(jnp.mean(values * values, axis=-1, keepdims=True) + EPS)
         scratch[...] = (values * scale * gain_ref[...]).astype(BF16)
-        for j in range(chunks):
-
-            @pl.when(pl.program_id(0) // steps == j)
+        now = pl.program_id(0)
+        for j in range(len(sizes)):
+
+            @pl.when((now >= begins[j]) & (now < begins[j] + steps[j]))
             def _():
                 for k in range(parts):
                     start = pl.multiple_of((index_ref[0] + k) % parts * block, block)
                     out_refs[j * parts + k][...] = scratch[:, pl.ds(start, block)]
 
     def place(j):
-        return lambda g: (jnp.clip(g - j * steps, 0, steps - 1), 0)
+        return lambda g: (jnp.clip(g - begins[j], 0, steps[j] - 1), 0)
 
     flat = pl.pallas_call(
         kernel,
         grid=(tokens // step,),
-        out_shape=[jax.ShapeDtypeStruct((tokens // chunks, block), BF16)] * (chunks * parts),
+        out_shape=[jax.ShapeDtypeStruct((size, block), BF16) for size in sizes for _ in range(parts)],
         in_specs=[
             SMEM,
             pl.BlockSpec((step, width), lambda g: (g, 0)),
             pl.BlockSpec((1, width), lambda g: (0, 0)),
         ],
         out_specs=[
-            pl.BlockSpec((step, block), place(j)) for j in range(chunks) for _ in range(parts)
+            pl.BlockSpec((step, block), place(j)) for j in range(len(sizes)) for _ in range(parts)
         ],
         scratch_shapes=[pltpu.VMEM((step, width), BF16)],
         name="text_norm",
     )(index, text, gain)
-    return [flat[j * parts : (j + 1) * parts] for j in range(chunks)]
+    return [flat[j * parts : (j + 1) * parts] for j in range(len(sizes))]
 
 
 def on_device(
@@ -521,8 +557,8 @@
     group_index = jnp.arange(groups, dtype=jnp.int32)
     own_counts = jnp.sum(jnp.where(group_index[None] == own, counts, 0), axis=1)
 
-    chunks = 2
-    text_blocks = text_norm(parts, chunks, index, text_embed[0], gain_line)
+    sizes = [tokens - tokens // 4, tokens // 4]
+    text_blocks = text_norm(parts, sizes, index, text_embed[0], gain_line)
 
     mine, sent = project(parts, index, images, vit_norm_gain.reshape(1, -1), vit_qkv)
 
@@ -533,7 +569,7 @@
     grads = image_grads(
         tokens, groups, capacity, index, grid, start, key_cotangent[0], cosine, sines
     )
-    grads = jnp.concatenate(gather_dp(grads), axis=0)
+    grads = gather_dp(grads)
 
     places = max(1, 4 // parts)
     pieces = max(1, parts // 4)
@@ -541,19 +577,22 @@
     scalars = jnp.concatenate([index[:1], own_counts])
     hidden_rows, sent = attend(parts, places, scalars, mine, received, images, vit_out)
     received = [shift(sent[k - 1], k) for k in others]
-    received, text_blocks, key_source = barrier((received, text_blocks, key_weight))
-    merged = merge(parts, places, own_counts, hidden_rows, received, grads)
+    received, text_blocks = barrier((received, text_blocks))
+    left, right = merge(parts, places, own_counts, hidden_rows, received, grads)
+    main = places * piece_width
     if pieces > 1:
-        taken = lax.dynamic_slice_in_dim(merged, (own_part % pieces) * piece_width, piece_width, 1)
-        merged = jnp.concatenate([taken, grads], axis=1)
-    merged_all, owners = gather_halves(merged)
-    main = places * piece_width
-    grads = jnp.concatenate([rows[:, main:] for rows in merged_all], axis=0)
+        merged = jnp.concatenate([left, right], axis=1)
+        begin = (own_part % pieces) * piece_width
+        taken = lax.dynamic_slice_in_dim(merged[:, :vit_width], begin, piece_width, 1)
+        merged = jnp.concatenate([taken, merged[:, vit_width:]], axis=1)
+        middle = min(merged.shape[1] // 2, main)
+        left, right = merged[:, :middle], merged[:, middle:]
+    merged_all, grads, owners = gather_halves(left, right, main)
 
     part_features = width // parts
     own_start = own * feature_cols
     holder_part = own_start // part_features
-    candidate = lax.dynamic_slice_in_dim(key_source, own_start % part_features, feature_cols, 0)
+    candidate = lax.dynamic_slice_in_dim(key_weight, own_start % part_features, feature_cols, 0)
     key_rows = jnp.where(own_part == holder_part, candidate, jnp.zeros_like(candidate))
     held_by = [g * feature_cols // part_features for g in range(groups)]
     for k in others:
@@ -573,7 +612,7 @@
 
     early_terms = text_terms(text_blocks[0])
 
-    grads = grads.reshape(groups, parts, capacity, key_width)
+    grads = jnp.concatenate(grads, axis=0).reshape(groups, parts, capacity, key_width)
     block_owner = (owners[:, None] == group_index[None, :]).astype(jnp.int32)
     block_range = jnp.sum(block_owner[None] * target_range[:, None, :], axis=-1)
     routing = (block_range[:, :, None] == owners[None, None, :]).astype(BF16)
@@ -588,18 +627,19 @@
         * own_gain
     )
 
-    embed_parts = [dot(rows[:, :main], merger) for rows in merged_all]
-    joined = jnp.concatenate([rows[:, :main] for rows in merged_all], axis=0)
+    embed_parts = [dot(rows, merger) for rows in merged_all]
+    joined = jnp.concatenate(merged_all, axis=0)
     received = [[shift(part.astype(BF16), k) for k in others] for part in embed_parts]
     received, late_blocks = barrier((received, text_blocks[1]))
-    embedded, sums, outgoing = features(
+    embedded, outgoing = features(
         parts, groups, owners, block_range[0], embed_parts, received, weighted, own_gain, key_rows
     )
-    sums = lax.all_to_all(sums, "ctx", 0, 0, tiled=True)
+    arrived = lax.all_to_all(outgoing, "ctx", 0, 0, tiled=True)
     late_terms = text_terms(late_blocks)
-    arrived = lax.all_to_all(outgoing, "ctx", 0, 0, tiled=True)
     returned = [text_return(early_terms), text_return(late_terms)]
-    scales, columns = norm_scales(groups, float(width), owners, sums)
+    scales, columns = norm_scales(
+        parts, groups, float(width), owners, arrived, capacity
+    )
     grad_embedded = columns[:, 0:1] * weighted - embedded.astype(F32) * columns[:, 1:2]
     grad_embedded = grad_embedded.astype(BF16)
     merger_grad = lax.dot_general(

time: 155 us -> 144 us (0.929)
  starting transfers between devices: 39.6 us -> 26.6 us
  local copies, waits for them, and re-layouts: 20.3 us -> 16.4 us
  waiting for transfers between devices: 39.3 us -> 43 us
  other arithmetic: 6.94 us -> 9.25 us
    ppermute x1, waiting for transfers between devices: 11.5 us -> 0.01 us  [on_device(): key_rows = key_rows + lax.ppermute(candidate, ('dp', 'ctx'), pairs)]
    ppermute x6, waiting for transfers between devices: 11.3 us -> 19.6 us  [xor_gather(): lax.ppermute(joined, 'ctx', [(i, i ^ stride) for i in range(size)])]
    ppermute x6, starting transfers between devices: 12.9 us -> 5.67 us  [xor_gather(): lax.ppermute(joined, 'ctx', [(i, i ^ stride) for i in range(size)])]
    slice x5 -> x2, local copies, waits for them, and re-layouts: 8.01 us -> 1.13 us  [the longest x1 1.08 us: gather_halves(): rest = rights[:, main - middle:]]
    ppermute x11, waiting for transfers between devices: 16.5 us -> 22.4 us  [shift(): return lax.ppermute(x, 'dp', [(i, (i + k) % size) for i in range(size)])]
    all_to_all x1 -> x0, starting transfers between devices: 5.77 us -> none  [on_device(): sums = lax.all_to_all(sums, 'ctx', 0, 0, tiled=True)]
    concatenate x4, other arithmetic: 0.08 us -> 3.76 us  [xor_gather(): joined = pieces[0] if len(pieces) == 1 else jnp.concatenate(pieces, axis=0)]
    all_to_all x1, starting transfers between devices: 6.02 us -> 3.73 us  [on_device(): arrived = lax.all_to_all(outgoing, 'ctx', 0, 0, tiled=True)]
  transfers between devices with their start and end apart: 21 -> 21, of which waited for: 10 -> 11; matrix products, arithmetic and copies ran while one was open for 26% -> 29% of each run, Pallas kernels for 12% -> 17%
where the time goes in v5:
time: 144 us; the launch traced here: 143 us
  waiting for transfers between devices  43 us (30%)
  Pallas kernels  26.8 us (19%)
  starting transfers between devices  26.6 us (18%)
  matrix products  19.8 us (14%)
  local copies, waits for them, and re-layouts  16.4 us (11%)
  other arithmetic  9.25 us (6%)
    ppermute x11, waiting for transfers between devices, shift(): return lax.ppermute(x, 'dp', [(i, (i + k) % size) for i in range(size)])  22.4 us
    pallas_call x8, Pallas kernels, call(): pl.pallas_call(kernel, out_shape=outs, in_specs=[SMEM] * scalars + [VMEM]...  22.1 us
    ppermute x6, waiting for transfers between devices, xor_gather(): lax.ppermute(joined, 'ctx', [(i, i ^ stride) for i in range(size)])  19.6 us
    ppermute x11, starting transfers between devices, shift(): return lax.ppermute(x, 'dp', [(i, (i + k) % size) for i in range(size)])  11.9 us
    dot_general x5, matrix products, dot(): return jnp.dot(a, b, preferred_element_type=F32, **kw)  11.9 us
    dot_general x1, matrix products, on_device(): lax.dot_general(joined, grad_embedded, (((0,), (0,)), ((), ())), preferre...  6.03 us
    ppermute x6, starting transfers between devices, xor_gather(): lax.ppermute(joined, 'ctx', [(i, i ^ stride) for i in range(size)])  5.67 us
    unnamed x54, local copies, waits for them, and re-layouts  5.36 us
  transfers between devices with their start and end apart: 21, of which 11 were waited for; matrix products, arithmetic and copies ran while one was open for 29% of the time, Pallas kernels for 17%

profile of v5, /device:TPU:0, one launch (start us, length us, event | category | flops | bytes accessed | tf_op | source)
XLA Modules:
  0.0 142.8 jit_solution(8491579458716487169)
XLA Ops:
  1.5 3.0 %collective-permute-start = (s32[3,16]{1,0:T(4,128)S(1)}, s32[3,16]{1,0:T(4,128)S(1)}, u32[]{:S(2)}, u32[]{:S(2)}) collective-permute-start(s32[3,16]{1,0:T(4,128)S(1)} %get-tuple-element.61), channel_id=1, source_target_pairs={{0,16},{16,0},{1,17},{17,1},{2,18},{18,2},{3,19},{19,3},{4,20},{20... | collective-permute-start | bytes 584 | tf_op jit(solution)/shard_map/ppermute | solution.py:34
  5.8 1.9 %constant_dynamic-slice_fusion = bf16[512,512]{1,0:T(8,128)(2,1)} fusion(bf16[4096,512]{1,0:T(8,128)(2,1)} %param.19, s32[]{:T(128)S(6)} %select_n.75), kind=kLoop, calls=%fused_computation.82 | loop fusion | bytes 1048580 | tf_op jit(solution)/shard_map/dynamic_slice | solution.py:595
  7.6 4.7 %collective-permute-start.19 = (bf16[512,512]{1,0:T(8,128)(2,1)}, bf16[512,512]{1,0:T(8,128)(2,1)}, u32[]{:S(2)}, u32[]{:S(2)}) collective-permute-start(bf16[512,512]{1,0:T(8,128)(2,1)} %constant_dynamic-slice_fusion), channel_id=1, source_target_pairs={{0,16},{1,17},{2,18},{3,19},{4,20},{5,21},{6,22},{7,23},{24,8},{25... | collective-permute-start | bytes 1572872 | tf_op jit(solution)/shard_map/ppermute | solution.py:602
  15.6 3.8 %shard_map.131 = (f32[2,64,960]{2,1,0:T(8,128)}, bf16[1,2,64,960]{3,2,1,0:T(8,128)(2,1)}) custom-call(s32[2]{0:T(128)} %pad_add_fusion.2.index_ref, bf16[64,1280]{1,0:T(8,128)(2,1)} %copy-done.4, bf16[64,1280]{1,0:T(8,128)(2,1)} %copy-done.10, f32[1,1280]{1,0:T(1,128)} %reshape.107.refs_2_, bf16[640,1920]{1,0:T(8,128)(2,1)} %refs_3_.1), custom_call_target="tpu_custom_call" | custom-call | tf_op jit(solution)/shard_map/pallas_call | solution.py:102
  20.7 1.6 %shard_map.133 = f32[128,128]{1,0:T(8,128)} custom-call(s32[2]{0:T(128)} %pad_add_fusion.2.index_ref, s32[1,16,2]{2,1,0:T(8,128)} %copy.24.grid_ref, s32[1,16]{1,0:T(1,128)} %start_ref.3, f32[1,128]{1,0:T(1,128)} %fusion.37.inverse_ref), custom_call_target="tpu_custom_call" | custom-call | tf_op jit(solution)/shard_map/pallas_call | solution.py:102
  22.3 1.7 %fusion.42 = (f32[128,128]{1,0:T(8,128)}, f32[128,128]{1,0:T(8,128)}) fusion(f32[128,128]{1,0:T(8,128)} %shard_map.133), kind=kLoop, calls=%fused_computation.88 | loop fusion | bytes 196608 | tf_op jit(solution)/shard_map/sin | solution.py:568
  24.0 1.9 %shard_map.134.refs_2_ = bf16[16,512]{1,0:T(8,128)(2,1)} custom-call(s32[2]{0:T(128)} %pad_add_fusion.2.index_ref, s32[1,16,2]{2,1,0:T(8,128)} %copy.24.grid_ref, s32[1,16]{1,0:T(1,128)} %start_ref.3, bf16[128,512]{1,0:T(8,128)(2,1)} %bitcast.43, f32[128,128]{1,0:T(8,128)} %get-tuple-element.57.cosine_ref.refs_6_, f32[128,128]{1,0:T(8,128)} %get-tuple-element.56.sine_ref.refs_7_), custom_call_target="tpu_custom_call" | custom-call | tf_op jit(solution)/shard_map/pallas_call | solution.py:102
  25.9 2.0 %collective-permute-start.5 = (bf16[16,512]{1,0:T(8,128)(2,1)}, bf16[16,512]{1,0:T(8,128)(2,1)S(1)}, u32[]{:S(2)}, u32[]{:S(2)}) collective-permute-start(bf16[16,512]{1,0:T(8,128)(2,1)} %shard_map.134.refs_2_), channel_id=1, source_target_pairs={{0,16},{16,0},{1,17},{17,1},{2,18},{18,2},{3,19},{19,3},{4,20},{20... | collective-permute-start | bytes 49160 | tf_op jit(solution)/shard_map/ppermute | solution.py:34
  29.0 3.5 %shard_map.132 = (f32[2,32,1280]{2,1,0:T(8,128)}, bf16[1,2,32,1280]{3,2,1,0:T(8,128)(2,1)}) custom-call(s32[3]{0:T(128)} %pad_add_fusion.3.scalar_ref, f32[2,64,960]{2,1,0:T(8,128)} %get-tuple-element.28.refs_0_, bf16[2,64,960]{2,1,0:T(8,128)(2,1)} %copy-done.15, bf16[64,1280]{1,0:T(8,128)(2,1)} %copy-done.4, bf16[64,1280]{1,0:T(8,128)(2,1)} %copy-done.10, ...), custom_call_target="tpu_custom_call" | custom-call | tf_op jit(solution)/shard_map/pallas_call | solution.py:102
  32.5 2.4 %collective-permute-start.3 = (bf16[2,32,1280]{2,1,0:T(8,128)(2,1)}, bf16[2,32,1280]{2,1,0:T(8,128)(2,1)S(1)}, u32[]{:S(2)}, u32[]{:S(2)}) collective-permute-start(bf16[2,32,1280]{2,1,0:T(8,128)(2,1)} %bitcast.51), channel_id=1, source_target_pairs={{0,16},{16,0},{1,17},{17,1},{2,18},{18,2},{3,19},{19,3},{4,20},{20... | collective-permute-start | bytes 491528 | tf_op jit(solution)/shard_map/ppermute | solution.py:34
  34.8 4.7 %text_norm.1 = (bf16[96,4096]{1,0:T(8,128)(2,1)}, bf16[96,4096]{1,0:T(8,128)(2,1)}, bf16[32,4096]{1,0:T(8,128)(2,1)}, bf16[32,4096]{1,0:T(8,128)(2,1)}) custom-call(s32[2]{0:T(128)} %pad_add_fusion.2.index_ref, bf16[128,8192]{1,0:T(8,128)(2,1)} %bitcast.40, f32[1,8192]{1,0:T(1,128)} %bitcast.44), custom_call_target="tpu_custom_call" | custom-call | tf_op jit(solution)/shard_map/text_norm/pallas_call | solution.py:504
  40.2 2.0 %shard_map.135 = (bf16[32,1536]{1,0:T(8,128)(2,1)}, bf16[32,1536]{1,0:T(8,128)(2,1)}) custom-call(s32[2]{0:T(128)} %copy-done.21, f32[2,32,1280]{2,1,0:T(8,128)} %get-tuple-element.38.refs_0_, bf16[2,32,1280]{2,1,0:T(8,128)(2,1)} %copy-done.16, bf16[16,512]{1,0:T(8,128)(2,1)} %shard_map.134.refs_2_, bf16[16,512]{1,0:T(8,128)(2,1)} %copy-done.18), custom_call_target="tpu_custom_call" | custom-call | tf_op jit(solution)/shard_map/pallas_call | solution.py:102
  42.2 1.5 %collective-permute-start.9 = (bf16[32,1536]{1,0:T(8,128)(2,1)}, bf16[32,1536]{1,0:T(8,128)(2,1)S(1)}, u32[]{:S(2)}, u32[]{:S(2)}) collective-permute-start(bf16[32,1536]{1,0:T(8,128)(2,1)} %get-tuple-element.43), channel_id=1, source_target_pairs={{0,2},{1,3},{2,0},{3,1},{4,6},{5,7},{6,4},{7,5},{8,10},{9,11},{10,... | collective-permute-start | bytes 294920 | tf_op jit(solution)/shard_map/ppermute | solution.py:52
  44.6 1.9 %collective-permute-start.6 = (bf16[32,1536]{1,0:T(8,128)(2,1)}, bf16[32,1536]{1,0:T(8,128)(2,1)S(1)}, u32[]{:S(2)}, u32[]{:S(2)}) collective-permute-start(bf16[32,1536]{1,0:T(8,128)(2,1)} %get-tuple-element.42), channel_id=1, source_target_pairs={{0,8},{1,9},{2,10},{3,11},{4,12},{5,13},{6,14},{7,15},{8,0},{9,1},... | collective-permute-start | bytes 294920 | tf_op jit(solution)/shard_map/ppermute | solution.py:52
  47.9 2.0 %collective-permute-start.10 = (bf16[64,1536]{1,0:T(8,128)(2,1)S(1)}, bf16[64,1536]{1,0:T(8,128)(2,1)S(1)}, u32[]{:S(2)}, u32[]{:S(2)}) collective-permute-start(bf16[64,1536]{1,0:T(8,128)(2,1)S(1)} %pad_maximum_fusion.5), channel_id=1, source_target_pairs={{0,8},{1,9},{2,10},{3,11},{4,12},{5,13},{6,14},{7,15},{8,0},{9,1},... | collective-permute-start | bytes 589832 | tf_op jit(solution)/shard_map/ppermute | solution.py:52
  49.9 5.7 %collective-permute-done.6 = bf16[32,1536]{1,0:T(8,128)(2,1)S(1)} collective-permute-done((bf16[32,1536]{1,0:T(8,128)(2,1)}, bf16[32,1536]{1,0:T(8,128)(2,1)S(1)}, u32[]{:S(2)}, u32[]{:S(2)}) %collective-permute-start.6) | collective-permute-done | bytes 98336 | tf_op jit(solution)/shard_map/ppermute | solution.py:52
  56.7 2.1 %collective-permute-done.10 = bf16[64,1536]{1,0:T(8,128)(2,1)S(1)} collective-permute-done((bf16[64,1536]{1,0:T(8,128)(2,1)S(1)}, bf16[64,1536]{1,0:T(8,128)(2,1)S(1)}, u32[]{:S(2)}, u32[]{:S(2)}) %collective-permute-start.10) | collective-permute-done | bytes 196640 | tf_op jit(solution)/shard_map/ppermute | solution.py:52
  59.8 4.6 %collective-permute-done.7 = bf16[64,1536]{1,0:T(8,128)(2,1)S(1)} collective-permute-done((bf16[64,1536]{1,0:T(8,128)(2,1)S(1)}, bf16[64,1536]{1,0:T(8,128)(2,1)S(1)}, u32[]{:S(2)}, u32[]{:S(2)}) %collective-permute-start.7) | collective-permute-done | bytes 196640 | tf_op jit(solution)/shard_map/ppermute | solution.py:52
  65.5 4.5 %collective-permute-done.11 = bf16[128,1536]{1,0:T(8,128)(2,1)S(1)} collective-permute-done((bf16[128,1536]{1,0:T(8,128)(2,1)S(1)}, bf16[128,1536]{1,0:T(8,128)(2,1)S(1)}, u32[]{:S(2)}, u32[]{:S(2)}) %collective-permute-start.11) | collective-permute-done | bytes 393248 | tf_op jit(solution)/shard_map/ppermute | solution.py:52
  71.1 2.2 %collective-permute-done.8 = bf16[128,1536]{1,0:T(8,128)(2,1)S(1)} collective-permute-done((bf16[128,1536]{1,0:T(8,128)(2,1)S(1)}, bf16[128,1536]{1,0:T(8,128)(2,1)S(1)}, u32[]{:S(2)}, u32[]{:S(2)}) %collective-permute-start.8) | collective-permute-done | bytes 393248 | tf_op jit(solution)/shard_map/ppermute | solution.py:52
  79.8 3.0 %fusion.43 = (bf16[256,512]{1,0:T(8,128)(2,1)S(1)}, f32[256,512]{1,0:T(8,128)}) fusion(bf16[256,2560]{1,0:T(8,128)(2,1)} %pad_maximum_fusion, bf16[2560,512]{1,0:T(8,128)(2,1)S(1)} %copy-done), kind=kOutput, calls=%fused_computation.89 | convolution fusion | flops 671219712 | bytes 4718592 | tf_op jit(solution)/shard_map/dot_general | solution.py:29
  82.7 1.6 %collective-permute-start.12 = (bf16[256,512]{1,0:T(8,128)(2,1)S(1)}, bf16[256,512]{1,0:T(8,128)(2,1)S(1)}, u32[]{:S(2)}, u32[]{:S(2)}) collective-permute-start(bf16[256,512]{1,0:T(8,128)(2,1)S(1)} %get-tuple-element.62), channel_id=1, source_target_pairs={{0,16},{16,0},{1,17},{17,1},{2,18},{18,2},{3,19},{19,3},{4,20},{20... | collective-permute-start | bytes 786440 | tf_op jit(solution)/shard_map/ppermute | solution.py:34
  85.2 3.0 %fusion.44 = (bf16[256,512]{1,0:T(8,128)(2,1)S(1)}, f32[256,512]{1,0:T(8,128)}) fusion(bf16[256,2560]{1,0:T(8,128)(2,1)} %collective-permute-done.13, bf16[2560,512]{1,0:T(8,128)(2,1)S(1)} %copy-done), kind=kOutput, calls=%fused_computation.90 | convolution fusion | flops 671219712 | bytes 4718592 | tf_op jit(solution)/shard_map/dot_general | solution.py:29
  90.0 14.4 %collective-permute-done.12.refs_2_ = bf16[256,512]{1,0:T(8,128)(2,1)S(1)} collective-permute-done((bf16[256,512]{1,0:T(8,128)(2,1)S(1)}, bf16[256,512]{1,0:T(8,128)(2,1)S(1)}, u32[]{:S(2)}, u32[]{:S(2)}) %collective-permute-start.12) | collective-permute-done | bytes 262176 | tf_op jit(solution)/shard_map/ppermute | solution.py:34
  104.4 5.2 %collective-permute-done.14.refs_3_ = bf16[256,512]{1,0:T(8,128)(2,1)} collective-permute-done((bf16[256,512]{1,0:T(8,128)(2,1)S(1)}, bf16[256,512]{1,0:T(8,128)(2,1)}, u32[]{:S(2)}, u32[]{:S(2)}) %collective-permute-start.14) | collective-permute-done | bytes 262176 | tf_op jit(solution)/shard_map/ppermute | solution.py:34
  109.6 5.0 %shard_map.136 = (bf16[512,512]{1,0:T(8,128)(2,1)}, bf16[16,24,512]{2,1,0:T(8,128)(2,1)}) custom-call(s32[16]{0:T(128)} %copy-done.20, s32[16]{0:T(128)} %slice_bitcast_fusion.holder_ref, f32[256,512]{1,0:T(8,128)} %get-tuple-element.63.refs_0_, f32[256,512]{1,0:T(8,128)} %get-tuple-element.65.refs_1_, bf16[256,512]{1,0:T(8,128)(2,1)} %copy-done.14, ...), custom_call_target="tpu_custom_call" | custom-call | tf_op jit(solution)/shard_map/pallas_call | solution.py:102
  114.6 3.7 %all-to-all-start = ((bf16[16,24,512]{2,1,0:T(8,128)(2,1)}), bf16[16,24,512]{2,1,0:T(8,128)(2,1)S(1)}, u32[]{:S(2)}, u32[]{:S(2)}) async-start(bf16[16,24,512]{2,1,0:T(8,128)(2,1)} %get-tuple-element.50), calls=%async_computation | async-start | bytes 786432 | tf_op jit(solution)/shard_map/all_to_all | solution.py:637
  119.0 4.0 %fusion.12.refs_0_ = f32[192,512]{1,0:T(8,128)S(1)} fusion(bf16[4096,512]{1,0:T(8,128)(2,1)} %param.19, bf16[96,4096]{1,0:T(8,128)(2,1)} %collective-permute-done.4, bf16[96,4096]{1,0:T(8,128)(2,1)} %get-tuple-element.36), kind=kOutput, calls=%fused_computation.13 | convolution fusion | flops 808452096 | bytes 6160384 | tf_op jit(solution)/shard_map/dot_general | solution.py:29
  124.8 2.4 %collective-permute-done.15 = bf16[32,4096]{1,0:T(8,128)(2,1)S(1)} collective-permute-done((bf16[32,4096]{1,0:T(8,128)(2,1)}, bf16[32,4096]{1,0:T(8,128)(2,1)S(1)}, u32[]{:S(2)}, u32[]{:S(2)}) %collective-permute-start.15) | collective-permute-done | bytes 262176 | tf_op jit(solution)/shard_map/ppermute | solution.py:34
  131.0 1.9 %shard_map.137 = (f32[8,512]{1,0:T(8,128)}, f32[512,8]{1,0:T(8,128)}) custom-call(s32[16]{0:T(128)} %copy-done.20, bf16[16,24,512]{2,1,0:T(8,128)(2,1)} %copy-done.3), custom_call_target="tpu_custom_call" | custom-call | tf_op jit(solution)/shard_map/pallas_call | solution.py:102
  134.3 6.0 %fusion = f32[2560,512]{1,0:T(8,128)} fusion(bf16[256,2560]{1,0:T(8,128)(2,1)} %collective-permute-done.13, bf16[256,1024]{1,0:T(8,128)(2,1)S(1)} %slice.72, bf16[128,1536]{1,0:T(8,128)(2,1)} %copy-done.12, bf16[64,1536]{1,0:T(8,128)(2,1)} %copy-done.8, bf16[32,1536]{1,0:T(8,128)(2,1)} %copy-done.7, bf16[32,1536]{1,0:T(8,128)(2,1)} %get-tuple-element.42, ...), kind=kOutput, calls=%fused_computation | convolution fusion | flops 1359216640 | bytes 9441280 | tf_op jit(solution)/shard_map/dot_general | solution.py:645
  140.3 2.5 %shard_map.138 = bf16[128,512]{1,0:T(8,128)(2,1)} custom-call(s32[2]{0:T(128)} %pad_add_fusion.2.index_ref, s32[1,16,2]{2,1,0:T(8,128)} %copy.27.grid_ref, s32[1,16]{1,0:T(1,128)} %start_ref.3, f32[192,512]{1,0:T(8,128)} %copy-done.11, f32[64,512]{1,0:T(8,128)} %copy-done.9, bf16[96,512]{1,0:T(8,128)(2,1)} %collective-permute-done.16.refs_2_, ...), custom_call_target="tpu_custom_call" | custom-call | tf_op jit(solution)/shard_map/pallas_call | solution.py:102
  (112 shorter events, 31.3 us)
Async XLA Ops:
  0.6 79.2 %copy-start = (bf16[2560,512]{1,0:T(8,128)(2,1)S(1)}, bf16[2560,512]{1,0:T(8,128)(2,1)}, u32[]{:S(2)}) copy-start(bf16[2560,512]{1,0:T(8,128)(2,1)} %param.16) | copy-start | bytes 7864324
  0.6 19.3 %copy-start.19 = (s32[1,16,2]{1,2,0:T(2,128)S(1)}, s32[1,16,2]{1,2,0:T(2,128)}, u32[]{:S(2)}) copy-start(s32[1,16,2]{1,2,0:T(2,128)} %param.21) | copy-start | bytes 388
  1.5 13.3 %collective-permute-start = (s32[3,16]{1,0:T(4,128)S(1)}, s32[3,16]{1,0:T(4,128)S(1)}, u32[]{:S(2)}, u32[]{:S(2)}) collective-permute-start(s32[3,16]{1,0:T(4,128)S(1)} %get-tuple-element.61), channel_id=1, source_target_pairs={{0,16},{16,0},{1,17},{17,1},{2,18},{18,2},{3,19},{19,3},{4,20},{20... | collective-permute-start | bytes 584 | tf_op jit(solution)/shard_map/ppermute | solution.py:34
  5.6 9.3 %copy-start.4 = (bf16[64,1280]{1,0:T(8,128)(2,1)}, bf16[64,1280]{1,0:T(8,128)(2,1)S(1)}, u32[]{:S(2)}) copy-start(bf16[64,1280]{1,0:T(8,128)(2,1)S(1)} %convolution_convert_fusion.refs_0_.refs_2_) | copy-start | bytes 491524
  5.7 9.3 %collective-permute-start.1 = (bf16[64,1280]{1,0:T(8,128)(2,1)S(1)}, bf16[64,1280]{1,0:T(8,128)(2,1)S(1)}, u32[]{:S(2)}, u32[]{:S(2)}) collective-permute-start(bf16[64,1280]{1,0:T(8,128)(2,1)S(1)} %convolution_convert_fusion.refs_0_.refs_2_), channel_id=1, source_target_pairs={{0,16},{16,0},{1,17},{17,1},{2,18},{18,2},{3,19},{19,3},{4,20},{20... | collective-permute-start | bytes 491528 | tf_op jit(solution)/shard_map/ppermute | solution.py:34
  7.6 69.0 %collective-permute-start.19 = (bf16[512,512]{1,0:T(8,128)(2,1)}, bf16[512,512]{1,0:T(8,128)(2,1)}, u32[]{:S(2)}, u32[]{:S(2)}) collective-permute-start(bf16[512,512]{1,0:T(8,128)(2,1)} %constant_dynamic-slice_fusion), channel_id=1, source_target_pairs={{0,16},{1,17},{2,18},{3,19},{4,20},{5,21},{6,22},{7,23},{24,8},{25... | collective-permute-start | bytes 1572872 | tf_op jit(solution)/shard_map/ppermute | solution.py:602
  14.9 24.6 %copy-start.21 = (s32[2]{0:T(128)}, s32[2]{0:T(128)S(1)}, u32[]{:S(2)}) copy-start(s32[2]{0:T(128)S(1)} %select_reduce_fusion.count_ref) | copy-start | bytes 28
  14.9 19.9 %copy-start.22 = (s32[16]{0:T(128)S(1)}, s32[16]{0:T(128)}, u32[]{:S(2)}) copy-start(s32[16]{0:T(128)} %constant.108.clone) | copy-start | bytes 196
  19.4 8.9 %collective-permute-start.2 = (bf16[2,64,960]{2,1,0:T(8,128)(2,1)}, bf16[2,64,960]{2,1,0:T(8,128)(2,1)S(1)}, u32[]{:S(2)}, u32[]{:S(2)}) collective-permute-start(bf16[2,64,960]{2,1,0:T(8,128)(2,1)} %bitcast.50), channel_id=1, source_target_pairs={{0,16},{16,0},{1,17},{17,1},{2,18},{18,2},{3,19},{19,3},{4,20},{20... | collective-permute-start | bytes 737288 | tf_op jit(solution)/shard_map/ppermute | solution.py:34
  25.9 13.6 %collective-permute-start.5 = (bf16[16,512]{1,0:T(8,128)(2,1)}, bf16[16,512]{1,0:T(8,128)(2,1)S(1)}, u32[]{:S(2)}, u32[]{:S(2)}) collective-permute-start(bf16[16,512]{1,0:T(8,128)(2,1)} %shard_map.134.refs_2_), channel_id=1, source_target_pairs={{0,16},{16,0},{1,17},{17,1},{2,18},{18,2},{3,19},{19,3},{4,20},{20... | collective-permute-start | bytes 49160 | tf_op jit(solution)/shard_map/ppermute | solution.py:34
  32.5 7.1 %collective-permute-start.3 = (bf16[2,32,1280]{2,1,0:T(8,128)(2,1)}, bf16[2,32,1280]{2,1,0:T(8,128)(2,1)S(1)}, u32[]{:S(2)}, u32[]{:S(2)}) collective-permute-start(bf16[2,32,1280]{2,1,0:T(8,128)(2,1)} %bitcast.51), channel_id=1, source_target_pairs={{0,16},{16,0},{1,17},{17,1},{2,18},{18,2},{3,19},{19,3},{4,20},{20... | collective-permute-start | bytes 491528 | tf_op jit(solution)/shard_map/ppermute | solution.py:34
  34.8 49.6 %copy-start.20 = (s32[16]{0:T(128)}, s32[16]{0:T(128)S(1)}, u32[]{:S(2)}) copy-start(s32[16]{0:T(128)S(1)} %broadcast_xor_fusion.owner_ref) | copy-start | bytes 196
  42.2 31.1 %copy-start.6 = (bf16[32,1536]{1,0:T(8,128)(2,1)S(1)}, bf16[32,1536]{1,0:T(8,128)(2,1)}, u32[]{:S(2)}) copy-start(bf16[32,1536]{1,0:T(8,128)(2,1)} %get-tuple-element.42) | copy-start | bytes 294916
  42.2 4.8 %collective-permute-start.9 = (bf16[32,1536]{1,0:T(8,128)(2,1)}, bf16[32,1536]{1,0:T(8,128)(2,1)S(1)}, u32[]{:S(2)}, u32[]{:S(2)}) collective-permute-start(bf16[32,1536]{1,0:T(8,128)(2,1)} %get-tuple-element.43), channel_id=1, source_target_pairs={{0,2},{1,3},{2,0},{3,1},{4,6},{5,7},{6,4},{7,5},{8,10},{9,11},{10,... | collective-permute-start | bytes 294920 | tf_op jit(solution)/shard_map/ppermute | solution.py:52
  44.6 11.0 %collective-permute-start.6 = (bf16[32,1536]{1,0:T(8,128)(2,1)}, bf16[32,1536]{1,0:T(8,128)(2,1)S(1)}, u32[]{:S(2)}, u32[]{:S(2)}) collective-permute-start(bf16[32,1536]{1,0:T(8,128)(2,1)} %get-tuple-element.42), channel_id=1, source_target_pairs={{0,8},{1,9},{2,10},{3,11},{4,12},{5,13},{6,14},{7,15},{8,0},{9,1},... | collective-permute-start | bytes 294920 | tf_op jit(solution)/shard_map/ppermute | solution.py:52
  47.9 10.9 %collective-permute-start.10 = (bf16[64,1536]{1,0:T(8,128)(2,1)S(1)}, bf16[64,1536]{1,0:T(8,128)(2,1)S(1)}, u32[]{:S(2)}, u32[]{:S(2)}) collective-permute-start(bf16[64,1536]{1,0:T(8,128)(2,1)S(1)} %pad_maximum_fusion.5), channel_id=1, source_target_pairs={{0,8},{1,9},{2,10},{3,11},{4,12},{5,13},{6,14},{7,15},{8,0},{9,1},... | collective-permute-start | bytes 589832 | tf_op jit(solution)/shard_map/ppermute | solution.py:52
  55.6 18.8 %copy-start.7 = (bf16[32,1536]{1,0:T(8,128)(2,1)}, bf16[32,1536]{1,0:T(8,128)(2,1)S(1)}, u32[]{:S(2)}) copy-start(bf16[32,1536]{1,0:T(8,128)(2,1)S(1)} %collective-permute-done.6) | copy-start | bytes 294916
  56.6 7.8 %collective-permute-start.7 = (bf16[64,1536]{1,0:T(8,128)(2,1)S(1)}, bf16[64,1536]{1,0:T(8,128)(2,1)S(1)}, u32[]{:S(2)}, u32[]{:S(2)}) collective-permute-start(bf16[64,1536]{1,0:T(8,128)(2,1)S(1)} %pad_maximum_fusion.4), channel_id=1, source_target_pairs={{0,4},{1,5},{2,6},{3,7},{4,0},{5,1},{6,2},{7,3},{8,12},{9,13},{10,... | collective-permute-start | bytes 589832 | tf_op jit(solution)/shard_map/ppermute | solution.py:52
  59.7 10.3 %collective-permute-start.11 = (bf16[128,1536]{1,0:T(8,128)(2,1)S(1)}, bf16[128,1536]{1,0:T(8,128)(2,1)S(1)}, u32[]{:S(2)}, u32[]{:S(2)}) collective-permute-start(bf16[128,1536]{1,0:T(8,128)(2,1)S(1)} %pad_maximum_fusion.3), channel_id=1, source_target_pairs={{0,4},{1,5},{2,6},{3,7},{4,0},{5,1},{6,2},{7,3},{8,12},{9,13},{10,... | collective-permute-start | bytes 1179656 | tf_op jit(solution)/shard_map/ppermute | solution.py:52
  64.4 10.0 %copy-start.8 = (bf16[64,1536]{1,0:T(8,128)(2,1)}, bf16[64,1536]{1,0:T(8,128)(2,1)S(1)}, u32[]{:S(2)}) copy-start(bf16[64,1536]{1,0:T(8,128)(2,1)S(1)} %collective-permute-done.7) | copy-start | bytes 589828
  65.4 7.8 %collective-permute-start.8 = (bf16[128,1536]{1,0:T(8,128)(2,1)S(1)}, bf16[128,1536]{1,0:T(8,128)(2,1)S(1)}, u32[]{:S(2)}, u32[]{:S(2)}) collective-permute-start(bf16[128,1536]{1,0:T(8,128)(2,1)S(1)} %pad_maximum_fusion.2), channel_id=1, source_target_pairs={{0,2},{1,3},{2,0},{3,1},{4,6},{5,7},{6,4},{7,5},{8,10},{9,11},{10,... | collective-permute-start | bytes 1179656 | tf_op jit(solution)/shard_map/ppermute | solution.py:52
  74.5 10.7 %collective-permute-start.13 = (bf16[256,2560]{1,0:T(8,128)(2,1)}, bf16[256,2560]{1,0:T(8,128)(2,1)}, u32[]{:S(2)}, u32[]{:S(2)}) collective-permute-start(bf16[256,2560]{1,0:T(8,128)(2,1)} %pad_maximum_fusion), channel_id=1, source_target_pairs={{0,1},{1,0},{2,3},{3,2},{4,5},{5,4},{6,7},{7,6},{8,9},{9,8},{10,11... | collective-permute-start | bytes 3932168 | tf_op jit(solution)/shard_map/ppermute | solution.py:78
  76.0 12.5 %copy-start.17 = (f32[512]{0:T(512)}, f32[512]{0:T(512)S(1)}, u32[]{:S(2)}) copy-start(f32[512]{0:T(512)S(1)} %dynamic_slice.7) | copy-start | bytes 6148
  78.1 10.5 %copy-start.2 = (bf16[512,512]{1,0:T(8,128)(2,1)}, bf16[512,512]{1,0:T(8,128)(2,1)S(1)}, u32[]{:S(2)}) copy-start(bf16[512,512]{1,0:T(8,128)(2,1)S(1)} %select_add_fusion.refs_6_) | copy-start | bytes 1572868
  78.1 41.0 %collective-permute-start.4 = (bf16[96,4096]{1,0:T(8,128)(2,1)}, bf16[96,4096]{1,0:T(8,128)(2,1)}, u32[]{:S(2)}, u32[]{:S(2)}) collective-permute-start(bf16[96,4096]{1,0:T(8,128)(2,1)} %get-tuple-element.37), channel_id=1, source_target_pairs={{0,16},{16,0},{1,17},{17,1},{2,18},{18,2},{3,19},{19,3},{4,20},{20... | collective-permute-start | bytes 2359304 | tf_op jit(solution)/shard_map/ppermute | solution.py:34
  79.2 5.1 %collective-permute-start.18 = (bf16[256,512]{1,0:T(8,128)(2,1)S(1)}, bf16[256,512]{1,0:T(8,128)(2,1)S(1)}, u32[]{:S(2)}, u32[]{:S(2)}) collective-permute-start(bf16[256,512]{1,0:T(8,128)(2,1)S(1)} %slice.75), channel_id=1, source_target_pairs={{0,1},{1,0},{2,3},{3,2},{4,5},{5,4},{6,7},{7,6},{8,9},{9,8},{10,11... | collective-permute-start | bytes 786440 | tf_op jit(solution)/shard_map/ppermute | solution.py:79
  82.7 21.6 %collective-permute-start.12 = (bf16[256,512]{1,0:T(8,128)(2,1)S(1)}, bf16[256,512]{1,0:T(8,128)(2,1)S(1)}, u32[]{:S(2)}, u32[]{:S(2)}) collective-permute-start(bf16[256,512]{1,0:T(8,128)(2,1)S(1)} %get-tuple-element.62), channel_id=1, source_target_pairs={{0,16},{16,0},{1,17},{17,1},{2,18},{18,2},{3,19},{19,3},{4,20},{20... | collective-permute-start | bytes 786440 | tf_op jit(solution)/shard_map/ppermute | solution.py:34
  88.1 21.5 %collective-permute-start.14 = (bf16[256,512]{1,0:T(8,128)(2,1)S(1)}, bf16[256,512]{1,0:T(8,128)(2,1)}, u32[]{:S(2)}, u32[]{:S(2)}) collective-permute-start(bf16[256,512]{1,0:T(8,128)(2,1)S(1)} %get-tuple-element.64), channel_id=1, source_target_pairs={{0,16},{16,0},{1,17},{17,1},{2,18},{18,2},{3,19},{19,3},{4,20},{20... | collective-permute-start | bytes 786440 | tf_op jit(solution)/shard_map/ppermute | solution.py:34
  114.6 15.7 %all-to-all-start = ((bf16[16,24,512]{2,1,0:T(8,128)(2,1)}), bf16[16,24,512]{2,1,0:T(8,128)(2,1)S(1)}, u32[]{:S(2)}, u32[]{:S(2)}) async-start(bf16[16,24,512]{2,1,0:T(8,128)(2,1)} %get-tuple-element.50), calls=%async_computation | async-start | bytes 786432 | tf_op jit(solution)/shard_map/all_to_all | solution.py:637
  118.4 8.9 %collective-permute-start.15 = (bf16[32,4096]{1,0:T(8,128)(2,1)}, bf16[32,4096]{1,0:T(8,128)(2,1)S(1)}, u32[]{:S(2)}, u32[]{:S(2)}) collective-permute-start(bf16[32,4096]{1,0:T(8,128)(2,1)} %get-tuple-element.47), channel_id=1, source_target_pairs={{0,16},{16,0},{1,17},{17,1},{2,18},{18,2},{3,19},{19,3},{4,20},{20... | collective-permute-start | bytes 786440 | tf_op jit(solution)/shard_map/ppermute | solution.py:34
  123.7 16.6 %collective-permute-start.16 = (bf16[96,512]{1,0:T(8,128)(2,1)}, bf16[96,512]{1,0:T(8,128)(2,1)}, u32[]{:S(2)}, u32[]{:S(2)}) collective-permute-start(bf16[96,512]{1,0:T(8,128)(2,1)} %slice.87), channel_id=1, source_target_pairs={{0,16},{16,0},{1,17},{17,1},{2,18},{18,2},{3,19},{19,3},{4,20},{20... | collective-permute-start | bytes 294920 | tf_op jit(solution)/shard_map/ppermute | solution.py:34
  128.8 11.5 %collective-permute-start.17 = (bf16[32,512]{1,0:T(8,128)(2,1)}, bf16[32,512]{1,0:T(8,128)(2,1)}, u32[]{:S(2)}, u32[]{:S(2)}) collective-permute-start(bf16[32,512]{1,0:T(8,128)(2,1)} %slice.88), channel_id=1, source_target_pairs={{0,16},{16,0},{1,17},{17,1},{2,18},{18,2},{3,19},{19,3},{4,20},{20... | collective-permute-start | bytes 98312 | tf_op jit(solution)/shard_map/ppermute | solution.py:34
  (12 other events, 35.0 us)

commit v6 on v5

--- a/solution.py
+++ b/solution.py
@@ -54,9 +54,8 @@
     return pieces, offsets
 
 
-def gather_halves(left, right, main):
+def gather_halves(left, right, main, own):
     size = lax.axis_size("ctx")
-    own = lax.axis_index("ctx")
     middle, rows = left.shape[1], left.shape[0]
     if size & (size - 1) or size < 8:
         x = jnp.concatenate([left, right], axis=1)
@@ -74,6 +73,7 @@
     rights = jnp.concatenate([found[o] for o in order], axis=0)
     low = jnp.concatenate([jnp.concatenate(lefts, axis=0), rights[:, : main - middle]], axis=1)
     rest = rights[:, main - middle :]
+    low, own = barrier((low, own))
     pairs = [(i, i ^ 1) for i in range(size)]
     lows = [low, lax.ppermute(low, "ctx", pairs)]
     rests = [rest, lax.ppermute(rest, "ctx", pairs)]
@@ -293,12 +293,13 @@
     )
 
 
-def norm_scales(parts, groups, width, owners, arrived, capacity):
-    rows = parts * capacity
-    total = groups * rows
+def norm_scales(parts, groups, width, owners, arrived, embedded, weighted):
+    total, columns = embedded.shape
+    rows = total // groups
+    capacity = rows // parts
     lines = total // arrived.shape[2]
 
-    def kernel(owner_ref, sums_ref, scale_ref, columns_ref, turned):
+    def kernel(owner_ref, sums_ref, embed_ref, weighted_ref, scale_ref, grad_ref, turned):
         summed = jnp.sum(sums_ref[:, capacity:, :].astype(F32), axis=0)
 
         def whole(q):
@@ -315,14 +316,15 @@
         scale_ref[...] = both
         turned[...] = jnp.transpose(both)
         for i in range(groups):
-            columns_ref[pl.ds(i * rows, rows), :] = turned[
-                pl.ds(pl.multiple_of(owner_ref[i] * rows, rows), rows), :
-            ]
-
-    return call(
-        kernel,
-        (jax.ShapeDtypeStruct((8, total), F32), jax.ShapeDtypeStruct((total, 8), F32)),
-        (owners, arrived),
+            at = pl.ds(i * rows, rows)
+            both = turned[pl.ds(pl.multiple_of(owner_ref[i] * rows, rows), rows), :]
+            grad = both[:, 0:1] * weighted_ref[at, :] - embed_ref[at, :].astype(F32) * both[:, 1:2]
+            grad_ref[at, :] = grad.astype(BF16)
+
+    return call(
+        kernel,
+        (jax.ShapeDtypeStruct((8, total), F32), jax.ShapeDtypeStruct((total, columns), BF16)),
+        (owners, arrived, embedded, weighted),
         scalars=1,
         scratch=[pltpu.VMEM((total, 8), F32)],
     )
@@ -577,7 +579,6 @@
     scalars = jnp.concatenate([index[:1], own_counts])
     hidden_rows, sent = attend(parts, places, scalars, mine, received, images, vit_out)
     received = [shift(sent[k - 1], k) for k in others]
-    received, text_blocks = barrier((received, text_blocks))
     left, right = merge(parts, places, own_counts, hidden_rows, received, grads)
     main = places * piece_width
     if pieces > 1:
@@ -587,12 +588,15 @@
         merged = jnp.concatenate([taken, merged[:, vit_width:]], axis=1)
         middle = min(merged.shape[1] // 2, main)
         left, right = merged[:, :middle], merged[:, middle:]
-    merged_all, grads, owners = gather_halves(left, right, main)
+    left, right, key_source, gain_source, own_later = barrier(
+        (left, right, key_weight, lang_norm_gain, own)
+    )
+    merged_all, grads, owners = gather_halves(left, right, main, own_later)
 
     part_features = width // parts
-    own_start = own * feature_cols
+    own_start = own_later * feature_cols
     holder_part = own_start // part_features
-    candidate = lax.dynamic_slice_in_dim(key_weight, own_start % part_features, feature_cols, 0)
+    candidate = lax.dynamic_slice_in_dim(key_source, own_start % part_features, feature_cols, 0)
     key_rows = jnp.where(own_part == holder_part, candidate, jnp.zeros_like(candidate))
     held_by = [g * feature_cols // part_features for g in range(groups)]
     for k in others:
@@ -600,7 +604,7 @@
             (held_by[g] * groups + g, (held_by[g] + k) % parts * groups + g) for g in range(groups)
         ]
         key_rows = key_rows + lax.ppermute(candidate, ("dp", "ctx"), pairs)
-    own_gain = lax.dynamic_slice_in_dim(lang_norm_gain, own_start, feature_cols, 0).reshape(1, -1)
+    own_gain = lax.dynamic_slice_in_dim(gain_source, own_start, feature_cols, 0).reshape(1, -1)
 
     def text_terms(blocks):
         rows = [blocks[0]] + [shift(blocks[k], k) for k in others]
@@ -630,18 +634,15 @@
     embed_parts = [dot(rows, merger) for rows in merged_all]
     joined = jnp.concatenate(merged_all, axis=0)
     received = [[shift(part.astype(BF16), k) for k in others] for part in embed_parts]
-    received, late_blocks = barrier((received, text_blocks[1]))
     embedded, outgoing = features(
         parts, groups, owners, block_range[0], embed_parts, received, weighted, own_gain, key_rows
     )
     arrived = lax.all_to_all(outgoing, "ctx", 0, 0, tiled=True)
-    late_terms = text_terms(late_blocks)
+    late_terms = text_terms(text_blocks[1])
     returned = [text_return(early_terms), text_return(late_terms)]
-    scales, columns = norm_scales(
-        parts, groups, float(width), owners, arrived, capacity
-    )
-    grad_embedded = columns[:, 0:1] * weighted - embedded.astype(F32) * columns[:, 1:2]
-    grad_embedded = grad_embedded.astype(BF16)
+    scales, grad_embedded = norm_scales(
+        parts, groups, float(width), owners, arrived, embedded, weighted
+    )
     merger_grad = lax.dot_general(
         joined, grad_embedded, (((0,), (0,)), ((), ())), preferred_element_type=F32
     )

time: 144 us -> 127 us (0.88)
  waiting for transfers between devices: 43 us -> 28.7 us
  local copies, waits for them, and re-layouts: 16.4 us -> 13.9 us
  matrix products: 19.8 us -> 17.6 us
  starting transfers between devices: 26.6 us -> 28.6 us
    ppermute x6, waiting for transfers between devices: 19.6 us -> 7.34 us  [xor_gather(): lax.ppermute(joined, 'ctx', [(i, i ^ stride) for i in range(size)])]
    ppermute x11, waiting for transfers between devices: 22.4 us -> 14.3 us  [shift(): return lax.ppermute(x, 'dp', [(i, (i + k) % size) for i in range(size)])]
    ppermute x1, waiting for transfers between devices: 0.01 us -> 4.06 us  [on_device(): key_rows = key_rows + lax.ppermute(candidate, ('dp', 'ctx'), pairs)]
    ppermute x6, starting transfers between devices: 5.67 us -> 8.85 us  [xor_gather(): lax.ppermute(joined, 'ctx', [(i, i ^ stride) for i in range(size)])]
    ppermute x1, starting transfers between devices: 4.69 us -> 2.48 us  [on_device(): key_rows = key_rows + lax.ppermute(candidate, ('dp', 'ctx'), pairs)]
    all_to_all x1, waiting for transfers between devices: 0.94 us -> 3.05 us  [on_device(): arrived = lax.all_to_all(outgoing, 'ctx', 0, 0, tiled=True)]
    dot_general x5, matrix products: 11.9 us -> 10 us  [dot(): return jnp.dot(a, b, preferred_element_type=F32, **kw)]
    all_to_all x1, starting transfers between devices: 3.73 us -> 5.21 us  [on_device(): arrived = lax.all_to_all(outgoing, 'ctx', 0, 0, tiled=True)]
  transfers between devices with their start and end apart: 21 -> 21, of which waited for: 11 -> 9; matrix products, arithmetic and copies ran while one was open for 29% -> 28% of each run, Pallas kernels for 17% -> 17%
where the time goes in v6:
time: 127 us; the launch traced here: 126 us
  waiting for transfers between devices  28.7 us (23%)
  starting transfers between devices  28.6 us (23%)
  Pallas kernels  27.7 us (22%)
  matrix products  17.6 us (14%)
  local copies, waits for them, and re-layouts  13.9 us (11%)
  other arithmetic  8.05 us (6%)
    pallas_call x8, Pallas kernels, call(): pl.pallas_call(kernel, out_shape=outs, in_specs=[SMEM] * scalars + [VMEM]...  23 us
    ppermute x11, waiting for transfers between devices, shift(): return lax.ppermute(x, 'dp', [(i, (i + k) % size) for i in range(size)])  14.3 us
    ppermute x11, starting transfers between devices, shift(): return lax.ppermute(x, 'dp', [(i, (i + k) % size) for i in range(size)])  11.4 us
    dot_general x5, matrix products, dot(): return jnp.dot(a, b, preferred_element_type=F32, **kw)  10 us
    ppermute x6, starting transfers between devices, xor_gather(): lax.ppermute(joined, 'ctx', [(i, i ^ stride) for i in range(size)])  8.85 us
    ppermute x6, waiting for transfers between devices, xor_gather(): lax.ppermute(joined, 'ctx', [(i, i ^ stride) for i in range(size)])  7.34 us
    unnamed x54, local copies, waits for them, and re-layouts  6.03 us
    dot_general x1, matrix products, on_device(): lax.dot_general(joined, grad_embedded, (((0,), (0,)), ((), ())), preferre...  5.75 us
  transfers between devices with their start and end apart: 21, of which 9 were waited for; matrix products, arithmetic and copies ran while one was open for 28% of the time, Pallas kernels for 17%

profile of v6, /device:TPU:0, one launch (start us, length us, event | category | flops | bytes accessed | tf_op | source)
XLA Modules:
  0.0 125.6 jit_solution(16396270629856147204)
XLA Ops:
  1.5 3.0 %collective-permute-start.4 = (s32[3,16]{1,0:T(4,128)S(1)}, s32[3,16]{1,0:T(4,128)S(1)}, u32[]{:S(2)}, u32[]{:S(2)}) collective-permute-start(s32[3,16]{1,0:T(4,128)S(1)} %get-tuple-element.55), channel_id=1, source_target_pairs={{0,16},{16,0},{1,17},{17,1},{2,18},{18,2},{3,19},{19,3},{4,20},{20... | collective-permute-start | bytes 584 | tf_op jit(solution)/shard_map/ppermute | solution.py:34
  8.2 3.2 %collective-permute-done.5.refs_1_.refs_3_ = bf16[64,1280]{1,0:T(8,128)(2,1)S(1)} collective-permute-done((bf16[64,1280]{1,0:T(8,128)(2,1)S(1)}, bf16[64,1280]{1,0:T(8,128)(2,1)S(1)}, u32[]{:S(2)}, u32[]{:S(2)}) %collective-permute-start.5) | collective-permute-done | bytes 163872 | tf_op jit(solution)/shard_map/ppermute | solution.py:34
  12.0 3.8 %shard_map.131 = (f32[2,64,960]{2,1,0:T(8,128)}, bf16[1,2,64,960]{3,2,1,0:T(8,128)(2,1)}) custom-call(s32[2]{0:T(128)} %pad_add_fusion.2.index_ref, bf16[64,1280]{1,0:T(8,128)(2,1)} %copy-done.5, bf16[64,1280]{1,0:T(8,128)(2,1)} %copy-done.10, f32[1,1280]{1,0:T(1,128)} %reshape.108.refs_2_, bf16[640,1920]{1,0:T(8,128)(2,1)} %refs_3_.1), custom_call_target="tpu_custom_call" | custom-call | tf_op jit(solution)/shard_map/pallas_call | solution.py:102
  17.6 1.6 %shard_map.133 = f32[128,128]{1,0:T(8,128)} custom-call(s32[2]{0:T(128)} %pad_add_fusion.2.index_ref, s32[1,16,2]{2,1,0:T(8,128)} %copy.24.grid_ref, s32[1,16]{1,0:T(1,128)} %start_ref.3, f32[1,128]{1,0:T(1,128)} %fusion.27.inverse_ref), custom_call_target="tpu_custom_call" | custom-call | tf_op jit(solution)/shard_map/pallas_call | solution.py:102
  19.2 3.7 %collective-permute-done.6.refs_1_ = bf16[2,64,960]{2,1,0:T(8,128)(2,1)S(1)} collective-permute-done((bf16[2,64,960]{2,1,0:T(8,128)(2,1)}, bf16[2,64,960]{2,1,0:T(8,128)(2,1)S(1)}, u32[]{:S(2)}, u32[]{:S(2)}) %collective-permute-start.6) | collective-permute-done | bytes 245792 | tf_op jit(solution)/shard_map/ppermute | solution.py:34
  23.6 3.5 %shard_map.132 = (f32[2,32,1280]{2,1,0:T(8,128)}, bf16[1,2,32,1280]{3,2,1,0:T(8,128)(2,1)}) custom-call(s32[3]{0:T(128)} %pad_add_fusion.3.scalar_ref, f32[2,64,960]{2,1,0:T(8,128)} %get-tuple-element.30.refs_0_, bf16[2,64,960]{2,1,0:T(8,128)(2,1)} %copy-done.14, bf16[64,1280]{1,0:T(8,128)(2,1)} %copy-done.5, bf16[64,1280]{1,0:T(8,128)(2,1)} %copy-done.10, ...), custom_call_target="tpu_custom_call" | custom-call | tf_op jit(solution)/shard_map/pallas_call | solution.py:102
  27.8 1.7 %fusion.32 = (f32[128,128]{1,0:T(8,128)}, f32[128,128]{1,0:T(8,128)}) fusion(f32[128,128]{1,0:T(8,128)} %shard_map.133), kind=kLoop, calls=%fused_computation.75 | loop fusion | bytes 196608 | tf_op jit(solution)/shard_map/sin | solution.py:570
  29.5 1.9 %shard_map.134.refs_2_ = bf16[16,512]{1,0:T(8,128)(2,1)} custom-call(s32[2]{0:T(128)} %pad_add_fusion.2.index_ref, s32[1,16,2]{2,1,0:T(8,128)} %copy.24.grid_ref, s32[1,16]{1,0:T(1,128)} %start_ref.3, bf16[128,512]{1,0:T(8,128)(2,1)} %bitcast.44, f32[128,128]{1,0:T(8,128)} %get-tuple-element.51.cosine_ref.refs_6_, f32[128,128]{1,0:T(8,128)} %get-tuple-element.50.sine_ref.refs_7_), custom_call_target="tpu_custom_call" | custom-call | tf_op jit(solution)/shard_map/pallas_call | solution.py:102
  32.8 4.7 %text_norm.1 = (bf16[96,4096]{1,0:T(8,128)(2,1)}, bf16[96,4096]{1,0:T(8,128)(2,1)}, bf16[32,4096]{1,0:T(8,128)(2,1)}, bf16[32,4096]{1,0:T(8,128)(2,1)}) custom-call(s32[2]{0:T(128)} %pad_add_fusion.2.index_ref, bf16[128,8192]{1,0:T(8,128)(2,1)} %bitcast.41, f32[1,8192]{1,0:T(1,128)} %bitcast.45), custom_call_target="tpu_custom_call" | custom-call | tf_op jit(solution)/shard_map/text_norm/pallas_call | solution.py:506
  40.9 2.0 %shard_map.135 = (bf16[32,1536]{1,0:T(8,128)(2,1)}, bf16[32,1536]{1,0:T(8,128)(2,1)}) custom-call(s32[2]{0:T(128)} %copy-done.21, f32[2,32,1280]{2,1,0:T(8,128)} %get-tuple-element.33.refs_0_, bf16[2,32,1280]{2,1,0:T(8,128)(2,1)} %copy-done.15, bf16[16,512]{1,0:T(8,128)(2,1)} %shard_map.134.refs_2_, bf16[16,512]{1,0:T(8,128)(2,1)} %copy-done.18), custom_call_target="tpu_custom_call" | custom-call | tf_op jit(solution)/shard_map/pallas_call | solution.py:102
  45.3 2.6 %collective-permute-start.9 = (bf16[32,1536]{1,0:T(8,128)(2,1)}, bf16[32,1536]{1,0:T(8,128)(2,1)S(1)}, u32[]{:S(2)}, u32[]{:S(2)}) collective-permute-start(bf16[32,1536]{1,0:T(8,128)(2,1)} %get-tuple-element.39), channel_id=1, source_target_pairs={{0,8},{1,9},{2,10},{3,11},{4,12},{5,13},{6,14},{7,15},{8,0},{9,1},... | collective-permute-start | bytes 294920 | tf_op jit(solution)/shard_map/ppermute | solution.py:52
  49.1 2.5 %collective-permute-start.19 = (bf16[512,512]{1,0:T(8,128)(2,1)S(1)}, bf16[512,512]{1,0:T(8,128)(2,1)S(1)}, u32[]{:S(2)}, u32[]{:S(2)}) collective-permute-start(bf16[512,512]{1,0:T(8,128)(2,1)S(1)} %constant_dynamic-slice_fusion), channel_id=1, source_target_pairs={{0,16},{1,17},{2,18},{3,19},{4,20},{5,21},{6,22},{7,23},{24,8},{25... | collective-permute-start | bytes 1572872 | tf_op jit(solution)/shard_map/ppermute | solution.py:606
  53.2 1.6 %collective-permute-start.10 = (bf16[64,1536]{1,0:T(8,128)(2,1)S(1)}, bf16[64,1536]{1,0:T(8,128)(2,1)S(1)}, u32[]{:S(2)}, u32[]{:S(2)}) collective-permute-start(bf16[64,1536]{1,0:T(8,128)(2,1)S(1)} %pad_maximum_fusion.4), channel_id=1, source_target_pairs={{0,4},{1,5},{2,6},{3,7},{4,0},{5,1},{6,2},{7,3},{8,12},{9,13},{10,... | collective-permute-start | bytes 589832 | tf_op jit(solution)/shard_map/ppermute | solution.py:52
  55.8 2.5 %collective-permute-start.13 = (bf16[64,1536]{1,0:T(8,128)(2,1)S(1)}, bf16[64,1536]{1,0:T(8,128)(2,1)S(1)}, u32[]{:S(2)}, u32[]{:S(2)}) collective-permute-start(bf16[64,1536]{1,0:T(8,128)(2,1)S(1)} %pad_maximum_fusion.5), channel_id=1, source_target_pairs={{0,8},{1,9},{2,10},{3,11},{4,12},{5,13},{6,14},{7,15},{8,0},{9,1},... | collective-permute-start | bytes 589832 | tf_op jit(solution)/shard_map/ppermute | solution.py:52
  58.3 2.7 %collective-permute-done.10 = bf16[64,1536]{1,0:T(8,128)(2,1)S(1)} collective-permute-done((bf16[64,1536]{1,0:T(8,128)(2,1)S(1)}, bf16[64,1536]{1,0:T(8,128)(2,1)S(1)}, u32[]{:S(2)}, u32[]{:S(2)}) %collective-permute-start.10) | collective-permute-done | bytes 196640 | tf_op jit(solution)/shard_map/ppermute | solution.py:52
  62.5 2.1 %collective-permute-done.13 = bf16[64,1536]{1,0:T(8,128)(2,1)S(1)} collective-permute-done((bf16[64,1536]{1,0:T(8,128)(2,1)S(1)}, bf16[64,1536]{1,0:T(8,128)(2,1)S(1)}, u32[]{:S(2)}, u32[]{:S(2)}) %collective-permute-start.13) | collective-permute-done | bytes 196640 | tf_op jit(solution)/shard_map/ppermute | solution.py:52
  65.7 4.1 %collective-permute-done.19 = bf16[512,512]{1,0:T(8,128)(2,1)S(1)} collective-permute-done((bf16[512,512]{1,0:T(8,128)(2,1)S(1)}, bf16[512,512]{1,0:T(8,128)(2,1)S(1)}, u32[]{:S(2)}, u32[]{:S(2)}) %collective-permute-start.19) | collective-permute-done | bytes 524320 | tf_op jit(solution)/shard_map/ppermute | solution.py:606
  71.0 2.5 %collective-permute-done.14 = bf16[128,1536]{1,0:T(8,128)(2,1)S(1)} collective-permute-done((bf16[128,1536]{1,0:T(8,128)(2,1)S(1)}, bf16[128,1536]{1,0:T(8,128)(2,1)S(1)}, u32[]{:S(2)}, u32[]{:S(2)}) %collective-permute-start.14) | collective-permute-done | bytes 393248 | tf_op jit(solution)/shard_map/ppermute | solution.py:52
  75.2 1.6 %fusion.33 = (bf16[256,512]{1,0:T(8,128)(2,1)S(1)}, f32[256,512]{1,0:T(8,128)}) fusion(bf16[256,2560]{1,0:T(8,128)(2,1)S(1)} %pad_maximum_fusion, bf16[2560,512]{1,0:T(8,128)(2,1)S(1)} %copy-done), kind=kOutput, calls=%fused_computation.76 | convolution fusion | flops 671219712 | bytes 4718592 | tf_op jit(solution)/shard_map/dot_general | solution.py:29
  78.5 1.6 %fusion.34 = (bf16[256,512]{1,0:T(8,128)(2,1)S(1)}, f32[256,512]{1,0:T(8,128)}) fusion(bf16[256,2560]{1,0:T(8,128)(2,1)S(1)} %collective-permute-done.15, bf16[2560,512]{1,0:T(8,128)(2,1)S(1)} %copy-done), kind=kOutput, calls=%fused_computation.77 | convolution fusion | flops 671219712 | bytes 4718592 | tf_op jit(solution)/shard_map/dot_general | solution.py:29
  80.1 1.9 %collective-permute-start.17 = (bf16[256,512]{1,0:T(8,128)(2,1)S(1)}, bf16[256,512]{1,0:T(8,128)(2,1)}, u32[]{:S(2)}, u32[]{:S(2)}) collective-permute-start(bf16[256,512]{1,0:T(8,128)(2,1)S(1)} %get-tuple-element.58), channel_id=1, source_target_pairs={{0,16},{16,0},{1,17},{17,1},{2,18},{18,2},{3,19},{19,3},{4,20},{20... | collective-permute-start | bytes 786440 | tf_op jit(solution)/shard_map/ppermute | solution.py:34
  83.5 2.5 %collective-permute-done.16.refs_2_ = bf16[256,512]{1,0:T(8,128)(2,1)S(1)} collective-permute-done((bf16[256,512]{1,0:T(8,128)(2,1)S(1)}, bf16[256,512]{1,0:T(8,128)(2,1)S(1)}, u32[]{:S(2)}, u32[]{:S(2)}) %collective-permute-start.16) | collective-permute-done | bytes 262176 | tf_op jit(solution)/shard_map/ppermute | solution.py:34
  86.0 4.8 %collective-permute-done.17.refs_3_ = bf16[256,512]{1,0:T(8,128)(2,1)} collective-permute-done((bf16[256,512]{1,0:T(8,128)(2,1)S(1)}, bf16[256,512]{1,0:T(8,128)(2,1)}, u32[]{:S(2)}, u32[]{:S(2)}) %collective-permute-start.17) | collective-permute-done | bytes 262176 | tf_op jit(solution)/shard_map/ppermute | solution.py:34
  90.9 4.9 %shard_map.136 = (bf16[512,512]{1,0:T(8,128)(2,1)}, bf16[16,24,512]{2,1,0:T(8,128)(2,1)}) custom-call(s32[16]{0:T(128)} %copy-done.20, s32[16]{0:T(128)} %slice_bitcast_fusion.holder_ref, f32[256,512]{1,0:T(8,128)} %get-tuple-element.57.refs_0_, f32[256,512]{1,0:T(8,128)} %get-tuple-element.59.refs_1_, bf16[256,512]{1,0:T(8,128)(2,1)} %copy-done.13, ...), custom_call_target="tpu_custom_call" | custom-call | tf_op jit(solution)/shard_map/pallas_call | solution.py:102
  95.8 5.2 %all-to-all-start = ((bf16[16,24,512]{2,1,0:T(8,128)(2,1)}), bf16[16,24,512]{2,1,0:T(8,128)(2,1)S(1)}, u32[]{:S(2)}, u32[]{:S(2)}) async-start(bf16[16,24,512]{2,1,0:T(8,128)(2,1)} %get-tuple-element.46), calls=%async_computation | async-start | bytes 786432 | tf_op jit(solution)/shard_map/all_to_all | solution.py:640
  101.1 3.2 %fusion.9.refs_1_ = f32[64,512]{1,0:T(8,128)S(1)} fusion(bf16[4096,512]{1,0:T(8,128)(2,1)} %param.19, bf16[32,4096]{1,0:T(8,128)(2,1)} %collective-permute-done.1, bf16[32,4096]{1,0:T(8,128)(2,1)S(1)} %copy-done.12), kind=kOutput, calls=%fused_computation.13 | convolution fusion | flops 269484032 | bytes 4849664 | tf_op jit(solution)/shard_map/dot_general | solution.py:29
  105.3 2.3 %fusion.4.refs_0_ = f32[192,512]{1,0:T(8,128)S(1)} fusion(bf16[4096,512]{1,0:T(8,128)(2,1)S(1)} %copy-done.1, bf16[96,4096]{1,0:T(8,128)(2,1)} %collective-permute-done, bf16[96,4096]{1,0:T(8,128)(2,1)} %get-tuple-element.26), kind=kOutput, calls=%fused_computation.5 | convolution fusion | flops 808452096 | bytes 6160384 | tf_op jit(solution)/shard_map/dot_general | solution.py:29
  108.4 1.7 %collective-permute-start.2 = (bf16[96,512]{1,0:T(8,128)(2,1)}, bf16[96,512]{1,0:T(8,128)(2,1)S(1)}, u32[]{:S(2)}, u32[]{:S(2)}) collective-permute-start(bf16[96,512]{1,0:T(8,128)(2,1)} %slice.77), channel_id=1, source_target_pairs={{0,16},{16,0},{1,17},{17,1},{2,18},{18,2},{3,19},{19,3},{4,20},{20... | collective-permute-start | bytes 294920 | tf_op jit(solution)/shard_map/ppermute | solution.py:34
  110.1 3.1 %all-to-all-done.sums_ref.refs_4_ = bf16[16,24,512]{2,1,0:T(8,128)(2,1)S(1)} async-done(((bf16[16,24,512]{2,1,0:T(8,128)(2,1)}), bf16[16,24,512]{2,1,0:T(8,128)(2,1)S(1)}, u32[]{:S(2)}, u32[]{:S(2)}) %all-to-all-start) | async-done | bytes 393248 | tf_op jit(solution)/shard_map/all_to_all | solution.py:640
  113.9 2.8 %shard_map.137 = (f32[8,512]{1,0:T(8,128)}, bf16[512,512]{1,0:T(8,128)(2,1)}) custom-call(s32[16]{0:T(128)} %copy-done.20, bf16[16,24,512]{2,1,0:T(8,128)(2,1)} %copy-done.4, bf16[512,512]{1,0:T(8,128)(2,1)} %get-tuple-element.47.embed_ref, f32[512,512]{1,0:T(8,128)} %convolution_multiply_fusion.refs_4_.weighted_ref), custom_call_target="tpu_custom_call" | custom-call | tf_op jit(solution)/shard_map/pallas_call | solution.py:102
  116.7 5.7 %fusion = f32[2560,512]{1,0:T(8,128)} fusion(bf16[512,512]{1,0:T(8,128)(2,1)} %get-tuple-element.49, bf16[256,2560]{1,0:T(8,128)(2,1)} %copy-done.6, bf16[256,2560]{1,0:T(8,128)(2,1)} %copy-done.2), kind=kOutput, calls=%fused_computation | convolution fusion | flops 1347420160 | bytes 8388608 | tf_op jit(solution)/shard_map/dot_general | solution.py:646
  123.1 2.5 %shard_map.138 = bf16[128,512]{1,0:T(8,128)(2,1)} custom-call(s32[2]{0:T(128)} %pad_add_fusion.2.index_ref, s32[1,16,2]{2,1,0:T(8,128)} %copy.27.grid_ref, s32[1,16]{1,0:T(1,128)} %start_ref.3, f32[192,512]{1,0:T(8,128)} %copy-done.11, f32[64,512]{1,0:T(8,128)} %copy-done.9, bf16[96,512]{1,0:T(8,128)(2,1)} %copy-done.16, ...), custom_call_target="tpu_custom_call" | custom-call | tf_op jit(solution)/shard_map/pallas_call | solution.py:102
  (111 shorter events, 30.8 us)
Async XLA Ops:
  0.6 74.6 %copy-start = (bf16[2560,512]{1,0:T(8,128)(2,1)S(1)}, bf16[2560,512]{1,0:T(8,128)(2,1)}, u32[]{:S(2)}) copy-start(bf16[2560,512]{1,0:T(8,128)(2,1)} %param.16) | copy-start | bytes 7864324
  0.6 16.3 %copy-start.19 = (s32[1,16,2]{1,2,0:T(2,128)S(1)}, s32[1,16,2]{1,2,0:T(2,128)}, u32[]{:S(2)}) copy-start(s32[1,16,2]{1,2,0:T(2,128)} %param.21) | copy-start | bytes 388
  1.5 14.6 %collective-permute-start.4 = (s32[3,16]{1,0:T(4,128)S(1)}, s32[3,16]{1,0:T(4,128)S(1)}, u32[]{:S(2)}, u32[]{:S(2)}) collective-permute-start(s32[3,16]{1,0:T(4,128)S(1)} %get-tuple-element.55), channel_id=1, source_target_pairs={{0,16},{16,0},{1,17},{17,1},{2,18},{18,2},{3,19},{19,3},{4,20},{20... | collective-permute-start | bytes 584 | tf_op jit(solution)/shard_map/ppermute | solution.py:34
  5.6 5.7 %copy-start.5 = (bf16[64,1280]{1,0:T(8,128)(2,1)}, bf16[64,1280]{1,0:T(8,128)(2,1)S(1)}, u32[]{:S(2)}) copy-start(bf16[64,1280]{1,0:T(8,128)(2,1)S(1)} %convolution_convert_fusion.refs_0_.refs_2_) | copy-start | bytes 491524
  5.7 5.7 %collective-permute-start.5 = (bf16[64,1280]{1,0:T(8,128)(2,1)S(1)}, bf16[64,1280]{1,0:T(8,128)(2,1)S(1)}, u32[]{:S(2)}, u32[]{:S(2)}) collective-permute-start(bf16[64,1280]{1,0:T(8,128)(2,1)S(1)} %convolution_convert_fusion.refs_0_.refs_2_), channel_id=1, source_target_pairs={{0,16},{16,0},{1,17},{17,1},{2,18},{18,2},{3,19},{19,3},{4,20},{20... | collective-permute-start | bytes 491528 | tf_op jit(solution)/shard_map/ppermute | solution.py:34
  15.8 7.1 %collective-permute-start.6 = (bf16[2,64,960]{2,1,0:T(8,128)(2,1)}, bf16[2,64,960]{2,1,0:T(8,128)(2,1)S(1)}, u32[]{:S(2)}, u32[]{:S(2)}) collective-permute-start(bf16[2,64,960]{2,1,0:T(8,128)(2,1)} %bitcast.51), channel_id=1, source_target_pairs={{0,16},{16,0},{1,17},{17,1},{2,18},{18,2},{3,19},{19,3},{4,20},{20... | collective-permute-start | bytes 737288 | tf_op jit(solution)/shard_map/ppermute | solution.py:34
  16.3 24.0 %copy-start.21 = (s32[2]{0:T(128)}, s32[2]{0:T(128)S(1)}, u32[]{:S(2)}) copy-start(s32[2]{0:T(128)S(1)} %select_reduce_fusion.count_ref) | copy-start | bytes 28
  27.2 13.1 %collective-permute-start.7 = (bf16[2,32,1280]{2,1,0:T(8,128)(2,1)}, bf16[2,32,1280]{2,1,0:T(8,128)(2,1)S(1)}, u32[]{:S(2)}, u32[]{:S(2)}) collective-permute-start(bf16[2,32,1280]{2,1,0:T(8,128)(2,1)} %bitcast.52), channel_id=1, source_target_pairs={{0,16},{16,0},{1,17},{17,1},{2,18},{18,2},{3,19},{19,3},{4,20},{20... | collective-permute-start | bytes 491528 | tf_op jit(solution)/shard_map/ppermute | solution.py:34
  31.4 8.9 %collective-permute-start.8 = (bf16[16,512]{1,0:T(8,128)(2,1)}, bf16[16,512]{1,0:T(8,128)(2,1)S(1)}, u32[]{:S(2)}, u32[]{:S(2)}) collective-permute-start(bf16[16,512]{1,0:T(8,128)(2,1)} %shard_map.134.refs_2_), channel_id=1, source_target_pairs={{0,16},{16,0},{1,17},{17,1},{2,18},{18,2},{3,19},{19,3},{4,20},{20... | collective-permute-start | bytes 49160 | tf_op jit(solution)/shard_map/ppermute | solution.py:34
  37.6 63.5 %collective-permute-start.1 = (bf16[32,4096]{1,0:T(8,128)(2,1)}, bf16[32,4096]{1,0:T(8,128)(2,1)}, u32[]{:S(2)}, u32[]{:S(2)}) collective-permute-start(bf16[32,4096]{1,0:T(8,128)(2,1)} %get-tuple-element.29), channel_id=1, source_target_pairs={{0,16},{16,0},{1,17},{17,1},{2,18},{18,2},{3,19},{19,3},{4,20},{20... | collective-permute-start | bytes 786440 | tf_op jit(solution)/shard_map/ppermute | solution.py:34
  38.1 67.1 %collective-permute-start = (bf16[96,4096]{1,0:T(8,128)(2,1)}, bf16[96,4096]{1,0:T(8,128)(2,1)}, u32[]{:S(2)}, u32[]{:S(2)}) collective-permute-start(bf16[96,4096]{1,0:T(8,128)(2,1)} %get-tuple-element.27), channel_id=1, source_target_pairs={{0,16},{16,0},{1,17},{17,1},{2,18},{18,2},{3,19},{19,3},{4,20},{20... | collective-permute-start | bytes 2359304 | tf_op jit(solution)/shard_map/ppermute | solution.py:34
  42.9 12.0 %collective-permute-start.12 = (bf16[32,1536]{1,0:T(8,128)(2,1)}, bf16[32,1536]{1,0:T(8,128)(2,1)}, u32[]{:S(2)}, u32[]{:S(2)}) collective-permute-start(bf16[32,1536]{1,0:T(8,128)(2,1)} %get-tuple-element.40), channel_id=1, source_target_pairs={{0,2},{1,3},{2,0},{3,1},{4,6},{5,7},{6,4},{7,5},{8,10},{9,11},{10,... | collective-permute-start | bytes 294920 | tf_op jit(solution)/shard_map/ppermute | solution.py:52
  45.3 7.0 %collective-permute-start.9 = (bf16[32,1536]{1,0:T(8,128)(2,1)}, bf16[32,1536]{1,0:T(8,128)(2,1)S(1)}, u32[]{:S(2)}, u32[]{:S(2)}) collective-permute-start(bf16[32,1536]{1,0:T(8,128)(2,1)} %get-tuple-element.39), channel_id=1, source_target_pairs={{0,8},{1,9},{2,10},{3,11},{4,12},{5,13},{6,14},{7,15},{8,0},{9,1},... | collective-permute-start | bytes 294920 | tf_op jit(solution)/shard_map/ppermute | solution.py:52
  47.9 16.7 %copy-start.8 = (bf16[32,1536]{1,0:T(8,128)(2,1)S(1)}, bf16[32,1536]{1,0:T(8,128)(2,1)}, u32[]{:S(2)}) copy-start(bf16[32,1536]{1,0:T(8,128)(2,1)} %get-tuple-element.40) | copy-start | bytes 294916
  49.1 20.7 %collective-permute-start.19 = (bf16[512,512]{1,0:T(8,128)(2,1)S(1)}, bf16[512,512]{1,0:T(8,128)(2,1)S(1)}, u32[]{:S(2)}, u32[]{:S(2)}) collective-permute-start(bf16[512,512]{1,0:T(8,128)(2,1)S(1)} %constant_dynamic-slice_fusion), channel_id=1, source_target_pairs={{0,16},{1,17},{2,18},{3,19},{4,20},{5,21},{6,22},{7,23},{24,8},{25... | collective-permute-start | bytes 1572872 | tf_op jit(solution)/shard_map/ppermute | solution.py:606
  52.3 29.7 %copy-start.17 = (f32[512]{0:T(512)}, f32[512]{0:T(512)S(1)}, u32[]{:S(2)}) copy-start(f32[512]{0:T(512)S(1)} %dynamic_slice.7) | copy-start | bytes 6148
  53.2 7.8 %collective-permute-start.10 = (bf16[64,1536]{1,0:T(8,128)(2,1)S(1)}, bf16[64,1536]{1,0:T(8,128)(2,1)S(1)}, u32[]{:S(2)}, u32[]{:S(2)}) collective-permute-start(bf16[64,1536]{1,0:T(8,128)(2,1)S(1)} %pad_maximum_fusion.4), channel_id=1, source_target_pairs={{0,4},{1,5},{2,6},{3,7},{4,0},{5,1},{6,2},{7,3},{8,12},{9,13},{10,... | collective-permute-start | bytes 589832 | tf_op jit(solution)/shard_map/ppermute | solution.py:52
  55.8 8.8 %collective-permute-start.13 = (bf16[64,1536]{1,0:T(8,128)(2,1)S(1)}, bf16[64,1536]{1,0:T(8,128)(2,1)S(1)}, u32[]{:S(2)}, u32[]{:S(2)}) collective-permute-start(bf16[64,1536]{1,0:T(8,128)(2,1)S(1)} %pad_maximum_fusion.5), channel_id=1, source_target_pairs={{0,8},{1,9},{2,10},{3,11},{4,12},{5,13},{6,14},{7,15},{8,0},{9,1},... | collective-permute-start | bytes 589832 | tf_op jit(solution)/shard_map/ppermute | solution.py:52
  62.0 12.5 %copy-start.7 = (bf16[32,1536]{1,0:T(8,128)(2,1)S(1)}, bf16[32,1536]{1,0:T(8,128)(2,1)}, u32[]{:S(2)}) copy-start(bf16[32,1536]{1,0:T(8,128)(2,1)} %get-tuple-element.39) | copy-start | bytes 294916
  62.0 12.5 %collective-permute-start.11 = (bf16[128,1536]{1,0:T(8,128)(2,1)S(1)}, bf16[128,1536]{1,0:T(8,128)(2,1)S(1)}, u32[]{:S(2)}, u32[]{:S(2)}) collective-permute-start(bf16[128,1536]{1,0:T(8,128)(2,1)S(1)} %pad_maximum_fusion.2), channel_id=1, source_target_pairs={{0,2},{1,3},{2,0},{3,1},{4,6},{5,7},{6,4},{7,5},{8,10},{9,11},{10,... | collective-permute-start | bytes 1179656 | tf_op jit(solution)/shard_map/ppermute | solution.py:52
  65.6 7.8 %collective-permute-start.14 = (bf16[128,1536]{1,0:T(8,128)(2,1)S(1)}, bf16[128,1536]{1,0:T(8,128)(2,1)S(1)}, u32[]{:S(2)}, u32[]{:S(2)}) collective-permute-start(bf16[128,1536]{1,0:T(8,128)(2,1)S(1)} %pad_maximum_fusion.3), channel_id=1, source_target_pairs={{0,4},{1,5},{2,6},{3,7},{4,0},{5,1},{6,2},{7,3},{8,12},{9,13},{10,... | collective-permute-start | bytes 1179656 | tf_op jit(solution)/shard_map/ppermute | solution.py:52
  70.9 11.1 %copy-start.3 = (bf16[512,512]{1,0:T(8,128)(2,1)}, bf16[512,512]{1,0:T(8,128)(2,1)S(1)}, u32[]{:S(2)}) copy-start(bf16[512,512]{1,0:T(8,128)(2,1)S(1)} %select_add_fusion.refs_6_) | copy-start | bytes 1572868
  74.6 3.1 %collective-permute-start.18 = (bf16[256,512]{1,0:T(8,128)(2,1)S(1)}, bf16[256,512]{1,0:T(8,128)(2,1)S(1)}, u32[]{:S(2)}, u32[]{:S(2)}) collective-permute-start(bf16[256,512]{1,0:T(8,128)(2,1)S(1)} %slice.67), channel_id=1, source_target_pairs={{0,1},{1,0},{2,3},{3,2},{4,5},{5,4},{6,7},{7,6},{8,9},{9,8},{10,11... | collective-permute-start | bytes 786440 | tf_op jit(solution)/shard_map/ppermute | solution.py:79
  74.7 3.8 %collective-permute-start.15 = (bf16[256,2560]{1,0:T(8,128)(2,1)S(1)}, bf16[256,2560]{1,0:T(8,128)(2,1)S(1)}, u32[]{:S(2)}, u32[]{:S(2)}) collective-permute-start(bf16[256,2560]{1,0:T(8,128)(2,1)S(1)} %pad_maximum_fusion), channel_id=1, source_target_pairs={{0,1},{1,0},{2,3},{3,2},{4,5},{5,4},{6,7},{7,6},{8,9},{9,8},{10,11... | collective-permute-start | bytes 3932168 | tf_op jit(solution)/shard_map/ppermute | solution.py:78
  76.9 9.2 %collective-permute-start.16 = (bf16[256,512]{1,0:T(8,128)(2,1)S(1)}, bf16[256,512]{1,0:T(8,128)(2,1)S(1)}, u32[]{:S(2)}, u32[]{:S(2)}) collective-permute-start(bf16[256,512]{1,0:T(8,128)(2,1)S(1)} %get-tuple-element.56), channel_id=1, source_target_pairs={{0,16},{16,0},{1,17},{17,1},{2,18},{18,2},{3,19},{19,3},{4,20},{20... | collective-permute-start | bytes 786440 | tf_op jit(solution)/shard_map/ppermute | solution.py:34
  78.5 5.0 %copy-start.6 = (bf16[256,2560]{1,0:T(8,128)(2,1)}, bf16[256,2560]{1,0:T(8,128)(2,1)S(1)}, u32[]{:S(2)}) copy-start(bf16[256,2560]{1,0:T(8,128)(2,1)S(1)} %collective-permute-done.15) | copy-start | bytes 3932164
  80.1 10.7 %collective-permute-start.17 = (bf16[256,512]{1,0:T(8,128)(2,1)S(1)}, bf16[256,512]{1,0:T(8,128)(2,1)}, u32[]{:S(2)}, u32[]{:S(2)}) collective-permute-start(bf16[256,512]{1,0:T(8,128)(2,1)S(1)} %get-tuple-element.58), channel_id=1, source_target_pairs={{0,16},{16,0},{1,17},{17,1},{2,18},{18,2},{3,19},{19,3},{4,20},{20... | collective-permute-start | bytes 786440 | tf_op jit(solution)/shard_map/ppermute | solution.py:34
  82.0 19.0 %copy-start.12 = (bf16[32,4096]{1,0:T(8,128)(2,1)S(1)}, bf16[32,4096]{1,0:T(8,128)(2,1)}, u32[]{:S(2)}) copy-start(bf16[32,4096]{1,0:T(8,128)(2,1)} %get-tuple-element.28) | copy-start | bytes 786436
  95.8 17.4 %all-to-all-start = ((bf16[16,24,512]{2,1,0:T(8,128)(2,1)}), bf16[16,24,512]{2,1,0:T(8,128)(2,1)S(1)}, u32[]{:S(2)}, u32[]{:S(2)}) async-start(bf16[16,24,512]{2,1,0:T(8,128)(2,1)} %get-tuple-element.46), calls=%async_computation | async-start | bytes 786432 | tf_op jit(solution)/shard_map/all_to_all | solution.py:640
  105.0 17.5 %collective-permute-start.3 = (bf16[32,512]{1,0:T(8,128)(2,1)}, bf16[32,512]{1,0:T(8,128)(2,1)}, u32[]{:S(2)}, u32[]{:S(2)}) collective-permute-start(bf16[32,512]{1,0:T(8,128)(2,1)} %slice.78), channel_id=1, source_target_pairs={{0,16},{16,0},{1,17},{17,1},{2,18},{18,2},{3,19},{19,3},{4,20},{20... | collective-permute-start | bytes 98312 | tf_op jit(solution)/shard_map/ppermute | solution.py:34
  107.6 14.8 %copy-start.11 = (f32[192,512]{1,0:T(8,128)}, f32[192,512]{1,0:T(8,128)S(1)}, u32[]{:S(2)}) copy-start(f32[192,512]{1,0:T(8,128)S(1)} %fusion.4.refs_0_) | copy-start | bytes 1179652
  108.4 14.1 %collective-permute-start.2 = (bf16[96,512]{1,0:T(8,128)(2,1)}, bf16[96,512]{1,0:T(8,128)(2,1)S(1)}, u32[]{:S(2)}, u32[]{:S(2)}) collective-permute-start(bf16[96,512]{1,0:T(8,128)(2,1)} %slice.77), channel_id=1, source_target_pairs={{0,16},{16,0},{1,17},{17,1},{2,18},{18,2},{3,19},{19,3},{4,20},{20... | collective-permute-start | bytes 294920 | tf_op jit(solution)/shard_map/ppermute | solution.py:34
  (12 other events, 25.1 us)

commit v7 on v6

--- a/solution.py
+++ b/solution.py
@@ -88,8 +88,8 @@
         start = start_ref[0, o]
         here = (start >= own * tokens) & (start < (own + 1) * tokens)
         first = jnp.where(here, start, first)
-        cols = jnp.where(here, grid_ref[0, o, 1], cols)
-        count = jnp.where(here, grid_ref[0, o, 0] * grid_ref[0, o, 1], count)
+        cols = jnp.where(here, grid_ref[1, o], cols)
+        count = jnp.where(here, grid_ref[0, o] * grid_ref[1, o], count)
         owner = jnp.where(here, o, owner)
     return first, cols, count, owner
 
@@ -564,7 +564,7 @@
 
     mine, sent = project(parts, index, images, vit_norm_gain.reshape(1, -1), vit_qkv)
 
-    sent, grid, start = barrier((sent, image_grid, image_start))
+    sent, grid, start = barrier((sent, image_grid[0].T, image_start))
     received = [shift(sent[k - 1], k) for k in others]
     angles = angle_table(tokens, groups, capacity, index, grid, start)
     cosine, sines = jnp.cos(angles), jnp.sin(angles)
@@ -650,7 +650,7 @@
         parts,
         groups,
         index,
-        image_grid,
+        image_grid[0].T,
         image_start,
         [early_terms, late_terms],
         returned,

time: 127 us -> 126 us (level)
  local copies, waits for them, and re-layouts: 13.9 us -> 12.5 us
    unnamed x54 -> x51, local copies, waits for them, and re-layouts: 6.03 us -> 5.33 us
  transfers between devices with their start and end apart: 21 -> 21, of which waited for: 9 -> 9; matrix products, arithmetic and copies ran while one was open for 28% -> 27% of each run, Pallas kernels for 17% -> 17%
where the time goes in v7:
time: 126 us
  waiting for transfers between devices  29.6 us (23%)
  starting transfers between devices  29.2 us (23%)
  Pallas kernels  27.6 us (22%)
  matrix products  17.6 us (14%)
  local copies, waits for them, and re-layouts  12.5 us (10%)
  other arithmetic  8.01 us (6%)
    pallas_call x8, Pallas kernels, call(): pl.pallas_call(kernel, out_shape=outs, in_specs=[SMEM] * scalars + [VMEM]...  22.9 us
    ppermute x11, waiting for transfers between devices, shift(): return lax.ppermute(x, 'dp', [(i, (i + k) % size) for i in range(size)])  15.1 us
    ppermute x11, starting transfers between devices, shift(): return lax.ppermute(x, 'dp', [(i, (i + k) % size) for i in range(size)])  11.5 us
    dot_general x5, matrix products, dot(): return jnp.dot(a, b, preferred_element_type=F32, **kw)  10 us
    ppermute x6, starting transfers between devices, xor_gather(): lax.ppermute(joined, 'ctx', [(i, i ^ stride) for i in range(size)])  8.83 us
    ppermute x6, waiting for transfers between devices, xor_gather(): lax.ppermute(joined, 'ctx', [(i, i ^ stride) for i in range(size)])  6.73 us
    all_to_all x1, starting transfers between devices, on_device(): arrived = lax.all_to_all(outgoing, 'ctx', 0, 0, tiled=True)  5.88 us
    dot_general x1, matrix products, on_device(): lax.dot_general(joined, grad_embedded, (((0,), (0,)), ((), ())), preferre...  5.75 us
  transfers between devices with their start and end apart: 21, of which 9 were waited for; matrix products, arithmetic and copies ran while one was open for 27% of the time, Pallas kernels for 17%

profile of v7, /device:TPU:0, one launch (start us, length us, event | category | flops | bytes accessed | tf_op | source)
XLA Modules:
  0.0 125.5 jit_solution(5643113479219348264)
XLA Ops:
  1.5 3.0 %collective-permute-start.4 = (s32[3,16]{1,0:T(4,128)S(1)}, s32[3,16]{1,0:T(4,128)S(1)}, u32[]{:S(2)}, u32[]{:S(2)}) collective-permute-start(s32[3,16]{1,0:T(4,128)S(1)} %get-tuple-element.55), channel_id=1, source_target_pairs={{0,16},{16,0},{1,17},{17,1},{2,18},{18,2},{3,19},{19,3},{4,20},{20... | collective-permute-start | bytes 584 | tf_op jit(solution)/shard_map/ppermute | solution.py:34
  8.2 3.2 %collective-permute-done.5.refs_1_.refs_3_ = bf16[64,1280]{1,0:T(8,128)(2,1)S(1)} collective-permute-done((bf16[64,1280]{1,0:T(8,128)(2,1)S(1)}, bf16[64,1280]{1,0:T(8,128)(2,1)S(1)}, u32[]{:S(2)}, u32[]{:S(2)}) %collective-permute-start.5) | collective-permute-done | bytes 163872 | tf_op jit(solution)/shard_map/ppermute | solution.py:34
  12.0 3.8 %shard_map.131 = (f32[2,64,960]{2,1,0:T(8,128)}, bf16[1,2,64,960]{3,2,1,0:T(8,128)(2,1)}) custom-call(s32[2]{0:T(128)} %pad_add_fusion.2.index_ref, bf16[64,1280]{1,0:T(8,128)(2,1)} %copy-done.5, bf16[64,1280]{1,0:T(8,128)(2,1)} %copy-done.10, f32[1,1280]{1,0:T(1,128)} %reshape.108.refs_2_, bf16[640,1920]{1,0:T(8,128)(2,1)} %refs_3_.1), custom_call_target="tpu_custom_call" | custom-call | tf_op jit(solution)/shard_map/pallas_call | solution.py:102
  16.9 1.5 %shard_map.133 = f32[128,128]{1,0:T(8,128)} custom-call(s32[2]{0:T(128)} %pad_add_fusion.2.index_ref, s32[2,16]{1,0:T(2,128)} %bitcast.48, s32[1,16]{1,0:T(1,128)} %start_ref.3, f32[1,128]{1,0:T(1,128)} %fusion.27.inverse_ref), custom_call_target="tpu_custom_call" | custom-call | tf_op jit(solution)/shard_map/pallas_call | solution.py:102
  18.4 4.5 %collective-permute-done.6.refs_1_ = bf16[2,64,960]{2,1,0:T(8,128)(2,1)S(1)} collective-permute-done((bf16[2,64,960]{2,1,0:T(8,128)(2,1)}, bf16[2,64,960]{2,1,0:T(8,128)(2,1)S(1)}, u32[]{:S(2)}, u32[]{:S(2)}) %collective-permute-start.6) | collective-permute-done | bytes 245792 | tf_op jit(solution)/shard_map/ppermute | solution.py:34
  23.6 3.5 %shard_map.132 = (f32[2,32,1280]{2,1,0:T(8,128)}, bf16[1,2,32,1280]{3,2,1,0:T(8,128)(2,1)}) custom-call(s32[3]{0:T(128)} %pad_add_fusion.3.scalar_ref, f32[2,64,960]{2,1,0:T(8,128)} %get-tuple-element.30.refs_0_, bf16[2,64,960]{2,1,0:T(8,128)(2,1)} %copy-done.14, bf16[64,1280]{1,0:T(8,128)(2,1)} %copy-done.5, bf16[64,1280]{1,0:T(8,128)(2,1)} %copy-done.10, ...), custom_call_target="tpu_custom_call" | custom-call | tf_op jit(solution)/shard_map/pallas_call | solution.py:102
  27.7 1.7 %fusion.32 = (f32[128,128]{1,0:T(8,128)}, f32[128,128]{1,0:T(8,128)}) fusion(f32[128,128]{1,0:T(8,128)} %shard_map.133), kind=kLoop, calls=%fused_computation.75 | loop fusion | bytes 196608 | tf_op jit(solution)/shard_map/sin | solution.py:570
  29.5 1.9 %shard_map.134.refs_2_ = bf16[16,512]{1,0:T(8,128)(2,1)} custom-call(s32[2]{0:T(128)} %pad_add_fusion.2.index_ref, s32[2,16]{1,0:T(2,128)} %bitcast.49, s32[1,16]{1,0:T(1,128)} %start_ref.3, bf16[128,512]{1,0:T(8,128)(2,1)} %bitcast.43, f32[128,128]{1,0:T(8,128)} %get-tuple-element.51.cosine_ref.refs_6_, f32[128,128]{1,0:T(8,128)} %get-tuple-element.50.sine_ref.refs_7_), custom_call_target="tpu_custom_call" | custom-call | tf_op jit(solution)/shard_map/pallas_call | solution.py:102
  32.8 4.7 %text_norm.1 = (bf16[96,4096]{1,0:T(8,128)(2,1)}, bf16[96,4096]{1,0:T(8,128)(2,1)}, bf16[32,4096]{1,0:T(8,128)(2,1)}, bf16[32,4096]{1,0:T(8,128)(2,1)}) custom-call(s32[2]{0:T(128)} %pad_add_fusion.2.index_ref, bf16[128,8192]{1,0:T(8,128)(2,1)} %bitcast.41, f32[1,8192]{1,0:T(1,128)} %bitcast.45), custom_call_target="tpu_custom_call" | custom-call | tf_op jit(solution)/shard_map/text_norm/pallas_call | solution.py:506
  40.2 2.0 %shard_map.135 = (bf16[32,1536]{1,0:T(8,128)(2,1)}, bf16[32,1536]{1,0:T(8,128)(2,1)}) custom-call(s32[2]{0:T(128)} %copy-done.20, f32[2,32,1280]{2,1,0:T(8,128)} %get-tuple-element.33.refs_0_, bf16[2,32,1280]{2,1,0:T(8,128)(2,1)} %copy-done.15, bf16[16,512]{1,0:T(8,128)(2,1)} %shard_map.134.refs_2_, bf16[16,512]{1,0:T(8,128)(2,1)} %copy-done.18), custom_call_target="tpu_custom_call" | custom-call | tf_op jit(solution)/shard_map/pallas_call | solution.py:102
  42.2 1.5 %collective-permute-start.12 = (bf16[32,1536]{1,0:T(8,128)(2,1)}, bf16[32,1536]{1,0:T(8,128)(2,1)}, u32[]{:S(2)}, u32[]{:S(2)}) collective-permute-start(bf16[32,1536]{1,0:T(8,128)(2,1)} %get-tuple-element.40), channel_id=1, source_target_pairs={{0,2},{1,3},{2,0},{3,1},{4,6},{5,7},{6,4},{7,5},{8,10},{9,11},{10,... | collective-permute-start | bytes 294920 | tf_op jit(solution)/shard_map/ppermute | solution.py:52
  44.6 2.6 %collective-permute-start.9 = (bf16[32,1536]{1,0:T(8,128)(2,1)}, bf16[32,1536]{1,0:T(8,128)(2,1)S(1)}, u32[]{:S(2)}, u32[]{:S(2)}) collective-permute-start(bf16[32,1536]{1,0:T(8,128)(2,1)} %get-tuple-element.39), channel_id=1, source_target_pairs={{0,8},{1,9},{2,10},{3,11},{4,12},{5,13},{6,14},{7,15},{8,0},{9,1},... | collective-permute-start | bytes 294920 | tf_op jit(solution)/shard_map/ppermute | solution.py:52
  48.3 2.5 %collective-permute-start.19 = (bf16[512,512]{1,0:T(8,128)(2,1)S(1)}, bf16[512,512]{1,0:T(8,128)(2,1)S(1)}, u32[]{:S(2)}, u32[]{:S(2)}) collective-permute-start(bf16[512,512]{1,0:T(8,128)(2,1)S(1)} %constant_dynamic-slice_fusion), channel_id=1, source_target_pairs={{0,16},{1,17},{2,18},{3,19},{4,20},{5,21},{6,22},{7,23},{24,8},{25... | collective-permute-start | bytes 1572872 | tf_op jit(solution)/shard_map/ppermute | solution.py:606
  52.5 1.6 %collective-permute-start.10 = (bf16[64,1536]{1,0:T(8,128)(2,1)S(1)}, bf16[64,1536]{1,0:T(8,128)(2,1)S(1)}, u32[]{:S(2)}, u32[]{:S(2)}) collective-permute-start(bf16[64,1536]{1,0:T(8,128)(2,1)S(1)} %pad_maximum_fusion.4), channel_id=1, source_target_pairs={{0,4},{1,5},{2,6},{3,7},{4,0},{5,1},{6,2},{7,3},{8,12},{9,13},{10,... | collective-permute-start | bytes 589832 | tf_op jit(solution)/shard_map/ppermute | solution.py:52
  55.1 2.5 %collective-permute-start.13 = (bf16[64,1536]{1,0:T(8,128)(2,1)S(1)}, bf16[64,1536]{1,0:T(8,128)(2,1)S(1)}, u32[]{:S(2)}, u32[]{:S(2)}) collective-permute-start(bf16[64,1536]{1,0:T(8,128)(2,1)S(1)} %pad_maximum_fusion.5), channel_id=1, source_target_pairs={{0,8},{1,9},{2,10},{3,11},{4,12},{5,13},{6,14},{7,15},{8,0},{9,1},... | collective-permute-start | bytes 589832 | tf_op jit(solution)/shard_map/ppermute | solution.py:52
  57.6 2.8 %collective-permute-done.10 = bf16[64,1536]{1,0:T(8,128)(2,1)S(1)} collective-permute-done((bf16[64,1536]{1,0:T(8,128)(2,1)S(1)}, bf16[64,1536]{1,0:T(8,128)(2,1)S(1)}, u32[]{:S(2)}, u32[]{:S(2)}) %collective-permute-start.10) | collective-permute-done | bytes 196640 | tf_op jit(solution)/shard_map/ppermute | solution.py:52
  61.8 2.1 %collective-permute-done.13 = bf16[64,1536]{1,0:T(8,128)(2,1)S(1)} collective-permute-done((bf16[64,1536]{1,0:T(8,128)(2,1)S(1)}, bf16[64,1536]{1,0:T(8,128)(2,1)S(1)}, u32[]{:S(2)}, u32[]{:S(2)}) %collective-permute-start.13) | collective-permute-done | bytes 196640 | tf_op jit(solution)/shard_map/ppermute | solution.py:52
  65.0 4.7 %collective-permute-done.19 = bf16[512,512]{1,0:T(8,128)(2,1)S(1)} collective-permute-done((bf16[512,512]{1,0:T(8,128)(2,1)S(1)}, bf16[512,512]{1,0:T(8,128)(2,1)S(1)}, u32[]{:S(2)}, u32[]{:S(2)}) %collective-permute-start.19) | collective-permute-done | bytes 524320 | tf_op jit(solution)/shard_map/ppermute | solution.py:606
  70.9 1.8 %collective-permute-done.14 = bf16[128,1536]{1,0:T(8,128)(2,1)S(1)} collective-permute-done((bf16[128,1536]{1,0:T(8,128)(2,1)S(1)}, bf16[128,1536]{1,0:T(8,128)(2,1)S(1)}, u32[]{:S(2)}, u32[]{:S(2)}) %collective-permute-start.14) | collective-permute-done | bytes 393248 | tf_op jit(solution)/shard_map/ppermute | solution.py:52
  74.5 1.6 %fusion.33 = (bf16[256,512]{1,0:T(8,128)(2,1)S(1)}, f32[256,512]{1,0:T(8,128)}) fusion(bf16[256,2560]{1,0:T(8,128)(2,1)S(1)} %pad_maximum_fusion, bf16[2560,512]{1,0:T(8,128)(2,1)S(1)} %copy-done), kind=kOutput, calls=%fused_computation.76 | convolution fusion | flops 671219712 | bytes 4718592 | tf_op jit(solution)/shard_map/dot_general | solution.py:29
  78.5 1.6 %fusion.34 = (bf16[256,512]{1,0:T(8,128)(2,1)S(1)}, f32[256,512]{1,0:T(8,128)}) fusion(bf16[256,2560]{1,0:T(8,128)(2,1)S(1)} %collective-permute-done.15, bf16[2560,512]{1,0:T(8,128)(2,1)S(1)} %copy-done), kind=kOutput, calls=%fused_computation.77 | convolution fusion | flops 671219712 | bytes 4718592 | tf_op jit(solution)/shard_map/dot_general | solution.py:29
  82.8 2.6 %collective-permute-done.16.refs_2_ = bf16[256,512]{1,0:T(8,128)(2,1)S(1)} collective-permute-done((bf16[256,512]{1,0:T(8,128)(2,1)S(1)}, bf16[256,512]{1,0:T(8,128)(2,1)S(1)}, u32[]{:S(2)}, u32[]{:S(2)}) %collective-permute-start.16) | collective-permute-done | bytes 262176 | tf_op jit(solution)/shard_map/ppermute | solution.py:34
  85.3 4.8 %collective-permute-done.17.refs_3_ = bf16[256,512]{1,0:T(8,128)(2,1)} collective-permute-done((bf16[256,512]{1,0:T(8,128)(2,1)S(1)}, bf16[256,512]{1,0:T(8,128)(2,1)}, u32[]{:S(2)}, u32[]{:S(2)}) %collective-permute-start.17) | collective-permute-done | bytes 262176 | tf_op jit(solution)/shard_map/ppermute | solution.py:34
  90.2 4.9 %shard_map.136 = (bf16[512,512]{1,0:T(8,128)(2,1)}, bf16[16,24,512]{2,1,0:T(8,128)(2,1)}) custom-call(s32[16]{0:T(128)} %copy-done.19, s32[16]{0:T(128)} %slice_bitcast_fusion.holder_ref, f32[256,512]{1,0:T(8,128)} %get-tuple-element.57.refs_0_, f32[256,512]{1,0:T(8,128)} %get-tuple-element.59.refs_1_, bf16[256,512]{1,0:T(8,128)(2,1)} %copy-done.13, ...), custom_call_target="tpu_custom_call" | custom-call | tf_op jit(solution)/shard_map/pallas_call | solution.py:102
  95.1 5.9 %all-to-all-start = ((bf16[16,24,512]{2,1,0:T(8,128)(2,1)}), bf16[16,24,512]{2,1,0:T(8,128)(2,1)S(1)}, u32[]{:S(2)}, u32[]{:S(2)}) async-start(bf16[16,24,512]{2,1,0:T(8,128)(2,1)} %get-tuple-element.46), calls=%async_computation | async-start | bytes 786432 | tf_op jit(solution)/shard_map/all_to_all | solution.py:640
  101.0 3.2 %fusion.9.refs_1_ = f32[64,512]{1,0:T(8,128)S(1)} fusion(bf16[4096,512]{1,0:T(8,128)(2,1)} %param.19, bf16[32,4096]{1,0:T(8,128)(2,1)} %collective-permute-done.1, bf16[32,4096]{1,0:T(8,128)(2,1)S(1)} %copy-done.12), kind=kOutput, calls=%fused_computation.13 | convolution fusion | flops 269484032 | bytes 4849664 | tf_op jit(solution)/shard_map/dot_general | solution.py:29
  105.2 2.3 %fusion.4.refs_0_ = f32[192,512]{1,0:T(8,128)S(1)} fusion(bf16[4096,512]{1,0:T(8,128)(2,1)S(1)} %copy-done.1, bf16[96,4096]{1,0:T(8,128)(2,1)} %collective-permute-done, bf16[96,4096]{1,0:T(8,128)(2,1)} %get-tuple-element.26), kind=kOutput, calls=%fused_computation.5 | convolution fusion | flops 808452096 | bytes 6160384 | tf_op jit(solution)/shard_map/dot_general | solution.py:29
  108.3 1.8 %collective-permute-start.2 = (bf16[96,512]{1,0:T(8,128)(2,1)}, bf16[96,512]{1,0:T(8,128)(2,1)S(1)}, u32[]{:S(2)}, u32[]{:S(2)}) collective-permute-start(bf16[96,512]{1,0:T(8,128)(2,1)} %slice.77), channel_id=1, source_target_pairs={{0,16},{16,0},{1,17},{17,1},{2,18},{18,2},{3,19},{19,3},{4,20},{20... | collective-permute-start | bytes 294920 | tf_op jit(solution)/shard_map/ppermute | solution.py:34
  110.1 3.1 %all-to-all-done.sums_ref.refs_4_ = bf16[16,24,512]{2,1,0:T(8,128)(2,1)S(1)} async-done(((bf16[16,24,512]{2,1,0:T(8,128)(2,1)}), bf16[16,24,512]{2,1,0:T(8,128)(2,1)S(1)}, u32[]{:S(2)}, u32[]{:S(2)}) %all-to-all-start) | async-done | bytes 393248 | tf_op jit(solution)/shard_map/all_to_all | solution.py:640
  113.9 2.8 %shard_map.137 = (f32[8,512]{1,0:T(8,128)}, bf16[512,512]{1,0:T(8,128)(2,1)}) custom-call(s32[16]{0:T(128)} %copy-done.19, bf16[16,24,512]{2,1,0:T(8,128)(2,1)} %copy-done.4, bf16[512,512]{1,0:T(8,128)(2,1)} %get-tuple-element.47.embed_ref, f32[512,512]{1,0:T(8,128)} %convolution_multiply_fusion.refs_4_.weighted_ref), custom_call_target="tpu_custom_call" | custom-call | tf_op jit(solution)/shard_map/pallas_call | solution.py:102
  116.7 5.7 %fusion = f32[2560,512]{1,0:T(8,128)} fusion(bf16[512,512]{1,0:T(8,128)(2,1)} %get-tuple-element.49, bf16[256,2560]{1,0:T(8,128)(2,1)} %copy-done.6, bf16[256,2560]{1,0:T(8,128)(2,1)} %copy-done.2), kind=kOutput, calls=%fused_computation | convolution fusion | flops 1347420160 | bytes 8388608 | tf_op jit(solution)/shard_map/dot_general | solution.py:646
  123.0 2.5 %shard_map.138 = bf16[128,512]{1,0:T(8,128)(2,1)} custom-call(s32[2]{0:T(128)} %pad_add_fusion.2.index_ref, s32[2,16]{1,0:T(2,128)} %bitcast.50, s32[1,16]{1,0:T(1,128)} %start_ref.3, f32[192,512]{1,0:T(8,128)} %copy-done.11, f32[64,512]{1,0:T(8,128)} %copy-done.9, bf16[96,512]{1,0:T(8,128)(2,1)} %copy-done.16, ...), custom_call_target="tpu_custom_call" | custom-call | tf_op jit(solution)/shard_map/pallas_call | solution.py:102
  (107 shorter events, 29.8 us)
Async XLA Ops:
  0.6 73.9 %copy-start = (bf16[2560,512]{1,0:T(8,128)(2,1)S(1)}, bf16[2560,512]{1,0:T(8,128)(2,1)}, u32[]{:S(2)}) copy-start(bf16[2560,512]{1,0:T(8,128)(2,1)} %param.16) | copy-start | bytes 7864324
  1.5 14.6 %collective-permute-start.4 = (s32[3,16]{1,0:T(4,128)S(1)}, s32[3,16]{1,0:T(4,128)S(1)}, u32[]{:S(2)}, u32[]{:S(2)}) collective-permute-start(s32[3,16]{1,0:T(4,128)S(1)} %get-tuple-element.55), channel_id=1, source_target_pairs={{0,16},{16,0},{1,17},{17,1},{2,18},{18,2},{3,19},{19,3},{4,20},{20... | collective-permute-start | bytes 584 | tf_op jit(solution)/shard_map/ppermute | solution.py:34
  5.6 5.7 %copy-start.5 = (bf16[64,1280]{1,0:T(8,128)(2,1)}, bf16[64,1280]{1,0:T(8,128)(2,1)S(1)}, u32[]{:S(2)}) copy-start(bf16[64,1280]{1,0:T(8,128)(2,1)S(1)} %convolution_convert_fusion.refs_0_.refs_2_) | copy-start | bytes 491524
  5.6 5.7 %collective-permute-start.5 = (bf16[64,1280]{1,0:T(8,128)(2,1)S(1)}, bf16[64,1280]{1,0:T(8,128)(2,1)S(1)}, u32[]{:S(2)}, u32[]{:S(2)}) collective-permute-start(bf16[64,1280]{1,0:T(8,128)(2,1)S(1)} %convolution_convert_fusion.refs_0_.refs_2_), channel_id=1, source_target_pairs={{0,16},{16,0},{1,17},{17,1},{2,18},{18,2},{3,19},{19,3},{4,20},{20... | collective-permute-start | bytes 491528 | tf_op jit(solution)/shard_map/ppermute | solution.py:34
  15.8 7.1 %collective-permute-start.6 = (bf16[2,64,960]{2,1,0:T(8,128)(2,1)}, bf16[2,64,960]{2,1,0:T(8,128)(2,1)S(1)}, u32[]{:S(2)}, u32[]{:S(2)}) collective-permute-start(bf16[2,64,960]{2,1,0:T(8,128)(2,1)} %bitcast.54), channel_id=1, source_target_pairs={{0,16},{16,0},{1,17},{17,1},{2,18},{18,2},{3,19},{19,3},{4,20},{20... | collective-permute-start | bytes 737288 | tf_op jit(solution)/shard_map/ppermute | solution.py:34
  16.3 23.3 %copy-start.20 = (s32[2]{0:T(128)}, s32[2]{0:T(128)S(1)}, u32[]{:S(2)}) copy-start(s32[2]{0:T(128)S(1)} %select_reduce_fusion.count_ref) | copy-start | bytes 28
  27.1 12.4 %collective-permute-start.7 = (bf16[2,32,1280]{2,1,0:T(8,128)(2,1)}, bf16[2,32,1280]{2,1,0:T(8,128)(2,1)S(1)}, u32[]{:S(2)}, u32[]{:S(2)}) collective-permute-start(bf16[2,32,1280]{2,1,0:T(8,128)(2,1)} %bitcast.55), channel_id=1, source_target_pairs={{0,16},{16,0},{1,17},{17,1},{2,18},{18,2},{3,19},{19,3},{4,20},{20... | collective-permute-start | bytes 491528 | tf_op jit(solution)/shard_map/ppermute | solution.py:34
  31.4 8.2 %collective-permute-start.8 = (bf16[16,512]{1,0:T(8,128)(2,1)}, bf16[16,512]{1,0:T(8,128)(2,1)S(1)}, u32[]{:S(2)}, u32[]{:S(2)}) collective-permute-start(bf16[16,512]{1,0:T(8,128)(2,1)} %shard_map.134.refs_2_), channel_id=1, source_target_pairs={{0,16},{16,0},{1,17},{17,1},{2,18},{18,2},{3,19},{19,3},{4,20},{20... | collective-permute-start | bytes 49160 | tf_op jit(solution)/shard_map/ppermute | solution.py:34
  37.5 63.5 %collective-permute-start.1 = (bf16[32,4096]{1,0:T(8,128)(2,1)}, bf16[32,4096]{1,0:T(8,128)(2,1)}, u32[]{:S(2)}, u32[]{:S(2)}) collective-permute-start(bf16[32,4096]{1,0:T(8,128)(2,1)} %get-tuple-element.29), channel_id=1, source_target_pairs={{0,16},{16,0},{1,17},{17,1},{2,18},{18,2},{3,19},{19,3},{4,20},{20... | collective-permute-start | bytes 786440 | tf_op jit(solution)/shard_map/ppermute | solution.py:34
  38.1 67.1 %collective-permute-start = (bf16[96,4096]{1,0:T(8,128)(2,1)}, bf16[96,4096]{1,0:T(8,128)(2,1)}, u32[]{:S(2)}, u32[]{:S(2)}) collective-permute-start(bf16[96,4096]{1,0:T(8,128)(2,1)} %get-tuple-element.27), channel_id=1, source_target_pairs={{0,16},{16,0},{1,17},{17,1},{2,18},{18,2},{3,19},{19,3},{4,20},{20... | collective-permute-start | bytes 2359304 | tf_op jit(solution)/shard_map/ppermute | solution.py:34
  42.2 12.0 %collective-permute-start.12 = (bf16[32,1536]{1,0:T(8,128)(2,1)}, bf16[32,1536]{1,0:T(8,128)(2,1)}, u32[]{:S(2)}, u32[]{:S(2)}) collective-permute-start(bf16[32,1536]{1,0:T(8,128)(2,1)} %get-tuple-element.40), channel_id=1, source_target_pairs={{0,2},{1,3},{2,0},{3,1},{4,6},{5,7},{6,4},{7,5},{8,10},{9,11},{10,... | collective-permute-start | bytes 294920 | tf_op jit(solution)/shard_map/ppermute | solution.py:52
  44.6 6.9 %collective-permute-start.9 = (bf16[32,1536]{1,0:T(8,128)(2,1)}, bf16[32,1536]{1,0:T(8,128)(2,1)S(1)}, u32[]{:S(2)}, u32[]{:S(2)}) collective-permute-start(bf16[32,1536]{1,0:T(8,128)(2,1)} %get-tuple-element.39), channel_id=1, source_target_pairs={{0,8},{1,9},{2,10},{3,11},{4,12},{5,13},{6,14},{7,15},{8,0},{9,1},... | collective-permute-start | bytes 294920 | tf_op jit(solution)/shard_map/ppermute | solution.py:52
  47.2 16.7 %copy-start.8 = (bf16[32,1536]{1,0:T(8,128)(2,1)S(1)}, bf16[32,1536]{1,0:T(8,128)(2,1)}, u32[]{:S(2)}) copy-start(bf16[32,1536]{1,0:T(8,128)(2,1)} %get-tuple-element.40) | copy-start | bytes 294916
  48.3 21.3 %collective-permute-start.19 = (bf16[512,512]{1,0:T(8,128)(2,1)S(1)}, bf16[512,512]{1,0:T(8,128)(2,1)S(1)}, u32[]{:S(2)}, u32[]{:S(2)}) collective-permute-start(bf16[512,512]{1,0:T(8,128)(2,1)S(1)} %constant_dynamic-slice_fusion), channel_id=1, source_target_pairs={{0,16},{1,17},{2,18},{3,19},{4,20},{5,21},{6,22},{7,23},{24,8},{25... | collective-permute-start | bytes 1572872 | tf_op jit(solution)/shard_map/ppermute | solution.py:606
  51.6 29.7 %copy-start.17 = (f32[512]{0:T(512)}, f32[512]{0:T(512)S(1)}, u32[]{:S(2)}) copy-start(f32[512]{0:T(512)S(1)} %dynamic_slice.7) | copy-start | bytes 6148
  52.5 7.8 %collective-permute-start.10 = (bf16[64,1536]{1,0:T(8,128)(2,1)S(1)}, bf16[64,1536]{1,0:T(8,128)(2,1)S(1)}, u32[]{:S(2)}, u32[]{:S(2)}) collective-permute-start(bf16[64,1536]{1,0:T(8,128)(2,1)S(1)} %pad_maximum_fusion.4), channel_id=1, source_target_pairs={{0,4},{1,5},{2,6},{3,7},{4,0},{5,1},{6,2},{7,3},{8,12},{9,13},{10,... | collective-permute-start | bytes 589832 | tf_op jit(solution)/shard_map/ppermute | solution.py:52
  55.1 8.8 %collective-permute-start.13 = (bf16[64,1536]{1,0:T(8,128)(2,1)S(1)}, bf16[64,1536]{1,0:T(8,128)(2,1)S(1)}, u32[]{:S(2)}, u32[]{:S(2)}) collective-permute-start(bf16[64,1536]{1,0:T(8,128)(2,1)S(1)} %pad_maximum_fusion.5), channel_id=1, source_target_pairs={{0,8},{1,9},{2,10},{3,11},{4,12},{5,13},{6,14},{7,15},{8,0},{9,1},... | collective-permute-start | bytes 589832 | tf_op jit(solution)/shard_map/ppermute | solution.py:52
  61.3 12.5 %copy-start.7 = (bf16[32,1536]{1,0:T(8,128)(2,1)S(1)}, bf16[32,1536]{1,0:T(8,128)(2,1)}, u32[]{:S(2)}) copy-start(bf16[32,1536]{1,0:T(8,128)(2,1)} %get-tuple-element.39) | copy-start | bytes 294916
  61.3 12.5 %collective-permute-start.11 = (bf16[128,1536]{1,0:T(8,128)(2,1)S(1)}, bf16[128,1536]{1,0:T(8,128)(2,1)S(1)}, u32[]{:S(2)}, u32[]{:S(2)}) collective-permute-start(bf16[128,1536]{1,0:T(8,128)(2,1)S(1)} %pad_maximum_fusion.2), channel_id=1, source_target_pairs={{0,2},{1,3},{2,0},{3,1},{4,6},{5,7},{6,4},{7,5},{8,10},{9,11},{10,... | collective-permute-start | bytes 1179656 | tf_op jit(solution)/shard_map/ppermute | solution.py:52
  64.9 7.8 %collective-permute-start.14 = (bf16[128,1536]{1,0:T(8,128)(2,1)S(1)}, bf16[128,1536]{1,0:T(8,128)(2,1)S(1)}, u32[]{:S(2)}, u32[]{:S(2)}) collective-permute-start(bf16[128,1536]{1,0:T(8,128)(2,1)S(1)} %pad_maximum_fusion.3), channel_id=1, source_target_pairs={{0,4},{1,5},{2,6},{3,7},{4,0},{5,1},{6,2},{7,3},{8,12},{9,13},{10,... | collective-permute-start | bytes 1179656 | tf_op jit(solution)/shard_map/ppermute | solution.py:52
  70.9 10.4 %copy-start.3 = (bf16[512,512]{1,0:T(8,128)(2,1)}, bf16[512,512]{1,0:T(8,128)(2,1)S(1)}, u32[]{:S(2)}) copy-start(bf16[512,512]{1,0:T(8,128)(2,1)S(1)} %select_add_fusion.refs_6_) | copy-start | bytes 1572868
  73.9 3.7 %collective-permute-start.18 = (bf16[256,512]{1,0:T(8,128)(2,1)S(1)}, bf16[256,512]{1,0:T(8,128)(2,1)S(1)}, u32[]{:S(2)}, u32[]{:S(2)}) collective-permute-start(bf16[256,512]{1,0:T(8,128)(2,1)S(1)} %slice.67), channel_id=1, source_target_pairs={{0,1},{1,0},{2,3},{3,2},{4,5},{5,4},{6,7},{7,6},{8,9},{9,8},{10,11... | collective-permute-start | bytes 786440 | tf_op jit(solution)/shard_map/ppermute | solution.py:79
  74.0 4.4 %collective-permute-start.15 = (bf16[256,2560]{1,0:T(8,128)(2,1)S(1)}, bf16[256,2560]{1,0:T(8,128)(2,1)S(1)}, u32[]{:S(2)}, u32[]{:S(2)}) collective-permute-start(bf16[256,2560]{1,0:T(8,128)(2,1)S(1)} %pad_maximum_fusion), channel_id=1, source_target_pairs={{0,1},{1,0},{2,3},{3,2},{4,5},{5,4},{6,7},{7,6},{8,9},{9,8},{10,11... | collective-permute-start | bytes 3932168 | tf_op jit(solution)/shard_map/ppermute | solution.py:78
  76.1 9.2 %collective-permute-start.16 = (bf16[256,512]{1,0:T(8,128)(2,1)S(1)}, bf16[256,512]{1,0:T(8,128)(2,1)S(1)}, u32[]{:S(2)}, u32[]{:S(2)}) collective-permute-start(bf16[256,512]{1,0:T(8,128)(2,1)S(1)} %get-tuple-element.56), channel_id=1, source_target_pairs={{0,16},{16,0},{1,17},{17,1},{2,18},{18,2},{3,19},{19,3},{4,20},{20... | collective-permute-start | bytes 786440 | tf_op jit(solution)/shard_map/ppermute | solution.py:34
  78.4 4.3 %copy-start.6 = (bf16[256,2560]{1,0:T(8,128)(2,1)}, bf16[256,2560]{1,0:T(8,128)(2,1)S(1)}, u32[]{:S(2)}) copy-start(bf16[256,2560]{1,0:T(8,128)(2,1)S(1)} %collective-permute-done.15) | copy-start | bytes 3932164
  80.1 10.1 %collective-permute-start.17 = (bf16[256,512]{1,0:T(8,128)(2,1)S(1)}, bf16[256,512]{1,0:T(8,128)(2,1)}, u32[]{:S(2)}, u32[]{:S(2)}) collective-permute-start(bf16[256,512]{1,0:T(8,128)(2,1)S(1)} %get-tuple-element.58), channel_id=1, source_target_pairs={{0,16},{16,0},{1,17},{17,1},{2,18},{18,2},{3,19},{19,3},{4,20},{20... | collective-permute-start | bytes 786440 | tf_op jit(solution)/shard_map/ppermute | solution.py:34
  81.3 19.7 %copy-start.12 = (bf16[32,4096]{1,0:T(8,128)(2,1)S(1)}, bf16[32,4096]{1,0:T(8,128)(2,1)}, u32[]{:S(2)}) copy-start(bf16[32,4096]{1,0:T(8,128)(2,1)} %get-tuple-element.28) | copy-start | bytes 786436
  85.3 4.8 %copy-start.13 = (bf16[256,512]{1,0:T(8,128)(2,1)}, bf16[256,512]{1,0:T(8,128)(2,1)S(1)}, u32[]{:S(2)}) copy-start(bf16[256,512]{1,0:T(8,128)(2,1)S(1)} %collective-permute-done.16.refs_2_) | copy-start | bytes 786436
  95.1 18.0 %all-to-all-start = ((bf16[16,24,512]{2,1,0:T(8,128)(2,1)}), bf16[16,24,512]{2,1,0:T(8,128)(2,1)S(1)}, u32[]{:S(2)}, u32[]{:S(2)}) async-start(bf16[16,24,512]{2,1,0:T(8,128)(2,1)} %get-tuple-element.46), calls=%async_computation | async-start | bytes 786432 | tf_op jit(solution)/shard_map/all_to_all | solution.py:640
  104.9 17.5 %collective-permute-start.3 = (bf16[32,512]{1,0:T(8,128)(2,1)}, bf16[32,512]{1,0:T(8,128)(2,1)}, u32[]{:S(2)}, u32[]{:S(2)}) collective-permute-start(bf16[32,512]{1,0:T(8,128)(2,1)} %slice.78), channel_id=1, source_target_pairs={{0,16},{16,0},{1,17},{17,1},{2,18},{18,2},{3,19},{19,3},{4,20},{20... | collective-permute-start | bytes 98312 | tf_op jit(solution)/shard_map/ppermute | solution.py:34
  107.6 14.8 %copy-start.11 = (f32[192,512]{1,0:T(8,128)}, f32[192,512]{1,0:T(8,128)S(1)}, u32[]{:S(2)}) copy-start(f32[192,512]{1,0:T(8,128)S(1)} %fusion.4.refs_0_) | copy-start | bytes 1179652
  108.3 14.1 %collective-permute-start.2 = (bf16[96,512]{1,0:T(8,128)(2,1)}, bf16[96,512]{1,0:T(8,128)(2,1)S(1)}, u32[]{:S(2)}, u32[]{:S(2)}) collective-permute-start(bf16[96,512]{1,0:T(8,128)(2,1)} %slice.77), channel_id=1, source_target_pairs={{0,16},{16,0},{1,17},{17,1},{2,18},{18,2},{3,19},{19,3},{4,20},{20... | collective-permute-start | bytes 294920 | tf_op jit(solution)/shard_map/ppermute | solution.py:34
  (11 other events, 21.5 us)
